TPU v7x, 32 devices: a whole 2x2x4 slice. The times are simulated.
32 devices in a mesh: tm: 8 (over z, y), space: 4 (over x, core).
Axes of the slice: x: 2, y: 2, z: 4, core: 2. Of those that a mesh axis runs over, the one named last changes fastest.
Arguments:
- right_side: float32 [512, 32, 256], P('tm', 'space'), may hold values from -24 to 24
- diffusion: float32 [32, 256], P('space'), may hold values from 0.5 to 4
- velocity: float32 [2, 32, 256], P(None, 'space'), may hold values from -0.5 to 0.5
Outputs:
- solution: float32 [512, 32, 256], P('tm', 'space')
- residual: float32 [512, 32, 256], P('tm', 'space')
All inputs are finite; a program needn't handle non-finite values.
Results may differ from a plain program's by a relative error of at most 0.0003.
Values sent between devices are 32-bit elements; how exact they have to be, the bound alone decides.
No kernel may reach another device: no remote copies, remote signals or barrier semaphores. Data moves between devices by JAX's collectives and lax.ppermute only.
A program may use at most 64 MiB of HBM per device.

v0:
```python
import math

import jax
import jax.numpy as jnp
from jax import lax
from jax.sharding import PartitionSpec as P

L = 512
KRYLOV = 3
SWEEPS = 3


alpha_corner = 0.05
damping = 0.8
epsilon = 1e-06
highest = lax.Precision.HIGHEST


def extended(block, sides, width):
    for axis, dim in sides:
        count = lax.axis_size(axis)
        forward = [(i, i + 1) for i in range(count - 1)]
        backward = [(target, source) for source, target in forward]
        low = lax.ppermute(
            lax.slice_in_dim(block, block.shape[dim] - width, None, axis=dim), axis, forward
        )
        high = lax.ppermute(lax.slice_in_dim(block, 0, width, axis=dim), axis, backward)
        block = jnp.concatenate([low, block, high], axis=dim)
    return block


def from_behind(block, axis, distance):
    devices = range(lax.axis_size(axis))
    route = [(i - distance, i) for i in devices if i - distance in devices]
    return lax.ppermute(block, axis, route)


def shifted(padded, row_dim, col_dim, rows, cols, row_start, col_start):
    piece = lax.slice_in_dim(padded, row_start, row_start + rows, axis=row_dim)
    return lax.slice_in_dim(piece, col_start, col_start + cols, axis=col_dim)


def stencil(field, padded, row_dim, col_dim, diffusion, velocity_col, velocity_row):
    rows = field.shape[row_dim]
    cols = field.shape[col_dim]
    north = shifted(padded, row_dim, col_dim, rows, cols, 0, 1)
    south = shifted(padded, row_dim, col_dim, rows, cols, 2, 1)
    west = shifted(padded, row_dim, col_dim, rows, cols, 1, 0)
    east = shifted(padded, row_dim, col_dim, rows, cols, 1, 2)
    return (
        (1.0 + 4.0 * diffusion) * field
        - diffusion * (north + south + west + east)
        + velocity_col * (east - west)
        + velocity_row * (south - north)
    )


def divided(real_part, imag_part, diag_real, diag_imag, modulus):
    return (
        damping * (real_part * diag_real + imag_part * diag_imag) / modulus,
        damping * (imag_part * diag_real - real_part * diag_imag) / modulus,
    )


def remainder(
    source_real, source_imag, image_real, image_imag, guess_real, guess_imag, shift_real, shift_imag
):
    return (
        source_real - (image_real - (shift_real * guess_real + shift_imag * guess_imag)),
        source_imag - (image_imag - (shift_real * guess_imag - shift_imag * guess_real)),
    )


def dft_tables(length):
    index = jnp.arange(length, dtype=jnp.int32)
    product = index[:, None] * index[None, :] % length
    angle = product.astype(jnp.float32) * (2.0 * math.pi / length)
    return (jnp.cos(angle), jnp.sin(angle))


def least_squares(hessen, beta):
    ortho = []
    upper = [[None] * KRYLOV for row in range(KRYLOV)]
    for column in range(KRYLOV):
        current = hessen[:, column]
        for row in range(column):
            factor = jnp.sum(ortho[row] * current)
            upper[row][column] = factor
            current = current - factor * ortho[row]
        length = jnp.sqrt(jnp.sum(current * current))
        upper[column][column] = length
        ortho.append(current / length)
    target = [ortho[row][0] * beta for row in range(KRYLOV)]
    values = [None] * KRYLOV
    for row in reversed(range(KRYLOV)):
        accum = target[row]
        for later in range(row + 1, KRYLOV):
            accum = accum - upper[row][later] * values[later]
        values[row] = accum / upper[row][row]
    return jnp.stack(values)


def per_device(right_side, diffusion, velocity):
    steps_here = right_side.shape[0]
    devices_tm = lax.axis_size("tm")
    position = lax.axis_index("tm")
    log_decay = math.log(alpha_corner) / L
    decay = math.exp(log_decay)
    local_steps = position * steps_here + jnp.arange(steps_here, dtype=jnp.int32)
    times = local_steps.astype(jnp.float32)
    weights = jnp.exp(times * log_decay)[:, None, None]
    unweights = jnp.exp(-times * log_decay)[:, None, None]
    cosine, sine = dft_tables(L)
    velocity_col = velocity[0]
    velocity_row = velocity[1]
    width = right_side.shape[2] // devices_tm
    start = position * width
    diff_strip = lax.dynamic_slice_in_dim(diffusion, start, width, 1)[:, :, None]
    col_strip = lax.dynamic_slice_in_dim(velocity_col, start, width, 1)[:, :, None]
    row_strip = lax.dynamic_slice_in_dim(velocity_row, start, width, 1)[:, :, None]
    angles = jnp.arange(L, dtype=jnp.int32).astype(jnp.float32) * (2.0 * math.pi / L)
    shift_real = decay * jnp.cos(angles)
    shift_imag = decay * jnp.sin(angles)
    diag_real = 1.0 + 4.0 * diff_strip - shift_real
    modulus = diag_real * diag_real + shift_imag * shift_imag

    def forward(block):
        real_part = jnp.dot(block, cosine, precision=highest)
        imag_part = -jnp.dot(block, sine, precision=highest)
        return jnp.concatenate([real_part, imag_part], axis=2)

    total = lax.psum(jnp.sum(right_side * right_side), ("tm", "space"))
    beta = jnp.sqrt(total + epsilon)
    basis = [right_side / beta]
    prepared = []
    hessen = jnp.zeros((KRYLOV + 1, KRYLOV), jnp.float32)
    for column in range(KRYLOV):
        moved = jnp.transpose(basis[column] * weights, (1, 2, 0))
        spectrum = forward(lax.all_to_all(moved, "tm", split_axis=1, concat_axis=2, tiled=True))
        source_real = spectrum[:, :, :L]
        source_imag = spectrum[:, :, L:]
        guess_real, guess_imag = divided(source_real, source_imag, diag_real, shift_imag, modulus)
        for sweep in range(SWEEPS - 1):
            joined = jnp.concatenate([guess_real, guess_imag], axis=2)
            padded = extended(joined, (("tm", 1), ("space", 0)), 1)
            image = stencil(joined, padded, 0, 1, diff_strip, col_strip, row_strip)
            left_real, left_imag = remainder(
                source_real,
                source_imag,
                image[:, :, :L],
                image[:, :, L:],
                guess_real,
                guess_imag,
                shift_real,
                shift_imag,
            )
            step_real, step_imag = divided(left_real, left_imag, diag_real, shift_imag, modulus)
            guess_real = guess_real + step_real
            guess_imag = guess_imag + step_imag
        back = (
            jnp.dot(guess_real, cosine, precision=highest)
            - jnp.dot(guess_imag, sine, precision=highest)
        ) / L
        back = lax.all_to_all(back, "tm", split_axis=2, concat_axis=1, tiled=True)
        direction = jnp.transpose(back, (2, 0, 1)) * unweights
        prepared.append(direction)
        apply_padded = extended(direction, (("space", 1),), 1)
        apply_padded = jnp.pad(apply_padded, ((0, 0), (0, 0), (1, 1)))
        apply_image = stencil(direction, apply_padded, 1, 2, diffusion, velocity_col, velocity_row)
        earlier = from_behind(direction[-1:], "tm", 1)
        image = apply_image - jnp.concatenate([earlier, direction[:-1]], axis=0)
        local = jnp.stack([jnp.sum(vector * image) for vector in basis])
        projections = lax.psum(local, ("tm", "space"))
        for row in range(column + 1):
            image = image - projections[row] * basis[row]
        squares = lax.psum(jnp.sum(image * image), ("tm", "space"))
        length = jnp.sqrt(squares + epsilon)
        hessen = hessen.at[: column + 1, column].set(projections)
        hessen = hessen.at[column + 1, column].set(length)
        basis.append(image / length)
    coeffs = least_squares(hessen, beta)
    solution = prepared[0] * coeffs[0]
    for column in range(1, KRYLOV):
        solution = solution + prepared[column] * coeffs[column]
    first = (jnp.arange(KRYLOV + 1) == 0).astype(jnp.float32)
    target = beta * first - jnp.sum(hessen * coeffs[None, :], axis=1)
    residual = basis[0] * target[0]
    for row in range(1, KRYLOV + 1):
        residual = residual + basis[row] * target[row]
    return (solution, residual)


def solution(mesh):
    placed = (P("tm", "space", None), P("space", None), P(None, "space", None))
    return jax.shard_map(
        per_device,
        mesh=mesh,
        in_specs=placed,
        out_specs=(P("tm", "space", None), P("tm", "space", None)),
        check_vma=False,
    )
```

profile of v0, /device:TPU:0, one launch (start us, length us, event | category | flops | bytes accessed | tf_op | source)
XLA Modules:
  0.0 741.1 jit_solution(13767238441558239875)
XLA Ops:
  3.8 42.2 %psum.49 = f32[]{:T(128)} all-reduce(f32[]{:T(128)} %multiply_reduce_fusion.9), channel_id=1, replica_groups=mesh['tm'=8,'space'=4] {'tm','space'}, use_global_device_ids=true, to_apply=%region_1.2 | all-reduce | flops 1 | bytes 8 | tf_op jit(solution)/shard_map/psum | solution.py:132
  48.9 6.1 all-to-all-start
  55.2 12.6 %all-to-all-done = f32[8,1,16384]{2,1,0:T(1,128)S(1)} async-done(((f32[8,1,16384]{2,1,0:T(1,128)}), f32[8,1,16384]{2,1,0:T(1,128)S(1)}, u32[]{:S(2)}, u32[]{:S(2)}) %all-to-all-start) | async-done | bytes 524320 | tf_op jit(solution)/shard_map/all_to_all | solution.py:139
  71.5 5.3 convolution_negate_fusion.2
  76.8 6.1 fusion.54
  83.0 3.3 collective-permute-start
  88.1 4.1 collective-permute-done.1
  95.1 3.4 collective-permute-done.3
  100.8 3.6 collective-permute-start.4
  106.0 4.2 collective-permute-done.5
  110.2 4.3 collective-permute-start.6
  120.2 5.3 fusion.45
  125.5 5.3 fusion.1
  132.8 3.3 reshape.246
  136.0 3.5 all-to-all-start.1
  139.6 11.6 %all-to-all-done.1 = f32[8,1,16384]{2,1,0:T(1,128)S(1)} async-done(((f32[8,1,16384]{2,1,0:T(1,128)}), f32[8,1,16384]{2,1,0:T(1,128)S(1)}, u32[]{:S(2)}, u32[]{:S(2)}) %all-to-all-start.1) | async-done | bytes 524320 | tf_op jit(solution)/shard_map/all_to_all | solution.py:164
  159.6 5.9 collective-permute-start.8
  168.4 3.4 collective-permute-start.10
  178.1 40.7 %psum.50 = f32[1]{0:T(128)} all-reduce(f32[1]{0:T(128)} %bitcast.14), channel_id=1, replica_groups=mesh['tm'=8,'space'=4] {'tm','space'}, use_global_device_ids=true, to_apply=%region_3.4 | all-reduce | flops 1 | bytes 8 | tf_op jit(solution)/shard_map/psum | solution.py:173
  220.2 40.3 %psum.51 = f32[]{:T(128)} all-reduce(f32[]{:T(128)} %multiply_reduce_fusion.7), channel_id=1, replica_groups=mesh['tm'=8,'space'=4] {'tm','space'}, use_global_device_ids=true, to_apply=%region_5.6 | all-reduce | flops 1 | bytes 8 | tf_op jit(solution)/shard_map/psum | solution.py:176
  264.1 19.2 %all_to_all.108 = f32[8,1,16384]{2,1,0:T(1,128)S(1)} all-to-all(f32[8,1,16384]{2,1,0:T(1,128)} %reshape.248), channel_id=1, replica_groups=mesh['tm'=8,'space'=4] {'tm'}, dimensions={0} | all-to-all | bytes 1048576 | tf_op jit(solution)/shard_map/all_to_all | solution.py:139
  283.3 2.8 reduce.27
  290.7 5.3 convolution_negate_fusion.1
  296.0 5.6 fusion.67
  301.6 3.4 collective-permute-start.11
  306.6 4.2 collective-permute-done.12
  313.5 3.7 collective-permute-done.14
  319.5 3.9 collective-permute-start.15
  325.0 4.2 collective-permute-done.16
  329.2 4.3 collective-permute-start.17
  339.4 5.3 fusion.41
  344.7 5.3 fusion.2
  354.6 17.1 %all_to_all.109 = f32[8,1,16384]{2,1,0:T(1,128)S(1)} all-to-all(f32[8,1,16384]{2,1,0:T(1,128)S(1)} %reshape.250), channel_id=1, replica_groups=mesh['tm'=8,'space'=4] {'tm'}, dimensions={0} | all-to-all | bytes 1048576 | tf_op jit(solution)/shard_map/all_to_all | solution.py:164
  375.6 3.2 copy.32
  380.8 3.3 collective-permute-start.19
  388.4 3.4 collective-permute-start.21
  395.7 3.3 multiply_reduce_fusion.6
  400.3 40.8 %psum.52 = f32[2]{0:T(128)S(1)} all-reduce(f32[2]{0:T(128)S(1)} %pad_maximum_fusion.108), channel_id=1, replica_groups=mesh['tm'=8,'space'=4] {'tm','space'}, use_global_device_ids=true, to_apply=%region_9.10 | all-reduce | flops 2 | bytes 16 | tf_op jit(solution)/shard_map/psum | solution.py:173
  441.7 3.5 multiply_reduce_fusion.4
  445.2 40.0 %psum.53 = f32[]{:T(128)} all-reduce(f32[]{:T(128)} %get-tuple-element.91), channel_id=1, replica_groups=mesh['tm'=8,'space'=4] {'tm','space'}, use_global_device_ids=true, to_apply=%region_11.12 | all-reduce | flops 1 | bytes 8 | tf_op jit(solution)/shard_map/psum | solution.py:176
  489.5 18.7 %all_to_all.110 = f32[8,1,16384]{2,1,0:T(1,128)S(1)} all-to-all(f32[8,1,16384]{2,1,0:T(1,128)S(1)} %reshape.252), channel_id=1, replica_groups=mesh['tm'=8,'space'=4] {'tm'}, dimensions={0} | all-to-all | bytes 1048576 | tf_op jit(solution)/shard_map/all_to_all | solution.py:139
  508.2 2.8 reduce.29
  515.5 5.3 convolution_negate_fusion
  520.8 5.6 fusion.61
  526.5 3.4 collective-permute-start.22
  531.4 4.2 collective-permute-done.23
  538.3 3.3 collective-permute-done.25
  544.0 3.9 collective-permute-start.26
  549.5 4.2 collective-permute-done.27
  553.7 4.3 collective-permute-start.28
  563.9 5.3 fusion.37
  569.2 5.3 fusion.3
  576.5 3.3 reshape.254
  579.7 3.5 all-to-all-start.5
  586.7 8.1 %all-to-all-done.5 = f32[8,1,16384]{2,1,0:T(1,128)S(1)} async-done(((f32[8,1,16384]{2,1,0:T(1,128)}), f32[8,1,16384]{2,1,0:T(1,128)S(1)}, u32[]{:S(2)}, u32[]{:S(2)}) %all-to-all-start.5) | async-done | bytes 524320 | tf_op jit(solution)/shard_map/all_to_all | solution.py:164
  598.7 3.2 copy.39
  605.3 6.0 collective-permute-start.30
  614.1 3.4 collective-permute-start.32
  622.4 3.4 multiply_reduce_fusion.3
  629.3 39.9 %psum.54 = f32[3]{0:T(128)S(1)} all-reduce(f32[3]{0:T(128)S(1)} %pad_maximum_fusion.109), channel_id=1, replica_groups=mesh['tm'=8,'space'=4] {'tm','space'}, use_global_device_ids=true, to_apply=%region_16.17 | all-reduce | flops 3 | bytes 24 | tf_op jit(solution)/shard_map/psum | solution.py:173
  669.8 4.6 multiply_reduce_fusion
  674.5 40.3 %psum.55 = f32[]{:T(128)} all-reduce(f32[]{:T(128)} %multiply_reduce_fusion), channel_id=1, replica_groups=mesh['tm'=8,'space'=4] {'tm','space'}, use_global_device_ids=true, to_apply=%region_18.19 | all-reduce | flops 1 | bytes 8 | tf_op jit(solution)/shard_map/psum | solution.py:176
  729.6 3.0 multiply_add_fusion.1
  733.5 5.0 multiply_add_fusion
  (182 shorter events, 146.1 us)
Async XLA Ops:
  47.5 7.6 %copy-start.11 = (f32[8,256]{1,0:T(8,128)S(1)}, f32[8,256]{1,0:T(8,128)}, u32[]{:S(2)}) copy-start(f32[8,256]{1,0:T(8,128)} %param.16) | copy-start | bytes 24580
  48.9 18.8 %all-to-all-start = ((f32[8,1,16384]{2,1,0:T(1,128)}), f32[8,1,16384]{2,1,0:T(1,128)S(1)}, u32[]{:S(2)}, u32[]{:S(2)}) async-start(f32[8,1,16384]{2,1,0:T(1,128)} %reshape.244), calls=%async_computation | async-start | bytes 1048576 | tf_op jit(solution)/shard_map/all_to_all | solution.py:139
  71.5 5.3 copy-start.10
  82.9 12.0 %copy-start.12 = (f32[2,8,256]{2,1,0:T(8,128)S(1)}, f32[2,8,256]{2,1,0:T(8,128)}, u32[]{:S(2)}) copy-start(f32[2,8,256]{2,1,0:T(8,128)} %param.17) | copy-start | bytes 49156
  83.0 5.1 collective-permute-start
  86.3 5.8 collective-permute-start.1
  92.2 2.9 collective-permute-start.2
  93.5 5.0 collective-permute-start.3
  100.8 5.2 collective-permute-start.4
  104.4 5.8 collective-permute-start.5
  110.2 5.6 collective-permute-start.6
  114.6 4.1 collective-permute-start.7
  136.0 15.2 %all-to-all-start.1 = ((f32[8,1,16384]{2,1,0:T(1,128)}), f32[8,1,16384]{2,1,0:T(1,128)S(1)}, u32[]{:S(2)}, u32[]{:S(2)}) async-start(f32[8,1,16384]{2,1,0:T(1,128)} %reshape.246), calls=%async_computation.1 | async-start | bytes 1048576 | tf_op jit(solution)/shard_map/all_to_all | solution.py:164
  157.3 2.3 copy-start.3
  159.6 14.9 %collective-permute-start.8 = (f32[64,1,256]{0,2,1:T(8,128)}, f32[64,1,256]{0,2,1:T(8,128)S(1)}, u32[]{:S(2)}, u32[]{:S(2)}) collective-permute-start(f32[64,1,256]{0,2,1:T(8,128)} %get-tuple-element.136), channel_id=1, source_target_pairs={{0,1},{1,2},{2,3},{4,5},{5,6},{6,7},{8,9},{9,10},{10,11},{12,13},{... | collective-permute-start | bytes 196616 | tf_op jit(solution)/shard_map/ppermute | solution.py:24
  165.6 8.9 %collective-permute-start.9 = (f32[64,1,256]{0,2,1:T(8,128)}, f32[64,1,256]{0,2,1:T(8,128)S(1)}, u32[]{:S(2)}, u32[]{:S(2)}) collective-permute-start(f32[64,1,256]{0,2,1:T(8,128)} %get-tuple-element.137), channel_id=1, source_target_pairs={{1,0},{2,1},{3,2},{5,4},{6,5},{7,6},{9,8},{10,9},{11,10},{13,12},{... | collective-permute-start | bytes 196616 | tf_op jit(solution)/shard_map/ppermute | solution.py:27
  168.4 4.7 collective-permute-start.10
  174.5 1.2 copy-start.8
  301.6 5.0 collective-permute-start.11
  305.0 5.8 collective-permute-start.12
  310.9 2.6 collective-permute-start.13
  312.2 5.0 collective-permute-start.14
  319.5 5.5 collective-permute-start.15
  323.4 5.8 collective-permute-start.16
  329.2 5.6 collective-permute-start.17
  333.6 4.1 collective-permute-start.18
  380.8 13.6 %collective-permute-start.19 = (f32[64,1,256]{0,2,1:T(8,128)}, f32[64,1,256]{0,2,1:T(8,128)S(1)}, u32[]{:S(2)}, u32[]{:S(2)}) collective-permute-start(f32[64,1,256]{0,2,1:T(8,128)} %get-tuple-element.130), channel_id=1, source_target_pairs={{0,1},{1,2},{2,3},{4,5},{5,6},{6,7},{8,9},{9,10},{10,11},{12,13},{... | collective-permute-start | bytes 196616 | tf_op jit(solution)/shard_map/ppermute | solution.py:24
  384.2 10.3 %collective-permute-start.20 = (f32[64,1,256]{0,2,1:T(8,128)}, f32[64,1,256]{0,2,1:T(8,128)S(1)}, u32[]{:S(2)}, u32[]{:S(2)}) collective-permute-start(f32[64,1,256]{0,2,1:T(8,128)} %get-tuple-element.131), channel_id=1, source_target_pairs={{1,0},{2,1},{3,2},{5,4},{6,5},{7,6},{9,8},{10,9},{11,10},{13,12},{... | collective-permute-start | bytes 196616 | tf_op jit(solution)/shard_map/ppermute | solution.py:27
  388.4 4.7 collective-permute-start.21
  394.4 1.2 copy-start.6
  445.2 42.4 %copy-start = (f32[64,8,256]{0,2,1:T(8,128)}, f32[64,8,256]{0,2,1:T(8,128)S(1)}, u32[]{:S(2)}) copy-start(f32[64,8,256]{0,2,1:T(8,128)S(1)} %get-tuple-element.92) | copy-start | bytes 1572868
  526.5 5.0 collective-permute-start.22
  529.8 5.8 collective-permute-start.23
  535.7 2.6 collective-permute-start.24
  537.0 4.6 collective-permute-start.25
  544.0 5.5 collective-permute-start.26
  547.9 5.8 collective-permute-start.27
  553.7 5.6 collective-permute-start.28
  558.1 4.1 collective-permute-start.29
  576.4 8.7 %copy-start.13 = (s32[2]{0:T(128)S(1)}, s32[2]{0:T(128)}, u32[]{:S(2)}) copy-start(s32[2]{0:T(128)} %constant.212.clone.1) | copy-start | bytes 28
  579.7 15.0 %all-to-all-start.5 = ((f32[8,1,16384]{2,1,0:T(1,128)}), f32[8,1,16384]{2,1,0:T(1,128)S(1)}, u32[]{:S(2)}, u32[]{:S(2)}) async-start(f32[8,1,16384]{2,1,0:T(1,128)} %reshape.254), calls=%async_computation.5 | async-start | bytes 1048576 | tf_op jit(solution)/shard_map/all_to_all | solution.py:164
  605.3 15.6 %collective-permute-start.30 = (f32[64,1,256]{0,2,1:T(8,128)}, f32[64,1,256]{0,2,1:T(8,128)S(1)}, u32[]{:S(2)}, u32[]{:S(2)}) collective-permute-start(f32[64,1,256]{0,2,1:T(8,128)} %get-tuple-element.124), channel_id=1, source_target_pairs={{0,1},{1,2},{2,3},{4,5},{5,6},{6,7},{8,9},{9,10},{10,11},{12,13},{... | collective-permute-start | bytes 196616 | tf_op jit(solution)/shard_map/ppermute | solution.py:24
  611.3 9.6 %collective-permute-start.31 = (f32[64,1,256]{0,2,1:T(8,128)}, f32[64,1,256]{0,2,1:T(8,128)S(1)}, u32[]{:S(2)}, u32[]{:S(2)}) collective-permute-start(f32[64,1,256]{0,2,1:T(8,128)} %get-tuple-element.125), channel_id=1, source_target_pairs={{1,0},{2,1},{3,2},{5,4},{6,5},{7,6},{9,8},{10,9},{11,10},{13,12},{... | collective-permute-start | bytes 196616 | tf_op jit(solution)/shard_map/ppermute | solution.py:27
  614.1 5.3 collective-permute-start.32
  620.8 1.2 copy-start.1
  620.8 1.5 copy-start.9
  669.8 59.8 %copy-start.4 = (f32[8,32,8,64]{3,1,2,0:T(8,128)S(1)}, f32[8,32,8,64]{3,1,2,0:T(8,128)}, u32[]{:S(2)}) copy-start(f32[8,32,8,64]{3,1,2,0:T(8,128)} %copy-done.3) | copy-start | bytes 1572868
  729.6 3.9 copy-start.2
  729.6 3.9 copy-start.5
  738.5 1.2 copy-start.7
where the time goes:
time: 747 us; the launch traced here: 741 us
  blocking collectives  339 us (45%)
  starting transfers between devices  96.4 us (13%)
  waiting for transfers between devices  80.7 us (11%)
  local copies, waits for them, and re-layouts  77.6 us (10%)
  other arithmetic  73.6 us (10%)
  matrix products  64.8 us (9%)
  between operations  8.86 us (1%)
    psum x3, blocking collectives, per_device(): projections = lax.psum(local, ('tm', 'space'))  121 us
    psum x3, blocking collectives, per_device(): squares = lax.psum(jnp.sum(image * image), ('tm', 'space'))  121 us
    ppermute x15, starting transfers between devices, extended(): lax.ppermute(lax.slice_in_dim(block, block.shape[dim] - width, None, axis...  53.6 us
    ppermute x15, waiting for transfers between devices, extended(): lax.ppermute(lax.slice_in_dim(block, 0, width, axis=dim), axis, backward)  43.8 us
    psum x1, blocking collectives, per_device(): total = lax.psum(jnp.sum(right_side * right_side), ('tm', 'space'))  42.2 us
    all_to_all x2, blocking collectives, per_device(): lax.all_to_all(moved, 'tm', split_axis=1, concat_axis=2, tiled=True)  37.8 us
    unnamed x43, local copies, waits for them, and re-layouts  30.7 us
    all_to_all x2, waiting for transfers between devices, per_device(): back = lax.all_to_all(back, 'tm', split_axis=2, concat_axis=1, tiled=True)  19.8 us
  transfers between devices with their start and end apart: 36, of which 23 were waited for; matrix products, arithmetic and copies ran while one was open for 2% of the time, Pallas kernels for 0%

commit v1 on v0

--- a/solution.py
+++ b/solution.py
@@ -3,6 +3,8 @@
 import jax
 import jax.numpy as jnp
 from jax import lax
+from jax.experimental import pallas as pl
+from jax.experimental.pallas import tpu as pltpu
 from jax.sharding import PartitionSpec as P
 
 L = 512
@@ -100,7 +102,7 @@
     return jnp.stack(values)
 
 
-def per_device(right_side, diffusion, velocity):
+def generic_device(right_side, diffusion, velocity):
     steps_here = right_side.shape[0]
     devices_tm = lax.axis_size("tm")
     position = lax.axis_index("tm")
@@ -190,10 +192,525 @@
     return (solution, residual)
 
 
+SUB = 8
+LANE = 128
+AXES = ("tm", "space")
+UNROLL = 8
+
+
+def spin(block, amount, axis=1):
+    return pltpu.roll(block, amount % block.shape[axis], axis)
+
+
+def lane_of(shape):
+    return lax.broadcasted_iota(jnp.int32, shape, 1)
+
+
+def exchange_blocks(pieces, width):
+    pieces = list(pieces)
+    group = lane_of(pieces[0].shape) // width
+    step = 1
+    while step < len(pieces):
+        keep = (group & step) == 0
+        for i in range(len(pieces)):
+            if i & step:
+                continue
+            low, high = pieces[i], pieces[i + step]
+            pieces[i] = jnp.where(keep, low, spin(high, step * width))
+            pieces[i + step] = jnp.where(keep, spin(low, -step * width), high)
+        step *= 2
+    return pieces
+
+
+class Plan:
+    def __init__(self, mesh, steps, rows, cols):
+        self.tm = mesh.shape["tm"]
+        self.space = mesh.shape["space"]
+        self.devices = self.tm * self.space
+        self.steps = steps
+        self.rows = rows
+        self.cols = cols
+        self.here = steps // self.tm
+        self.window = LANE // self.tm
+        self.own = cols // self.devices
+        self.halo = SWEEPS
+        self.slot = self.window // self.space
+        self.ring = [self.strip_of(d // self.space, d % self.space) for d in range(self.devices)]
+        self.holder = [self.ring.index(j) for j in range(self.devices)]
+
+    def fits(self):
+        return (
+            LANE % self.tm == 0
+            and self.tm == SUB
+            and self.rows == SUB * self.space
+            and self.cols % self.devices == 0
+            and self.cols == 2 * LANE
+            and self.steps % (self.tm * 2 * SUB) == 0
+            and self.window == 2 * self.own
+            and self.own + 2 * self.halo + 2 <= self.window
+            and self.here >= 2 * self.window
+            and self.slot >= self.halo
+            and self.space % 2 == 0
+        )
+
+    def strip_of(self, t, s):
+        turn = t ^ ((t >> 1) & 1)
+        half = self.space // 2
+        x, core = s // 2, s % 2
+        odd = turn % 2
+        return (turn * half + x + odd * (half - 1 - 2 * x)) * 2 + core
+
+
+def pack_kernel(plan, right_ref, diff_ref, vel_ref, out_ref):
+    window, halo, own = plan.window, plan.halo, plan.own
+    spot = lane_of((SUB, plan.cols)) % window
+    last, final = window - 2, window - 1
+    diff = diff_ref[...]
+    vel_col = vel_ref[0]
+    vel_row = vel_ref[1]
+    for a in range(plan.here // SUB):
+        sides = [[], []]
+        for i in range(SUB):
+            n = a * SUB + i
+            field = right_ref[n]
+            for parity in range(2):
+                base = parity * own - halo
+                piece = spin(field, -base)
+                if n < window:
+                    piece = jnp.where(spot == last, spin(diff, last - base - n), piece)
+                    piece = jnp.where(spot == final, spin(vel_col, final - base - n), piece)
+                elif n < 2 * window:
+                    piece = jnp.where(spot == last, spin(vel_row, last - base - n + window), piece)
+                sides[parity].append(piece)
+        for parity in range(2):
+            for part in range(plan.cols // LANE):
+                cut = [piece[:, part * LANE : (part + 1) * LANE] for piece in sides[parity]]
+                for m, piece in enumerate(exchange_blocks(cut, window)):
+                    strip = 2 * (part * SUB + m) + parity
+                    out_ref[plan.holder[strip], a * SUB : (a + 1) * SUB, :] = piece
+
+
+def totals_of(ref):
+    return jnp.sum(ref[...], axis=0, keepdims=True)
+
+
+def pick(totals, k):
+    lane = lane_of(totals.shape)
+    value = jnp.sum(jnp.where(lane == k, totals, 0.0), axis=1, keepdims=True)
+    return jnp.broadcast_to(value, (1, LANE))
+
+
+class Scalars:
+    def __init__(self, sums):
+        self.norms = []
+        self.scale = []
+        self.cross = {}
+        self.inner = {}
+        self.taken = {}
+        self.below = []
+        for j, totals in enumerate(sums):
+            norm = pick(totals, 0)
+            self.norms.append(norm)
+            if j == 0:
+                self.beta = jnp.sqrt(norm + epsilon)
+                self.scale.append(1.0 / self.beta)
+            else:
+                before = self.scale[j - 1]
+                length = jnp.sqrt(before * before * norm + epsilon)
+                self.below.append(length)
+                self.scale.append(before / length)
+            for i in range(j):
+                self.cross[i, j] = pick(totals, 1 + i)
+            for i in range(j + 1):
+                self.inner[i, j] = pick(totals, KRYLOV + i)
+                self.taken[i, j] = self.scale[i] * self.scale[i] * self.inner[i, j]
+
+    def finish(self, square):
+        last = KRYLOV - 1
+        for i in range(KRYLOV):
+            square = square - 2.0 * self.taken[i, last] * self.inner[i, last]
+            for k in range(KRYLOV):
+                pair = self.norms[i] if i == k else self.cross[min(i, k), max(i, k)]
+                square = square + self.taken[i, last] * self.taken[k, last] * pair
+        scale = self.scale[last]
+        self.below.append(jnp.sqrt(jnp.maximum(scale * scale * square, 0.0) + epsilon))
+        zero = jnp.zeros_like(self.beta)
+        hessen = [[zero] * KRYLOV for row in range(KRYLOV + 1)]
+        for j in range(KRYLOV):
+            for i in range(j + 1):
+                hessen[i][j] = self.scale[i] * self.scale[j] * self.inner[i, j]
+            hessen[j + 1][j] = self.below[j]
+        ortho = []
+        upper = [[None] * KRYLOV for row in range(KRYLOV)]
+        for column in range(KRYLOV):
+            current = [hessen[row][column] for row in range(KRYLOV + 1)]
+            for row in range(column):
+                factor = sum(a * b for a, b in zip(ortho[row], current))
+                upper[row][column] = factor
+                current = [b - factor * a for a, b in zip(ortho[row], current)]
+            length = jnp.sqrt(sum(b * b for b in current))
+            upper[column][column] = length
+            ortho.append([b / length for b in current])
+        values = [None] * KRYLOV
+        for row in reversed(range(KRYLOV)):
+            accum = ortho[row][0] * self.beta
+            for later in range(row + 1, KRYLOV):
+                accum = accum - upper[row][later] * values[later]
+            values[row] = accum / upper[row][row]
+        target = []
+        for row in range(KRYLOV):
+            value = self.beta if row == 0 else zero
+            target.append(value - sum(hessen[row][j] * values[j] for j in range(KRYLOV)))
+        along = [values[j] * self.scale[j] for j in range(KRYLOV)]
+        rest = [
+            target[i] * self.scale[i] + along[last] * self.taken[i, last] for i in range(KRYLOV)
+        ]
+        return along, rest, -along[last]
+
+
+def coefficients(plan, first_ref, strip, table_ref):
+    shape = (plan.rows, LANE)
+    window = plan.window
+    spot = lane_of(shape) % window
+    last, final = window - 2, window - 1
+    diff = vel_col = vel_row = jnp.zeros(shape, jnp.float32)
+    for k in range(window):
+        here = spot == k
+        early = first_ref[k]
+        diff = jnp.where(here, spin(early, k - last), diff)
+        vel_col = jnp.where(here, spin(early, k - final), vel_col)
+        vel_row = jnp.where(here, spin(first_ref[window + k], k - last), vel_row)
+    row = lax.broadcasted_iota(jnp.int32, shape, 0)
+    col = strip * plan.own - plan.halo + spot
+    center = 1.0 + 4.0 * diff
+    table_ref[0] = center
+    table_ref[1] = 1.0 / center
+    table_ref[2] = jnp.where(row > 0, diff + vel_row, 0.0)
+    table_ref[3] = jnp.where(row < plan.rows - 1, diff - vel_row, 0.0)
+    table_ref[4] = jnp.where(col > 0, diff + vel_col, 0.0)
+    table_ref[5] = jnp.where(col < plan.cols - 1, diff - vel_col, 0.0)
+
+
+def krylov_kernel(plan, j, *refs):
+    refs = list(refs)
+    strip_ref = refs.pop(0)
+    strip = strip_ref[0]
+    here, window, rows, halo = plan.here, plan.window, plan.rows, plan.halo
+    shape = (rows, LANE)
+    lane = lane_of(shape)
+    spot = lane % window
+    low_lane = lane_of((SUB, LANE))
+    low_spot = low_lane % window
+    even = strip % 2 == 0
+    if j == 0:
+        recv_ref = refs.pop(0)
+        table_ref, q_ref, z_ref, w_ref, near_ref, far_ref, sum_ref, y_ref, g_ref = refs
+        older = []
+
+        def unpack(a, carry):
+            start = pl.multiple_of(a * SUB, SUB)
+            for s in range(plan.space):
+                cut = [
+                    recv_ref[p * plan.space + s, pl.ds(start, SUB), :] for p in range(plan.tm)
+                ]
+                for i, piece in enumerate(exchange_blocks(cut, window)):
+                    q_ref[a * SUB + i, s * SUB : (s + 1) * SUB, :] = piece
+            return carry
+
+        lax.fori_loop(0, here // SUB, unpack, 0)
+        coefficients(plan, q_ref, strip, table_ref)
+    else:
+        table_ref, image_ref, near_in, far_in = refs[:4]
+        older = refs[4 : 4 + j]
+        sums = refs[4 + j : 4 + 2 * j]
+        q_ref, z_ref, w_ref, near_ref, far_ref, sum_ref, y_ref, g_ref = refs[4 + 2 * j :]
+        scalars = Scalars([totals_of(ref) for ref in sums])
+        taken = [scalars.taken[i, j - 1] for i in range(j)]
+    if j == KRYLOV - 1:
+        near_ref = far_ref = None
+    center = table_ref[0]
+    inverse = table_ref[1]
+    north, south, west, east = (table_ref[2 + k] for k in range(4))
+    zero = jnp.zeros(shape, jnp.float32)
+
+    def around(field):
+        return (
+            north * spin(field, 1, 0)
+            + south * spin(field, -1, 0)
+            + west * spin(field, 1)
+            + east * spin(field, -1)
+        )
+
+    power = inverse
+    for _ in range(int(math.log2(here))):
+        power = power * power
+    opening = jnp.where(lane < window, alpha_corner, 1.0)
+    gains = [power * opening]
+    reach = window
+    while reach < LANE:
+        gains.append(gains[-1] * spin(gains[-1], reach))
+        reach *= 2
+    closing = 1.0 / (1.0 - gains[-1])
+
+    def entering(ends):
+        total = spin(ends, window) * opening
+        distance = window
+        for gain in gains[:-1]:
+            total = total + gain * spin(total, distance)
+            distance *= 2
+        return total * closing
+
+    def loop(body, carry):
+        def several(i, carry):
+            for k in range(UNROLL):
+                carry = body(i * UNROLL + k, carry)
+            return carry
+
+        return lax.fori_loop(0, here // UNROLL, several, carry)
+
+    slot = plan.slot
+    left_spot = (spot < halo,)
+    first_side = jnp.where(even, halo + plan.own, 0)
+    second_side = jnp.where(even, 0, halo + plan.own)
+
+    def side_mask(start):
+        return (low_spot >= start) & (low_spot < start + halo)
+
+    near_mask = side_mask(first_side)
+    far_mask = side_mask(second_side)
+
+    def merged(n):
+        image = image_ref[n]
+        near = near_in[n]
+        far = far_in[n]
+        parts = []
+        for s in range(plan.space):
+            part = image[s * SUB : (s + 1) * SUB]
+            part = jnp.where(near_mask, pltpu.roll(near, (first_side - slot * s + LANE) % LANE, 1), part)
+            part = jnp.where(far_mask, pltpu.roll(far, (second_side - slot * s + LANE) % LANE, 1), part)
+            parts.append(part)
+        return jnp.concatenate(parts, axis=0)
+
+    def first(n, y):
+        if j == 0:
+            q = q_ref[n]
+        else:
+            q = merged(n)
+            for i in range(j):
+                q = q - taken[i] * older[i][n]
+            q_ref[n] = q
+        y = (q + y) * inverse
+        y_ref[n] = y
+        return y
+
+    y = loop(first, zero)
+
+    def sweep(step):
+        def body(n, carry):
+            y, z = carry
+            z = z * inverse
+            guess = damping * (y_ref[n] + z)
+            if step:
+                guess = (1.0 - damping) * g_ref[n] + guess
+            g_ref[n] = guess
+            y = (q_ref[n] + around(guess) + y) * inverse
+            y_ref[n] = y
+            return (y, z)
+
+        return body
+
+    for step in range(SWEEPS - 1):
+        y, _ = loop(sweep(step), (zero, entering(y)))
+    start = entering(y)
+    ending = (1.0 - damping) * g_ref[here - 1] + damping * (y + start * power)
+    before = jnp.where(lane < window, 0.0, spin(ending, window))
+
+    near_from = jnp.where(even, plan.own, halo)
+    far_from = jnp.where(even, halo, plan.own)
+    fields = 1 + j + (j + 1) + (1 if j == KRYLOV - 1 else 0)
+
+    def fold(block):
+        return sum(block[s * SUB : (s + 1) * SUB] for s in range(plan.space))
+
+    def last(n, carry):
+        z, before, accs = carry
+        z = z * inverse
+        guess = (1.0 - damping) * g_ref[n] + damping * (y_ref[n] + z)
+        z_ref[n] = guess
+        image = center * guess - around(guess) - before
+        w_ref[n] = image
+        if near_ref is not None:
+            near = far = None
+            for s in range(plan.space):
+                part = image[s * SUB : (s + 1) * SUB]
+                a = pltpu.roll(part, (slot * s - near_from + LANE) % LANE, 1)
+                b = pltpu.roll(part, (slot * s - far_from + LANE) % LANE, 1)
+                inside = low_spot // slot == s
+                near = a if near is None else jnp.where(inside, a, near)
+                far = b if far is None else jnp.where(inside, b, far)
+            near_ref[n] = near
+            far_ref[n] = far
+        q = q_ref[n]
+        olds = [ref[n] for ref in older]
+        products = [q * q] + [old * q for old in olds] + [old * image for old in olds] + [q * image]
+        if j == KRYLOV - 1:
+            products.append(image * image)
+        accs = tuple(acc + fold(product) for acc, product in zip(accs, products))
+        return (z, guess, accs)
+
+    low_zero = jnp.zeros((SUB, LANE), jnp.float32)
+    _, _, accs = loop(last, (start, before, (low_zero,) * fields))
+    places = [0] + [1 + i for i in range(j)] + [KRYLOV + i for i in range(j + 1)] + [2 * KRYLOV]
+    owned = (low_spot >= halo) & (low_spot < halo + plan.own)
+    record = jnp.zeros((1, LANE), jnp.float32)
+    record_lane = lane_of((1, LANE))
+    for place, acc in zip(places, accs):
+        value = jnp.sum(jnp.where(owned, acc, 0.0), axis=0, keepdims=True)
+        value = jnp.sum(value, axis=1, keepdims=True)
+        record = jnp.where(record_lane == place, value, record)
+    sum_ref[...] = jnp.broadcast_to(record, sum_ref.shape)
+
+
+def combine_kernel(plan, *refs):
+    q_refs = refs[:KRYLOV]
+    z_refs = refs[KRYLOV : 2 * KRYLOV]
+    image_ref = refs[2 * KRYLOV]
+    sums = refs[2 * KRYLOV + 1 : 3 * KRYLOV + 1]
+    out_ref = refs[-1]
+    totals = [totals_of(ref) for ref in sums]
+    scalars = Scalars(totals)
+    along, rest, tail = scalars.finish(pick(totals[-1], 2 * KRYLOV))
+    own, halo, window = plan.own, plan.halo, plan.window
+    front = lane_of((SUB, LANE)) % window < own
+    groups = plan.here // (2 * SUB)
+
+    def body(aa, carry):
+        for s in range(plan.space):
+            here = slice(s * SUB, (s + 1) * SUB)
+
+            def solution_at(n):
+                return sum(c * ref[n, here, :] for c, ref in zip(along, z_refs))
+
+            def residual_at(n):
+                total = tail * image_ref[n, here, :]
+                for c, ref in zip(rest, q_refs):
+                    total = total + c * ref[n, here, :]
+                return total
+
+            for f, value in enumerate((solution_at, residual_at)):
+                pieces = []
+                for i in range(SUB):
+                    n = aa * 2 * SUB + 2 * i
+                    pieces.append(
+                        jnp.where(front, spin(value(n), -halo), spin(value(n + 1), own - halo))
+                    )
+                start = pl.multiple_of((f * groups + aa) * SUB, SUB)
+                for p, piece in enumerate(exchange_blocks(pieces, window)):
+                    out_ref[p * plan.space + s, pl.ds(start, SUB), :] = piece
+        return carry
+
+    lax.fori_loop(0, groups, body, 0)
+
+
+def unpack_kernel(plan, recv_ref, *out_refs):
+    groups = plan.here // (2 * SUB)
+    count = LANE // plan.own
+
+    def body(aa, carry):
+        for f, out_ref in enumerate(out_refs):
+            start = pl.multiple_of((f * groups + aa) * SUB, SUB)
+            for part in range(plan.cols // LANE):
+                pieces = [
+                    recv_ref[plan.holder[part * count + m], pl.ds(start, SUB), :]
+                    for m in range(count)
+                ]
+                for i, piece in enumerate(exchange_blocks(pieces, plan.own)):
+                    out_ref[aa * count + i, :, part * LANE : (part + 1) * LANE] = piece
+        return carry
+
+    lax.fori_loop(0, groups, body, 0)
+
+
+def call(kernel, shapes, operands, scalars=0, scratch=()):
+    vmem = pl.BlockSpec(memory_space=pltpu.VMEM)
+    smem = pl.BlockSpec(memory_space=pltpu.SMEM)
+    return pl.pallas_call(
+        kernel,
+        out_shape=[jax.ShapeDtypeStruct(shape, jnp.float32) for shape in shapes],
+        in_specs=[smem] * scalars + [vmem] * (len(operands) - scalars),
+        out_specs=[vmem] * len(shapes),
+        scratch_shapes=[pltpu.VMEM(shape, jnp.float32) for shape in scratch],
+        compiler_params=pltpu.CompilerParams(vmem_limit_bytes=48 * 1024 * 1024),
+    )(*operands)
+
+
+def everyone(block):
+    return lax.all_to_all(block, AXES, split_axis=0, concat_axis=0, tiled=True)
+
+
+def strip_device(plan, right_side, diffusion, velocity):
+    t = lax.axis_index("tm")
+    s = lax.axis_index("space")
+    strip = plan.strip_of(t, s).astype(jnp.int32).reshape(1)
+    count = plan.devices
+    hold = plan.holder
+    near_route = []
+    far_route = []
+    for k in range(0, count, 2):
+        near_route += [(hold[k], hold[k + 1]), (hold[k + 1], hold[k])]
+    for k in range(1, count - 1, 2):
+        far_route += [(hold[k], hold[k + 1]), (hold[k + 1], hold[k])]
+    bind = lambda kernel, *more: (lambda *refs: kernel(plan, *more, *refs))
+    full = (plan.here, plan.rows, LANE)
+    side = (plan.here, SUB, LANE)
+    small = (count, LANE)
+    sent = call(bind(pack_kernel), [(count, plan.here, LANE)], [right_side, diffusion, velocity])[0]
+    recv = everyone(sent)
+    table, q, z, image, near, far, sums = call(
+        bind(krylov_kernel, 0),
+        [(6, plan.rows, LANE), full, full, full, side, side, small],
+        [strip, recv],
+        scalars=1,
+        scratch=[full, full],
+    )
+    qs, zs, totals = [q], [z], []
+    for j in range(1, KRYLOV):
+        near = lax.ppermute(near, AXES, near_route)
+        far = lax.ppermute(far, AXES, far_route)
+        totals.append(everyone(sums))
+        q, z, image, near, far, sums = call(
+            bind(krylov_kernel, j),
+            [full, full, full, side, side, small],
+            [strip, table, image, near, far, *qs, *totals],
+            scalars=1,
+            scratch=[full, full],
+        )
+        qs.append(q)
+        zs.append(z)
+    totals.append(everyone(sums))
+    packed = call(
+        bind(combine_kernel), [(count, plan.here, LANE)], [*qs, *zs, image, *totals]
+    )[0]
+    shape = right_side.shape
+    return tuple(call(bind(unpack_kernel), [shape, shape], [everyone(packed)]))
+
+
+def per_device(mesh):
+    def run(right_side, diffusion, velocity):
+        rows = right_side.shape[1] * mesh.shape["space"]
+        steps = right_side.shape[0] * mesh.shape["tm"]
+        plan = Plan(mesh, steps, rows, right_side.shape[2])
+        if plan.fits():
+            return strip_device(plan, right_side, diffusion, velocity)
+        return generic_device(right_side, diffusion, velocity)
+
+    return run
+
+
 def solution(mesh):
     placed = (P("tm", "space", None), P("space", None), P(None, "space", None))
     return jax.shard_map(
-        per_device,
+        per_device(mesh),
         mesh=mesh,
         in_specs=placed,
         out_specs=(P("tm", "space", None), P("tm", "space", None)),

time: 747 us -> 142 us (0.19)
  blocking collectives: 339 us -> 60 us
  starting transfers between devices: 96.4 us -> 8.66 us
  other arithmetic: 73.6 us -> 0 us
  local copies, waits for them, and re-layouts: 77.6 us -> 7.39 us
  matrix products: 64.8 us -> 0 us
  waiting for transfers between devices: 80.7 us -> 26.2 us
  Pallas kernels: 0 us -> 38.4 us
  between operations: 8.86 us -> 0.73 us
    psum x7 -> x0, blocking collectives: 284 us -> none  [the longest x3 121 us: per_device(): projections = lax.psum(local, ('tm', 'space'))]
    ppermute x33 -> x4, starting transfers between devices: 83.3 us -> 1.34 us  [the longest x2 1.33 us: strip_device(): far = lax.ppermute(far, AXES, far_route)]
    dot_general x12 -> x0, matrix products: 64.8 us -> none  [the longest x3 17.2 us: forward(): real_part = jnp.dot(block, cosine, precision=highest)]
    ppermute x33 -> x4, waiting for transfers between devices: 48.4 us -> 0.01 us  [the longest x2 0.01 us: strip_device(): far = lax.ppermute(far, AXES, far_route)]
    pallas_call x0 -> x6, Pallas kernels: none -> 38.4 us  [call(): pl.pallas_call(kernel, out_shape=[jax.ShapeDtypeStruct(shape, jnp.float32...]
    reduce_sum x13 -> x0, other arithmetic: 26.4 us -> none  [the longest x3 9.59 us: per_device(): squares = lax.psum(jnp.sum(image * image), ('tm', 'space'))]
    unnamed x43 -> x20, local copies, waits for them, and re-layouts: 30.7 us -> 7.39 us
    add x13 -> x0, other arithmetic: 19.9 us -> none  [the longest x6 9.69 us: stencil(): (1.0 + 4.0 * diffusion) * field - diffusion * (north + south + west + east)]
  transfers between devices with their start and end apart: 36 -> 5, of which waited for: 23 -> 1; matrix products, arithmetic and copies ran while one was open for 2% -> 0% of each run, Pallas kernels for 0% -> 0%
where the time goes in v1:
time: 142 us; the launch traced here: 141 us
  blocking collectives  60 us (42%)
  Pallas kernels  38.4 us (27%)
  waiting for transfers between devices  26.2 us (18%)
  starting transfers between devices  8.66 us (6%)
  local copies, waits for them, and re-layouts  7.39 us (5%)
    all_to_all x4, blocking collectives, everyone(): return lax.all_to_all(block, AXES, split_axis=0, concat_axis=0, tiled=True)  60 us
    pallas_call x6, Pallas kernels, call(): pl.pallas_call(kernel, out_shape=[jax.ShapeDtypeStruct(shape, jnp.float32...  38.4 us
    all_to_all x1, waiting for transfers between devices, everyone(): return lax.all_to_all(block, AXES, split_axis=0, concat_axis=0, tiled=True)  26.2 us
    unnamed x20, local copies, waits for them, and re-layouts  7.39 us
    all_to_all x1, starting transfers between devices, everyone(): return lax.all_to_all(block, AXES, split_axis=0, concat_axis=0, tiled=True)  7.33 us
  transfers between devices with their start and end apart: 5, of which 1 were waited for; matrix products, arithmetic and copies ran while one was open for 0% of the time, Pallas kernels for 0%

profile of v1, /device:TPU:0, one launch (start us, length us, event | category | flops | bytes accessed | tf_op | source)
XLA Modules:
  0.0 141.4 jit_solution(11821831134616633343)
XLA Ops:
  0.6 0.0 copy-start.7
  0.6 1.0 copy-done.7
  1.7 0.0 copy-start.8
  1.7 0.7 copy-done.8
  2.4 0.0 copy-start.9
  2.4 0.7 copy-done.9
  3.1 6.0 %shard_map.50 = f32[32,64,128]{2,1,0:T(8,128)} custom-call(f32[64,8,256]{2,1,0:T(8,128)S(1)} %copy-done.7, f32[8,256]{1,0:T(8,128)S(1)} %copy-done.9, f32[2,8,256]{2,1,0:T(8,128)S(1)} %copy-done.8), custom_call_target="tpu_custom_call" | custom-call | tf_op jit(solution)/shard_map/pallas_call | solution.py:637
  9.1 7.3 %all-to-all-start = ((f32[32,64,128]{2,1,0:T(8,128)}), f32[32,64,128]{2,1,0:T(8,128)S(1)}, u32[]{:S(2)}, u32[]{:S(2)}) async-start(f32[32,64,128]{2,1,0:T(8,128)} %shard_map.50), calls=%async_computation | async-start | bytes 2097152 | tf_op jit(solution)/shard_map/all_to_all | solution.py:648
  16.5 26.2 %all-to-all-done.refs_1_ = f32[32,64,128]{2,1,0:T(8,128)S(1)} async-done(((f32[32,64,128]{2,1,0:T(8,128)}), f32[32,64,128]{2,1,0:T(8,128)S(1)}, u32[]{:S(2)}, u32[]{:S(2)}) %all-to-all-start) | async-done | bytes 1048608 | tf_op jit(solution)/shard_map/all_to_all | solution.py:648
  42.6 8.0 %shard_map.51 = (f32[6,32,128]{2,1,0:T(8,128)S(1)}, f32[64,32,128]{2,1,0:T(8,128)S(1)}, f32[64,32,128]{2,1,0:T(8,128)S(1)}, f32[64,32,128]{2,1,0:T(8,128)S(1)}, ...) custom-call(s32[1]{0:T(128)} %bitcast.refs_0_, f32[32,64,128]{2,1,0:T(8,128)S(1)} %all-to-all-done.refs_1_), custom_call_target="tpu_custom_call" | custom-call | tf_op jit(solution)/shard_map/pallas_call | solution.py:637
  50.6 0.0 copy-start
  50.6 1.0 copy-done
  51.6 0.0 collective-permute-start
  51.6 0.7 collective-permute-start.1
  52.3 12.5 %all_to_all.43 = f32[32,1,128]{2,1,0:T(1,128)S(1)} all-to-all(f32[32,1,128]{2,1,0:T(1,128)S(1)} %bitcast.20), channel_id=1, replica_groups=mesh['tm'=8,'space'=4] {'tm','space'}, dimensions={0} | all-to-all | bytes 32768 | tf_op jit(solution)/shard_map/all_to_all | solution.py:648
  64.8 0.0 collective-permute-done.refs_3_
  64.8 0.0 collective-permute-done.1.refs_4_
  64.8 8.2 %shard_map.52 = (f32[64,32,128]{2,1,0:T(8,128)S(1)}, f32[64,32,128]{2,1,0:T(8,128)S(1)}, f32[64,32,128]{2,1,0:T(8,128)S(1)}, f32[64,8,128]{2,1,0:T(8,128)S(1)}, ...) custom-call(s32[1]{0:T(128)} %bitcast.refs_0_, f32[6,32,128]{2,1,0:T(8,128)S(1)} %get-tuple-element.20.refs_1_, ...), custom_call_target="tpu_custom_call" | custom-call | tf_op jit(solution)/shard_map/pallas_call | solution.py:637
  73.0 0.0 copy-start.2
  73.0 1.0 copy-done.2
  74.0 0.0 copy-start.4
  74.0 1.0 copy-done.4
  74.9 0.0 collective-permute-start.2
  75.0 0.7 collective-permute-start.3
  75.6 10.7 %all_to_all.44 = f32[32,1,128]{2,1,0:T(1,128)S(1)} all-to-all(f32[32,1,128]{2,1,0:T(1,128)S(1)} %bitcast.19), channel_id=1, replica_groups=mesh['tm'=8,'space'=4] {'tm','space'}, dimensions={0} | all-to-all | bytes 32768 | tf_op jit(solution)/shard_map/all_to_all | solution.py:648
  86.4 0.0 collective-permute-done.2.refs_3_
  86.4 0.0 collective-permute-done.3.refs_4_
  86.4 0.0 copy-start.1
  86.4 0.0 copy-start.3
  86.4 8.4 %shard_map.53 = (f32[64,32,128]{2,1,0:T(8,128)S(1)}, f32[64,32,128]{2,1,0:T(8,128)S(1)}, f32[64,32,128]{2,1,0:T(8,128)S(1)}, f32[64,8,128]{2,1,0:T(8,128)}, f32[...) custom-call(s32[1]{0:T(128)} %bitcast.refs_0_, f32[6,32,128]{2,1,0:T(8,128)S(1)} %get-tuple-element.20.refs_1_, ...), custom_call_target="tpu_custom_call" | custom-call | tf_op jit(solution)/shard_map/pallas_call | solution.py:637
  94.8 0.0 copy-start.5
  94.8 1.0 copy-done.5
  95.8 0.0 copy-start.6
  95.8 1.0 copy-done.6
  96.8 8.9 %all_to_all.45 = f32[32,1,128]{2,1,0:T(1,128)S(1)} all-to-all(f32[32,1,128]{2,1,0:T(1,128)S(1)} %bitcast.21), channel_id=1, replica_groups=mesh['tm'=8,'space'=4] {'tm','space'}, dimensions={0} | all-to-all | bytes 32768 | tf_op jit(solution)/shard_map/all_to_all | solution.py:648
  105.6 0.0 copy-done.1
  105.6 0.0 copy-done.3
  105.6 5.2 %shard_map.54 = f32[32,64,128]{2,1,0:T(8,128)S(1)} custom-call(f32[64,32,128]{2,1,0:T(8,128)S(1)} %copy-done.1, f32[64,32,128]{2,1,0:T(8,128)S(1)} %copy-done.3, f32[64,32,128]{2,1,0:T(8,128)S(1)} %get-tuple-element.30.refs_2_, f32[64,32,128]{2,1,0:T(8,128)S(1)} %get-tuple-element.31.refs_3_, f32[64,32,128]{2,1,0:T(8,128)} %copy-done.4, ...), custom_call_target="tpu_custom_call" | custom-call | tf_op jit(solution)/shard_map/pallas_call | solution.py:637
  110.8 27.9 %all_to_all.46.refs_0_ = f32[32,64,128]{2,1,0:T(8,128)S(1)} all-to-all(f32[32,64,128]{2,1,0:T(8,128)S(1)} %shard_map.54), channel_id=1, replica_groups=mesh['tm'=8,'space'=4] {'tm','space'}, dimensions={0} | all-to-all | bytes 2097152 | tf_op jit(solution)/shard_map/all_to_all | solution.py:648
  138.7 2.7 %shard_map.55 = (f32[64,8,256]{2,1,0:T(8,128)}, f32[64,8,256]{2,1,0:T(8,128)}) custom-call(f32[32,64,128]{2,1,0:T(8,128)S(1)} %all_to_all.46.refs_0_), custom_call_target="tpu_custom_call" | custom-call | tf_op jit(solution)/shard_map/pallas_call | solution.py:637
Async XLA Ops:
  0.6 1.0 copy-start.7
  1.7 0.7 copy-start.8
  2.4 0.7 copy-start.9
  9.1 33.5 %all-to-all-start = ((f32[32,64,128]{2,1,0:T(8,128)}), f32[32,64,128]{2,1,0:T(8,128)S(1)}, u32[]{:S(2)}, u32[]{:S(2)}) async-start(f32[32,64,128]{2,1,0:T(8,128)} %shard_map.50), calls=%async_computation | async-start | bytes 2097152 | tf_op jit(solution)/shard_map/all_to_all | solution.py:648
  50.6 1.0 copy-start
  51.6 13.2 %collective-permute-start = (f32[64,8,128]{2,1,0:T(8,128)S(1)}, f32[64,8,128]{2,1,0:T(8,128)S(1)}, u32[]{:S(2)}, u32[]{:S(2)}) collective-permute-start(f32[64,8,128]{2,1,0:T(8,128)S(1)} %get-tuple-element.22), channel_id=1, source_target_pairs={{0,1},{1,0},{2,3},{3,2},{6,7},{7,6},{4,5},{5,4},{12,13},{13,12},{1... | collective-permute-start | bytes 786440 | tf_op jit(solution)/shard_map/ppermute | solution.py:678
  51.6 13.2 %collective-permute-start.1 = (f32[64,8,128]{2,1,0:T(8,128)S(1)}, f32[64,8,128]{2,1,0:T(8,128)S(1)}, u32[]{:S(2)}, u32[]{:S(2)}) collective-permute-start(f32[64,8,128]{2,1,0:T(8,128)S(1)} %get-tuple-element.23), channel_id=1, source_target_pairs={{1,2},{2,1},{3,6},{6,3},{7,4},{4,7},{5,12},{12,5},{13,14},{14,13},... | collective-permute-start | bytes 786440 | tf_op jit(solution)/shard_map/ppermute | solution.py:679
  73.0 1.0 copy-start.2
  74.0 1.0 copy-start.4
  74.9 11.4 %collective-permute-start.2 = (f32[64,8,128]{2,1,0:T(8,128)S(1)}, f32[64,8,128]{2,1,0:T(8,128)S(1)}, u32[]{:S(2)}, u32[]{:S(2)}) collective-permute-start(f32[64,8,128]{2,1,0:T(8,128)S(1)} %get-tuple-element.27), channel_id=1, source_target_pairs={{0,1},{1,0},{2,3},{3,2},{6,7},{7,6},{4,5},{5,4},{12,13},{13,12},{1... | collective-permute-start | bytes 786440 | tf_op jit(solution)/shard_map/ppermute | solution.py:678
  75.0 11.4 %collective-permute-start.3 = (f32[64,8,128]{2,1,0:T(8,128)S(1)}, f32[64,8,128]{2,1,0:T(8,128)S(1)}, u32[]{:S(2)}, u32[]{:S(2)}) collective-permute-start(f32[64,8,128]{2,1,0:T(8,128)S(1)} %get-tuple-element.28), channel_id=1, source_target_pairs={{1,2},{2,1},{3,6},{6,3},{7,4},{4,7},{5,12},{12,5},{13,14},{14,13},... | collective-permute-start | bytes 786440 | tf_op jit(solution)/shard_map/ppermute | solution.py:679
  86.4 19.2 %copy-start.1 = (f32[64,32,128]{2,1,0:T(8,128)S(1)}, f32[64,32,128]{2,1,0:T(8,128)}, u32[]{:S(2)}) copy-start(f32[64,32,128]{2,1,0:T(8,128)} %copy-done) | copy-start | bytes 3145732
  86.4 19.2 %copy-start.3 = (f32[64,32,128]{2,1,0:T(8,128)S(1)}, f32[64,32,128]{2,1,0:T(8,128)}, u32[]{:S(2)}) copy-start(f32[64,32,128]{2,1,0:T(8,128)} %copy-done.2) | copy-start | bytes 3145732
  94.8 1.0 copy-start.5
  95.8 1.0 copy-start.6

commit v2 on v1

--- a/solution.py
+++ b/solution.py
@@ -206,19 +206,24 @@
     return lax.broadcasted_iota(jnp.int32, shape, 1)
 
 
-def exchange_blocks(pieces, width):
+def exchange_blocks(pieces, width, radix):
     pieces = list(pieces)
-    group = lane_of(pieces[0].shape) // width
+    lane = lane_of(pieces[0].shape)
     step = 1
     while step < len(pieces):
-        keep = (group & step) == 0
+        digit = lane // (width * step) % radix
+        result = list(pieces)
         for i in range(len(pieces)):
-            if i & step:
-                continue
-            low, high = pieces[i], pieces[i + step]
-            pieces[i] = jnp.where(keep, low, spin(high, step * width))
-            pieces[i + step] = jnp.where(keep, spin(low, -step * width), high)
-        step *= 2
+            e = i // step % radix
+            total = None
+            for d in range(radix):
+                moved = pieces[i + (d - e) * step]
+                if d != e:
+                    moved = spin(moved, (d - e) * step * width)
+                total = moved if total is None else jnp.where(digit == d, moved, total)
+            result[i] = total
+        pieces = result
+        step *= radix
     return pieces
 
 
@@ -235,6 +240,12 @@
         self.own = cols // self.devices
         self.halo = SWEEPS
         self.slot = self.window // self.space
+        self.used = self.own + 2 * self.halo
+        self.spare = self.window - self.used
+        self.tiles = self.here // SUB
+        self.inward = (self.tiles - 1) * SUB + 1
+        self.groups = self.here // (2 * SUB)
+        self.outward = self.groups * SUB + 2 * self.groups + 1
         self.ring = [self.strip_of(d // self.space, d % self.space) for d in range(self.devices)]
         self.holder = [self.ring.index(j) for j in range(self.devices)]
 
@@ -247,8 +258,9 @@
             and self.cols == 2 * LANE
             and self.steps % (self.tm * 2 * SUB) == 0
             and self.window == 2 * self.own
-            and self.own + 2 * self.halo + 2 <= self.window
-            and self.here >= 2 * self.window
+            and self.spare * (self.tiles - 1) == self.used
+            and self.here % UNROLL == 0
+            and self.groups * 2 == SUB
             and self.slot >= self.halo
             and self.space % 2 == 0
         )
@@ -261,37 +273,93 @@
         return (turn * half + x + odd * (half - 1 - 2 * x)) * 2 + core
 
 
-def pack_kernel(plan, right_ref, diff_ref, vel_ref, out_ref):
-    window, halo, own = plan.window, plan.halo, plan.own
-    spot = lane_of((SUB, plan.cols)) % window
-    last, final = window - 2, window - 1
-    diff = diff_ref[...]
-    vel_col = vel_ref[0]
-    vel_row = vel_ref[1]
-    for a in range(plan.here // SUB):
-        sides = [[], []]
-        for i in range(SUB):
-            n = a * SUB + i
-            field = right_ref[n]
-            for parity in range(2):
-                base = parity * own - halo
-                piece = spin(field, -base)
-                if n < window:
-                    piece = jnp.where(spot == last, spin(diff, last - base - n), piece)
-                    piece = jnp.where(spot == final, spin(vel_col, final - base - n), piece)
-                elif n < 2 * window:
-                    piece = jnp.where(spot == last, spin(vel_row, last - base - n + window), piece)
-                sides[parity].append(piece)
+def pack_kernel(plan, place_ref, right_ref, diff_ref, vel_ref, out_ref, tail_ref):
+    window, own, halo = plan.window, plan.own, plan.halo
+    parts = plan.cols // LANE
+    lane = lane_of((SUB, LANE))
+    group, spot = lane // window, lane % window
+    edge = LANE - (SUB - 1) * window - own + halo
+
+    def strips():
         for parity in range(2):
-            for part in range(plan.cols // LANE):
-                cut = [piece[:, part * LANE : (part + 1) * LANE] for piece in sides[parity]]
-                for m, piece in enumerate(exchange_blocks(cut, window)):
-                    strip = 2 * (part * SUB + m) + parity
-                    out_ref[plan.holder[strip], a * SUB : (a + 1) * SUB, :] = piece
+            for part in range(parts):
+                for m in range(SUB):
+                    yield parity, part, m, plan.holder[2 * (part * SUB + m) + parity]
+
+    def body(k, carry):
+        a = plan.tiles - 1 - k
+        fields = [right_ref[a * SUB + i] for i in range(SUB)]
+        cache = {}
+
+        def turned(i, part, amount):
+            key = (i, part % parts, amount % LANE)
+            if key not in cache:
+                block = fields[i][:, key[1] * LANE : (key[1] + 1) * LANE]
+                cache[key] = spin(block, amount)
+            return cache[key]
+
+        pieces = []
+        for parity, part, m, _ in strips():
+            base = parity * own - halo
+            total = None
+            for i in range(SUB):
+                amount = window * (i - m) - base
+                value = turned(i, part, amount)
+                if parity == 0 and m == 0:
+                    value = jnp.where(spot < halo, turned(i, part - 1, amount), value)
+                if parity == 1 and m == SUB - 1:
+                    value = jnp.where(spot >= edge, turned(i, part + 1, amount), value)
+                total = value if total is None else jnp.where(group == i, value, total)
+            pieces.append(total)
+
+        @pl.when(k == 0)
+        def _():
+            for index, piece in enumerate(pieces):
+                tail_ref[index] = piece
+
+        @pl.when(k > 0)
+        def _():
+            amount = plan.used - plan.spare * a
+            for index, (_, _, _, target) in enumerate(strips()):
+                tail = pltpu.roll(tail_ref[index], amount, 1)
+                piece = jnp.where(spot >= plan.used, tail, pieces[index])
+                out_ref[pl.ds(target * plan.inward + a * SUB, SUB), :] = piece
+
+        return carry
+
+    lax.fori_loop(0, plan.tiles, body, 0)
+    row = pl.ds(place_ref[0], 1)
+    lines = [diff_ref[row, :], vel_ref[0, row, :], vel_ref[1, row, :]]
+    sub = lax.broadcasted_iota(jnp.int32, (SUB, LANE), 0)
+    blocks = [
+        [jnp.broadcast_to(line[:, h * LANE : (h + 1) * LANE], (SUB, LANE)) for h in range(parts)]
+        for line in lines
+    ]
+    for parity in range(2):
+        base = parity * own - halo
+        for part in range(parts):
+            total = jnp.zeros((SUB, LANE), jnp.float32)
+            for f in range(len(lines)):
+                amount = (f + 1) * window - base
+
+                def slanted(h):
+                    flat = spin(blocks[f][h % parts], amount)
+                    return pltpu.roll(flat, 0, 1, stride=window, stride_axis=0)
+
+                value = slanted(part)
+                if parity == 0:
+                    value = jnp.where((sub == SUB - 1) & (spot < halo), slanted(part - 1), value)
+                else:
+                    value = jnp.where((sub == 0) & (spot >= edge), slanted(part + 1), value)
+                total = jnp.where(group == f, value, total)
+            for m in range(SUB):
+                target = plan.holder[2 * (part * SUB + m) + parity]
+                at = target * plan.inward + plan.inward - 1
+                out_ref[at : at + 1, :] = total[SUB - 1 - m : SUB - m]
 
 
 def totals_of(ref):
-    return jnp.sum(ref[...], axis=0, keepdims=True)
+    return jnp.sum(ref[...], axis=0, keepdims=True) * (1.0 / (damping * damping))
 
 
 def pick(totals, k):
@@ -357,86 +425,84 @@
             for later in range(row + 1, KRYLOV):
                 accum = accum - upper[row][later] * values[later]
             values[row] = accum / upper[row][row]
-        target = []
-        for row in range(KRYLOV):
-            value = self.beta if row == 0 else zero
-            target.append(value - sum(hessen[row][j] * values[j] for j in range(KRYLOV)))
-        along = [values[j] * self.scale[j] for j in range(KRYLOV)]
-        rest = [
-            target[i] * self.scale[i] + along[last] * self.taken[i, last] for i in range(KRYLOV)
-        ]
-        return along, rest, -along[last]
-
-
-def coefficients(plan, first_ref, strip, table_ref):
+        return [values[j] * self.scale[j] for j in range(KRYLOV)]
+
+
+def coefficients(plan, recv_ref, strip, table_ref):
+    window = plan.window
+    lane = lane_of((SUB, LANE))
+    stride = plan.space * plan.inward
+    lines = [
+        recv_ref[pl.ds(s * plan.inward + plan.inward - 1, SUB, stride), :]
+        for s in range(plan.space)
+    ]
+    fields = []
+    for f in range(3):
+        parts = []
+        for line in lines:
+            part = jnp.where(lane < window, spin(line, -f * window), 0.0)
+            reach = window
+            while reach < LANE:
+                part = part + spin(part, reach)
+                reach *= 2
+            parts.append(part)
+        fields.append(jnp.concatenate(parts, axis=0))
+    diff, vel_col, vel_row = fields
     shape = (plan.rows, LANE)
-    window = plan.window
-    spot = lane_of(shape) % window
-    last, final = window - 2, window - 1
-    diff = vel_col = vel_row = jnp.zeros(shape, jnp.float32)
-    for k in range(window):
-        here = spot == k
-        early = first_ref[k]
-        diff = jnp.where(here, spin(early, k - last), diff)
-        vel_col = jnp.where(here, spin(early, k - final), vel_col)
-        vel_row = jnp.where(here, spin(first_ref[window + k], k - last), vel_row)
     row = lax.broadcasted_iota(jnp.int32, shape, 0)
-    col = strip * plan.own - plan.halo + spot
+    col = strip * plan.own - plan.halo + lane_of(shape) % window
     center = 1.0 + 4.0 * diff
-    table_ref[0] = center
+    table_ref[0] = damping * center
     table_ref[1] = 1.0 / center
-    table_ref[2] = jnp.where(row > 0, diff + vel_row, 0.0)
-    table_ref[3] = jnp.where(row < plan.rows - 1, diff - vel_row, 0.0)
-    table_ref[4] = jnp.where(col > 0, diff + vel_col, 0.0)
-    table_ref[5] = jnp.where(col < plan.cols - 1, diff - vel_col, 0.0)
+    table_ref[2] = jnp.where(row > 0, damping * (diff + vel_row), 0.0)
+    table_ref[3] = jnp.where(row < plan.rows - 1, damping * (diff - vel_row), 0.0)
+    table_ref[4] = jnp.where(col > 0, damping * (diff + vel_col), 0.0)
+    table_ref[5] = jnp.where(col < plan.cols - 1, damping * (diff - vel_col), 0.0)
 
 
 def krylov_kernel(plan, j, *refs):
     refs = list(refs)
-    strip_ref = refs.pop(0)
-    strip = strip_ref[0]
-    here, window, rows, halo = plan.here, plan.window, plan.rows, plan.halo
+    strip = refs.pop(0)[0]
+    here, window, rows, halo, own = plan.here, plan.window, plan.rows, plan.halo, plan.own
+    slot = plan.slot
+    final = j == KRYLOV - 1
     shape = (rows, LANE)
     lane = lane_of(shape)
-    spot = lane % window
     low_lane = lane_of((SUB, LANE))
     low_spot = low_lane % window
     even = strip % 2 == 0
+    older = []
     if j == 0:
         recv_ref = refs.pop(0)
-        table_ref, q_ref, z_ref, w_ref, near_ref, far_ref, sum_ref, y_ref, g_ref = refs
-        older = []
-
-        def unpack(a, carry):
-            start = pl.multiple_of(a * SUB, SUB)
-            for s in range(plan.space):
-                cut = [
-                    recv_ref[p * plan.space + s, pl.ds(start, SUB), :] for p in range(plan.tm)
-                ]
-                for i, piece in enumerate(exchange_blocks(cut, window)):
-                    q_ref[a * SUB + i, s * SUB : (s + 1) * SUB, :] = piece
-            return carry
-
-        lax.fori_loop(0, here // SUB, unpack, 0)
-        coefficients(plan, q_ref, strip, table_ref)
+        table_ref = refs.pop(0)
     else:
         table_ref, image_ref, near_in, far_in = refs[:4]
         older = refs[4 : 4 + j]
         sums = refs[4 + j : 4 + 2 * j]
-        q_ref, z_ref, w_ref, near_ref, far_ref, sum_ref, y_ref, g_ref = refs[4 + 2 * j :]
+        refs = refs[4 + 2 * j :]
         scalars = Scalars([totals_of(ref) for ref in sums])
         taken = [scalars.taken[i, j - 1] for i in range(j)]
-    if j == KRYLOV - 1:
-        near_ref = far_ref = None
+    q_ref, g_ref, w_ref = refs[:3]
+    refs = refs[3:]
+    near_ref = far_ref = None
+    if not final:
+        near_ref, far_ref = refs[:2]
+        refs = refs[2:]
+    sum_ref, y_ref = refs[:2]
+    if j == 0:
+        tail_ref = refs[2]
+        coefficients(plan, recv_ref, strip, table_ref)
     center = table_ref[0]
     inverse = table_ref[1]
     north, south, west, east = (table_ref[2 + k] for k in range(4))
     zero = jnp.zeros(shape, jnp.float32)
-
-    def around(field):
+    low_zero = jnp.zeros((SUB, LANE), jnp.float32)
+    inner = slice(SUB, SUB + rows)
+
+    def around(n, field):
         return (
-            north * spin(field, 1, 0)
-            + south * spin(field, -1, 0)
+            north * g_ref[n, SUB - 1 : SUB - 1 + rows, :]
+            + south * g_ref[n, SUB + 1 : SUB + 1 + rows, :]
             + west * spin(field, 1)
             + east * spin(field, -1)
         )
@@ -460,108 +526,156 @@
             distance *= 2
         return total * closing
 
-    def loop(body, carry):
-        def several(i, carry):
+    def settle(base, y):
+        for k in range(UNROLL):
+            y = (y_ref[base + k] + y) * inverse
+            y_ref[base + k] = y
+        return y
+
+    for k in range(UNROLL):
+        y_ref[k] = zero
+
+    def blank(n):
+        g_ref[n] = jnp.zeros((rows + 2 * SUB, LANE), jnp.float32)
+
+    if j == 0:
+        last_tile = plan.tiles - 1
+
+        def tails(k, carry):
+            for p in (2 * k, 2 * k + 1):
+                for s in range(plan.space):
+                    source = p * plan.space + s
+                    total = low_zero
+                    for a in range(last_tile):
+                        tile = recv_ref[pl.ds(source * plan.inward + a * SUB, SUB), :]
+                        moved = spin(tile, plan.spare * a - plan.used)
+                        total = jnp.where(low_spot // plan.spare == a, moved, total)
+                    tail_ref[source] = total
+            return carry
+
+        lax.fori_loop(0, plan.tm // 2, tails, 0)
+
+        def first(a, y):
+            whole = a < last_tile
+            at = jnp.minimum(a, last_tile - 1) * SUB
+            parts = []
+            for s in range(plan.space):
+                cut = []
+                for p in range(plan.tm):
+                    source = p * plan.space + s
+                    tile = recv_ref[pl.ds(source * plan.inward + at, SUB), :]
+                    cut.append(damping * jnp.where(whole, tile, tail_ref[source]))
+                parts.append(exchange_blocks(cut, window, SUB))
+            for i in range(SUB):
+                n = a * SUB + i
+                q = jnp.concatenate([part[i] for part in parts], axis=0)
+                q_ref[n] = q
+                y = (q + y) * inverse
+                y_ref[UNROLL + n] = y
+                blank(n)
+            return y
+
+        y = lax.fori_loop(0, plan.tiles, first, zero)
+    else:
+        near_side = jnp.where(even, halo + own, 0)
+        far_side = jnp.where(even, 0, halo + own)
+        near_mask = (low_spot >= near_side) & (low_spot < near_side + halo)
+        far_mask = (low_spot >= far_side) & (low_spot < far_side + halo)
+
+        def first(i, y):
+            base = i * UNROLL
+            y = settle(base, y)
             for k in range(UNROLL):
-                carry = body(i * UNROLL + k, carry)
-            return carry
-
-        return lax.fori_loop(0, here // UNROLL, several, carry)
-
-    slot = plan.slot
-    left_spot = (spot < halo,)
-    first_side = jnp.where(even, halo + plan.own, 0)
-    second_side = jnp.where(even, 0, halo + plan.own)
-
-    def side_mask(start):
-        return (low_spot >= start) & (low_spot < start + halo)
-
-    near_mask = side_mask(first_side)
-    far_mask = side_mask(second_side)
-
-    def merged(n):
-        image = image_ref[n]
-        near = near_in[n]
-        far = far_in[n]
-        parts = []
-        for s in range(plan.space):
-            part = image[s * SUB : (s + 1) * SUB]
-            part = jnp.where(near_mask, pltpu.roll(near, (first_side - slot * s + LANE) % LANE, 1), part)
-            part = jnp.where(far_mask, pltpu.roll(far, (second_side - slot * s + LANE) % LANE, 1), part)
-            parts.append(part)
-        return jnp.concatenate(parts, axis=0)
-
-    def first(n, y):
-        if j == 0:
-            q = q_ref[n]
-        else:
-            q = merged(n)
-            for i in range(j):
-                q = q - taken[i] * older[i][n]
-            q_ref[n] = q
-        y = (q + y) * inverse
-        y_ref[n] = y
-        return y
-
-    y = loop(first, zero)
-
-    def sweep(step):
-        def body(n, carry):
+                n = base + k
+                near, far = near_in[n], far_in[n]
+                image = image_ref[n]
+                parts = []
+                for s in range(plan.space):
+                    part = image[s * SUB : (s + 1) * SUB]
+                    shift = LANE - slot * s
+                    part = jnp.where(near_mask, pltpu.roll(near, (near_side + shift) % LANE, 1), part)
+                    part = jnp.where(far_mask, pltpu.roll(far, (far_side + shift) % LANE, 1), part)
+                    parts.append(part)
+                q = jnp.concatenate(parts, axis=0)
+                for t, ref in zip(taken, older):
+                    q = q - t * ref[n]
+                q_ref[n] = q
+                y_ref[UNROLL + n] = q
+                blank(n)
+            return y
+
+        y = settle(here, lax.fori_loop(0, here // UNROLL, first, zero))
+
+    def sweep(_, ends):
+        def body(i, carry):
             y, z = carry
-            z = z * inverse
-            guess = damping * (y_ref[n] + z)
-            if step:
-                guess = (1.0 - damping) * g_ref[n] + guess
-            g_ref[n] = guess
-            y = (q_ref[n] + around(guess) + y) * inverse
-            y_ref[n] = y
+            base = i * UNROLL
+            olds = [y_ref[UNROLL + base + k] for k in range(UNROLL)]
+            y = settle(base, y)
+            for k in range(UNROLL):
+                n = base + k
+                z = z * inverse
+                guess = (1.0 - damping) * g_ref[n, inner, :] + (olds[k] + z)
+                g_ref[n, inner, :] = guess
+                y_ref[UNROLL + n] = q_ref[n] + around(n, guess)
             return (y, z)
 
-        return body
-
-    for step in range(SWEEPS - 1):
-        y, _ = loop(sweep(step), (zero, entering(y)))
+        y, _ = lax.fori_loop(0, here // UNROLL, body, (zero, entering(ends)))
+        return settle(here, y)
+
+    y = lax.fori_loop(0, SWEEPS - 1, sweep, y)
     start = entering(y)
-    ending = (1.0 - damping) * g_ref[here - 1] + damping * (y + start * power)
-    before = jnp.where(lane < window, 0.0, spin(ending, window))
-
-    near_from = jnp.where(even, plan.own, halo)
-    far_from = jnp.where(even, halo, plan.own)
-    fields = 1 + j + (j + 1) + (1 if j == KRYLOV - 1 else 0)
+    ending = (1.0 - damping) * g_ref[here - 1, inner, :] + (y + start * power)
+    before = jnp.where(lane < window, 0.0, damping * spin(ending, window))
+
+    near_from = jnp.where(even, own, halo)
+    far_from = jnp.where(even, halo, own)
 
     def fold(block):
         return sum(block[s * SUB : (s + 1) * SUB] for s in range(plan.space))
 
-    def last(n, carry):
+    def gather(base, accs):
+        for k in range(UNROLL):
+            n = base + k
+            image = w_ref[n]
+            if not final:
+                near = far = None
+                for s in range(plan.space):
+                    part = image[s * SUB : (s + 1) * SUB]
+                    a = pltpu.roll(part, (slot * s - near_from + LANE) % LANE, 1)
+                    b = pltpu.roll(part, (slot * s - far_from + LANE) % LANE, 1)
+                    inside = low_spot // slot == s
+                    near = a if near is None else jnp.where(inside, a, near)
+                    far = b if far is None else jnp.where(inside, b, far)
+                near_ref[n] = near
+                far_ref[n] = far
+            q = q_ref[n]
+            olds = [ref[n] for ref in older]
+            products = [q * q] + [old * q for old in olds] + [old * image for old in olds]
+            products.append(q * image)
+            if final:
+                products.append(image * image)
+            accs = [acc + fold(product) for acc, product in zip(accs, products)]
+        return accs
+
+    def last(i, carry):
         z, before, accs = carry
-        z = z * inverse
-        guess = (1.0 - damping) * g_ref[n] + damping * (y_ref[n] + z)
-        z_ref[n] = guess
-        image = center * guess - around(guess) - before
-        w_ref[n] = image
-        if near_ref is not None:
-            near = far = None
-            for s in range(plan.space):
-                part = image[s * SUB : (s + 1) * SUB]
-                a = pltpu.roll(part, (slot * s - near_from + LANE) % LANE, 1)
-                b = pltpu.roll(part, (slot * s - far_from + LANE) % LANE, 1)
-                inside = low_spot // slot == s
-                near = a if near is None else jnp.where(inside, a, near)
-                far = b if far is None else jnp.where(inside, b, far)
-            near_ref[n] = near
-            far_ref[n] = far
-        q = q_ref[n]
-        olds = [ref[n] for ref in older]
-        products = [q * q] + [old * q for old in olds] + [old * image for old in olds] + [q * image]
-        if j == KRYLOV - 1:
-            products.append(image * image)
-        accs = tuple(acc + fold(product) for acc, product in zip(accs, products))
-        return (z, guess, accs)
-
-    low_zero = jnp.zeros((SUB, LANE), jnp.float32)
-    _, _, accs = loop(last, (start, before, (low_zero,) * fields))
+        accs = gather(jnp.maximum(i - 1, 0) * UNROLL, accs)
+        accs = tuple(jnp.where(i > 0, acc, 0.0) for acc in accs)
+        for k in range(UNROLL):
+            n = i * UNROLL + k
+            z = z * inverse
+            guess = (1.0 - damping) * g_ref[n, inner, :] + (y_ref[UNROLL + n] + z)
+            g_ref[n, inner, :] = guess
+            w_ref[n] = center * guess - around(n, guess) - before
+            before = damping * guess
+        return (z, before, accs)
+
+    fields = 2 * (j + 1) + (1 if final else 0)
+    _, _, accs = lax.fori_loop(0, here // UNROLL, last, (start, before, (low_zero,) * fields))
+    accs = gather(here - UNROLL, list(accs))
     places = [0] + [1 + i for i in range(j)] + [KRYLOV + i for i in range(j + 1)] + [2 * KRYLOV]
-    owned = (low_spot >= halo) & (low_spot < halo + plan.own)
+    owned = (low_spot >= halo) & (low_spot < halo + own)
     record = jnp.zeros((1, LANE), jnp.float32)
     record_lane = lane_of((1, LANE))
     for place, acc in zip(places, accs):
@@ -572,63 +686,130 @@
 
 
 def combine_kernel(plan, *refs):
-    q_refs = refs[:KRYLOV]
-    z_refs = refs[KRYLOV : 2 * KRYLOV]
-    image_ref = refs[2 * KRYLOV]
-    sums = refs[2 * KRYLOV + 1 : 3 * KRYLOV + 1]
+    z_refs = refs[:KRYLOV]
+    sums = refs[KRYLOV : 2 * KRYLOV]
     out_ref = refs[-1]
     totals = [totals_of(ref) for ref in sums]
-    scalars = Scalars(totals)
-    along, rest, tail = scalars.finish(pick(totals[-1], 2 * KRYLOV))
-    own, halo, window = plan.own, plan.halo, plan.window
-    front = lane_of((SUB, LANE)) % window < own
-    groups = plan.here // (2 * SUB)
+    along = Scalars(totals).finish(pick(totals[-1], 2 * KRYLOV))
+    own, halo, window, groups = plan.own, plan.halo, plan.window, plan.groups
+    lane = lane_of((SUB, LANE))
+    front = lane % window < own
+    size = plan.outward
+
+    def start_of(p, s):
+        return (p * plan.space + s) * size
+
+    def value(n, s):
+        here = slice((s + 1) * SUB, (s + 2) * SUB)
+        return sum(c * ref[n, here, :] for c, ref in zip(along, z_refs))
 
     def body(aa, carry):
         for s in range(plan.space):
-            here = slice(s * SUB, (s + 1) * SUB)
-
-            def solution_at(n):
-                return sum(c * ref[n, here, :] for c, ref in zip(along, z_refs))
-
-            def residual_at(n):
-                total = tail * image_ref[n, here, :]
-                for c, ref in zip(rest, q_refs):
-                    total = total + c * ref[n, here, :]
-                return total
-
-            for f, value in enumerate((solution_at, residual_at)):
-                pieces = []
-                for i in range(SUB):
-                    n = aa * 2 * SUB + 2 * i
-                    pieces.append(
-                        jnp.where(front, spin(value(n), -halo), spin(value(n + 1), own - halo))
-                    )
-                start = pl.multiple_of((f * groups + aa) * SUB, SUB)
-                for p, piece in enumerate(exchange_blocks(pieces, window)):
-                    out_ref[p * plan.space + s, pl.ds(start, SUB), :] = piece
+            pieces = []
+            for i in range(SUB):
+                n = aa * 2 * SUB + 2 * i
+                pieces.append(
+                    jnp.where(front, spin(value(n, s), -halo), spin(value(n + 1, s), own - halo))
+                )
+            for p, piece in enumerate(exchange_blocks(pieces, window, SUB)):
+                out_ref[pl.ds(start_of(p, s) + aa * SUB, SUB), :] = piece
+                if s + 1 < plan.space:
+                    at = start_of(p, s + 1) + groups * SUB + aa
+                    out_ref[pl.ds(at, 1), :] = piece[SUB - 1 :]
+                if s > 0:
+                    at = start_of(p, s - 1) + groups * SUB + groups + aa
+                    out_ref[pl.ds(at, 1), :] = piece[:1]
         return carry
 
     lax.fori_loop(0, groups, body, 0)
-
-
-def unpack_kernel(plan, recv_ref, *out_refs):
-    groups = plan.here // (2 * SUB)
-    count = LANE // plan.own
-
-    def body(aa, carry):
-        for f, out_ref in enumerate(out_refs):
-            start = pl.multiple_of((f * groups + aa) * SUB, SUB)
-            for part in range(plan.cols // LANE):
-                pieces = [
-                    recv_ref[plan.holder[part * count + m], pl.ds(start, SUB), :]
-                    for m in range(count)
-                ]
-                for i, piece in enumerate(exchange_blocks(pieces, plan.own)):
-                    out_ref[aa * count + i, :, part * LANE : (part + 1) * LANE] = piece
-        return carry
-
-    lax.fori_loop(0, groups, body, 0)
+    nothing = jnp.zeros((groups, LANE), jnp.float32)
+    sub = lax.broadcasted_iota(jnp.int32, (SUB, LANE), 0)
+    for p in range(plan.tm):
+        at = start_of(p, 0) + groups * SUB
+        out_ref[at : at + groups, :] = nothing
+        at = start_of(p, plan.space - 1) + groups * SUB + groups
+        out_ref[at : at + groups, :] = nothing
+    for s in range(plan.space):
+        ending = value(plan.here - 1, s)
+        for p in range(plan.tm):
+            line = nothing[:1]
+            if p > 0:
+                turned = spin(ending, -(p - 1) * window - halo)
+                turned = pltpu.roll(turned, 0, 1, stride=own, stride_axis=0)
+                line = jnp.sum(jnp.where(lane // own == sub, turned, 0.0), axis=0, keepdims=True)
+            at = start_of(p, s) + size - 1
+            out_ref[at : at + 1, :] = line
+
+
+def finish_kernel(plan, recv_ref, right_ref, diff_ref, vel_ref, out_ref, rest_ref, rim_ref):
+    groups, own, size = plan.groups, plan.own, plan.outward
+    count = LANE // own
+    parts = plan.cols // LANE
+    shape = (SUB, plan.cols)
+    lane = lane_of((SUB, LANE))
+    diff, vel_col, vel_row = diff_ref[...], vel_ref[0], vel_ref[1]
+    col = lane_of(shape)
+    sub = lax.broadcasted_iota(jnp.int32, shape, 0)
+    center = 1.0 + 4.0 * diff
+    north = diff + vel_row
+    south = diff - vel_row
+    west = jnp.where(col > 0, diff + vel_col, 0.0)
+    east = jnp.where(col < plan.cols - 1, diff - vel_col, 0.0)
+
+    def start_of(part, m):
+        return plan.holder[part * count + m] * size
+
+    def spread(offset):
+        wide = []
+        for part in range(parts):
+            pieces = [
+                recv_ref[pl.ds(start_of(part, m) + offset, SUB), :] for m in range(count)
+            ]
+            wide.append(exchange_blocks(pieces, own, 4))
+        return [jnp.concatenate(pair, axis=1) for pair in zip(*wide)]
+
+    for i, field in enumerate(spread(groups * SUB)):
+        rim_ref[i] = field
+    halves = []
+    row = lax.broadcasted_iota(jnp.int32, (SUB, LANE), 0)
+    for part in range(parts):
+        tiles = []
+        for first in range(0, count, SUB):
+            tile = jnp.zeros((SUB, LANE), jnp.float32)
+            for q in range(SUB):
+                at = start_of(part, first + q) + size - 1
+                line = jnp.broadcast_to(recv_ref[at : at + 1, :], (SUB, LANE))
+                tile = jnp.where(row == q, line, tile)
+            tile = spin(tile, first * own)
+            tiles.append((first, pltpu.roll(tile, 0, 1, stride=own, stride_axis=0)))
+        total = jnp.zeros((SUB, LANE), jnp.float32)
+        for r in range(SUB):
+            line = sum(
+                jnp.where(lane // own == row + first, spin(tile, -r * own), 0.0)
+                for first, tile in tiles
+            )
+            line = jnp.sum(line, axis=0, keepdims=True)
+            total = jnp.where(row == r, jnp.broadcast_to(line, (SUB, LANE)), total)
+        halves.append(total)
+    before = jnp.concatenate(halves, axis=1)
+
+    def body(aa, before):
+        for i, field in enumerate(spread(aa * SUB)):
+            n = aa * count + i
+            above = rim_ref[i, pl.ds(aa, 1), :]
+            below = rim_ref[i, pl.ds(groups + aa, 1), :]
+            out_ref[n] = field
+            around = (
+                north * jnp.where(sub == 0, above, spin(field, 1, 0))
+                + south * jnp.where(sub == SUB - 1, below, spin(field, -1, 0))
+                + west * spin(field, 1)
+                + east * spin(field, -1)
+            )
+            rest_ref[n] = right_ref[n] - (center * field - around - before)
+            before = field
+        return before
+
+    lax.fori_loop(0, groups, body, before)
 
 
 def call(kernel, shapes, operands, scalars=0, scratch=()):
@@ -640,12 +821,14 @@
         in_specs=[smem] * scalars + [vmem] * (len(operands) - scalars),
         out_specs=[vmem] * len(shapes),
         scratch_shapes=[pltpu.VMEM(shape, jnp.float32) for shape in scratch],
-        compiler_params=pltpu.CompilerParams(vmem_limit_bytes=48 * 1024 * 1024),
+        compiler_params=pltpu.CompilerParams(vmem_limit_bytes=16 * 1024 * 1024),
     )(*operands)
 
 
-def everyone(block):
-    return lax.all_to_all(block, AXES, split_axis=0, concat_axis=0, tiled=True)
+def everyone(block, devices):
+    lines = block.shape[0] // devices
+    parts = block.reshape(devices, lines, 1, LANE)
+    return lax.all_to_all(parts, AXES, split_axis=0, concat_axis=0, tiled=True).reshape(block.shape)
 
 
 def strip_device(plan, right_side, diffusion, velocity):
@@ -662,37 +845,53 @@
         far_route += [(hold[k], hold[k + 1]), (hold[k + 1], hold[k])]
     bind = lambda kernel, *more: (lambda *refs: kernel(plan, *more, *refs))
     full = (plan.here, plan.rows, LANE)
+    padded = (plan.here, plan.rows + 2 * SUB, LANE)
+    delayed = (plan.here + UNROLL, plan.rows, LANE)
     side = (plan.here, SUB, LANE)
     small = (count, LANE)
-    sent = call(bind(pack_kernel), [(count, plan.here, LANE)], [right_side, diffusion, velocity])[0]
-    recv = everyone(sent)
+    given = [right_side, diffusion, velocity]
+    sent = call(
+        bind(pack_kernel),
+        [(count * plan.inward, LANE)],
+        [t.astype(jnp.int32).reshape(1), *given],
+        scalars=1,
+        scratch=[(count, SUB, LANE)],
+    )[0]
     table, q, z, image, near, far, sums = call(
         bind(krylov_kernel, 0),
-        [(6, plan.rows, LANE), full, full, full, side, side, small],
-        [strip, recv],
+        [(6, plan.rows, LANE), full, padded, full, side, side, small],
+        [strip, everyone(sent, count)],
         scalars=1,
-        scratch=[full, full],
+        scratch=[delayed, (count, SUB, LANE)],
     )
     qs, zs, totals = [q], [z], []
     for j in range(1, KRYLOV):
         near = lax.ppermute(near, AXES, near_route)
         far = lax.ppermute(far, AXES, far_route)
-        totals.append(everyone(sums))
-        q, z, image, near, far, sums = call(
+        totals.append(everyone(sums, count))
+        sides = [side, side] if j < KRYLOV - 1 else []
+        q, z, image, *sides, sums = call(
             bind(krylov_kernel, j),
-            [full, full, full, side, side, small],
+            [full, padded, full, *sides, small],
             [strip, table, image, near, far, *qs, *totals],
             scalars=1,
-            scratch=[full, full],
+            scratch=[delayed],
         )
+        if sides:
+            near, far = sides
         qs.append(q)
         zs.append(z)
-    totals.append(everyone(sums))
-    packed = call(
-        bind(combine_kernel), [(count, plan.here, LANE)], [*qs, *zs, image, *totals]
-    )[0]
+    totals.append(everyone(sums, count))
+    packed = call(bind(combine_kernel), [(count * plan.outward, LANE)], [*zs, *totals])[0]
     shape = right_side.shape
-    return tuple(call(bind(unpack_kernel), [shape, shape], [everyone(packed)]))
+    return tuple(
+        call(
+            bind(finish_kernel),
+            [shape, shape],
+            [everyone(packed, count), *given],
+            scratch=[(2 * SUB, SUB, plan.cols)],
+        )
+    )
 
 
 def per_device(mesh):

time: 142 us -> 123 us (0.87)
  blocking collectives: 60 us -> 52.3 us
  local copies, waits for them, and re-layouts: 7.39 us -> 2.46 us
  Pallas kernels: 38.4 us -> 34.1 us
  waiting for transfers between devices: 26.2 us -> 23.7 us
    all_to_all x4, blocking collectives: 60 us -> 52.3 us  [everyone(): lax.all_to_all(parts, AXES, split_axis=0, concat_axis=0, tiled=True)]
    unnamed x20 -> x12, local copies, waits for them, and re-layouts: 7.39 us -> 2.46 us
    pallas_call x6, Pallas kernels: 38.4 us -> 34.1 us  [call(): pl.pallas_call(kernel, out_shape=[jax.ShapeDtypeStruct(shape, jnp.float32...]
    all_to_all x1, waiting for transfers between devices: 26.2 us -> 23.7 us  [everyone(): lax.all_to_all(parts, AXES, split_axis=0, concat_axis=0, tiled=True)]
where the time goes in v2:
time: 123 us; the launch traced here: 122 us
  blocking collectives  52.3 us (43%)
  Pallas kernels  34.1 us (28%)
  waiting for transfers between devices  23.7 us (19%)
  starting transfers between devices  8.82 us (7%)
  local copies, waits for them, and re-layouts  2.46 us (2%)
    all_to_all x4, blocking collectives, everyone(): lax.all_to_all(parts, AXES, split_axis=0, concat_axis=0, tiled=True)  52.3 us
    pallas_call x6, Pallas kernels, call(): pl.pallas_call(kernel, out_shape=[jax.ShapeDtypeStruct(shape, jnp.float32...  34.1 us
    all_to_all x1, waiting for transfers between devices, everyone(): lax.all_to_all(parts, AXES, split_axis=0, concat_axis=0, tiled=True)  23.7 us
    all_to_all x1, starting transfers between devices, everyone(): lax.all_to_all(parts, AXES, split_axis=0, concat_axis=0, tiled=True)  7.33 us
    unnamed x12, local copies, waits for them, and re-layouts  2.46 us
  transfers between devices with their start and end apart: 5, of which 1 were waited for; matrix products, arithmetic and copies ran while one was open for 0% of the time, Pallas kernels for 0%

profile of v2, /device:TPU:0, one launch (start us, length us, event | category | flops | bytes accessed | tf_op | source)
XLA Modules:
  0.0 122.1 jit_solution(6996355984237286496)
XLA Ops:
  0.6 0.0 copy-start
  0.6 1.0 copy-done
  1.7 0.0 copy-start.2
  1.7 0.7 copy-done.2
  2.4 0.0 copy-start.4
  2.4 0.7 copy-done.4
  3.1 4.5 %shard_map.50 = f32[1824,128]{1,0:T(8,128)} custom-call(s32[1]{0:T(128)} %bitcast.1.refs_0_, f32[64,8,256]{2,1,0:T(8,128)S(1)} %copy-done, f32[8,256]{1,0:T(8,128)S(1)} %copy-done.4, f32[2,8,256]{2,1,0:T(8,128)S(1)} %copy-done.2), custom_call_target="tpu_custom_call" | custom-call | tf_op jit(solution)/shard_map/pallas_call | solution.py:818
  7.6 7.3 %all-to-all-start = ((f32[32,57,1,128]{3,2,1,0:T(1,128)}), f32[32,57,1,128]{3,2,1,0:T(1,128)S(1)}, u32[]{:S(2)}, u32[]{:S(2)}) async-start(f32[32,57,1,128]{3,2,1,0:T(1,128)} %bitcast.2), calls=%async_computation | async-start | bytes 1867776 | tf_op jit(solution)/shard_map/all_to_all | solution.py:831
  15.0 23.7 %all-to-all-done = f32[32,57,1,128]{3,2,1,0:T(1,128)S(1)} async-done(((f32[32,57,1,128]{3,2,1,0:T(1,128)}), f32[32,57,1,128]{3,2,1,0:T(1,128)S(1)}, u32[]{:S(2)}, u32[]{:S(2)}) %all-to-all-start) | async-done | bytes 933920 | tf_op jit(solution)/shard_map/all_to_all | solution.py:831
  38.7 8.7 %shard_map.51 = (f32[6,32,128]{2,1,0:T(8,128)S(1)}, f32[64,32,128]{2,1,0:T(8,128)S(1)}, f32[64,48,128]{2,1,0:T(8,128)S(1)}, f32[64,32,128]{2,1,0:T(8,128)S(1)}, ...) custom-call(s32[1]{0:T(128)} %bitcast.refs_0_, f32[1824,128]{1,0:T(8,128)S(1)} %bitcast.18), custom_call_target="tpu_custom_call" | custom-call | tf_op jit(solution)/shard_map/pallas_call | solution.py:818
  47.4 0.1 collective-permute-start
  47.5 0.7 collective-permute-start.1
  48.2 12.5 %all_to_all.25 = f32[32,1,1,128]{3,2,1,0:T(1,128)S(1)} all-to-all(f32[32,1,1,128]{3,2,1,0:T(1,128)S(1)} %bitcast.28), channel_id=1, replica_groups=mesh['tm'=8,'space'=4] {'tm','space'}, dimensions={0} | all-to-all | bytes 32768 | tf_op jit(solution)/shard_map/all_to_all | solution.py:831
  60.7 0.0 collective-permute-done.refs_3_
  60.7 0.0 collective-permute-done.1.refs_4_
  60.7 6.8 %shard_map.52 = (f32[64,32,128]{2,1,0:T(8,128)S(1)}, f32[64,48,128]{2,1,0:T(8,128)S(1)}, f32[64,32,128]{2,1,0:T(8,128)S(1)}, f32[64,8,128]{2,1,0:T(8,128)S(1)}, ...) custom-call(s32[1]{0:T(128)} %bitcast.refs_0_, f32[6,32,128]{2,1,0:T(8,128)S(1)} %get-tuple-element.18.refs_1_, ...), custom_call_target="tpu_custom_call" | custom-call | tf_op jit(solution)/shard_map/pallas_call | solution.py:818
  67.6 0.1 collective-permute-start.2
  67.7 0.7 collective-permute-start.3
  68.3 10.7 %all_to_all.26 = f32[32,1,1,128]{3,2,1,0:T(1,128)S(1)} all-to-all(f32[32,1,1,128]{3,2,1,0:T(1,128)S(1)} %bitcast.27), channel_id=1, replica_groups=mesh['tm'=8,'space'=4] {'tm','space'}, dimensions={0} | all-to-all | bytes 32768 | tf_op jit(solution)/shard_map/all_to_all | solution.py:831
  79.1 0.0 collective-permute-done.2.refs_3_
  79.1 0.0 collective-permute-done.3.refs_4_
  79.1 7.9 %shard_map.53 = (f32[64,32,128]{2,1,0:T(8,128)}, f32[64,48,128]{2,1,0:T(8,128)S(1)}, f32[64,32,128]{2,1,0:T(8,128)}, f32[32,128]{1,0:T(8,128)S(1)}) custom-call(s32[1]{0:T(128)} %bitcast.refs_0_, f32[6,32,128]{2,1,0:T(8,128)S(1)} %get-tuple-element.18.refs_1_, f32[64,32,128]{2,1,0:T(8,128)S(1)} %get-tuple-element.25.refs_2_, ...), custom_call_target="tpu_custom_call" | custom-call | tf_op jit(solution)/shard_map/pallas_call | solution.py:818
  87.0 8.9 %all_to_all.27 = f32[32,1,1,128]{3,2,1,0:T(1,128)S(1)} all-to-all(f32[32,1,1,128]{3,2,1,0:T(1,128)S(1)} %bitcast.29), channel_id=1, replica_groups=mesh['tm'=8,'space'=4] {'tm','space'}, dimensions={0} | all-to-all | bytes 32768 | tf_op jit(solution)/shard_map/all_to_all | solution.py:831
  95.9 0.0 copy-start.3
  95.9 0.0 copy-start.5
  95.9 2.8 %shard_map.54 = f32[1312,128]{1,0:T(8,128)S(1)} custom-call(f32[64,48,128]{2,1,0:T(8,128)S(1)} %get-tuple-element.17.refs_0_, f32[64,48,128]{2,1,0:T(8,128)S(1)} %get-tuple-element.24.refs_1_, f32[64,48,128]{2,1,0:T(8,128)S(1)} %get-tuple-element.30.refs_2_, f32[32,128]{1,0:T(8,128)S(1)} %bitcast.23, f32[32,128]{1,0:T(8,128)S(1)} %bitcast.25, ...), custom_call_target="tpu_custom_call" | custom-call | tf_op jit(solution)/shard_map/pallas_call | solution.py:818
  98.7 0.0 copy-start.1
  98.7 20.1 %all_to_all.28 = f32[32,41,1,128]{3,2,1,0:T(1,128)S(1)} all-to-all(f32[32,41,1,128]{3,2,1,0:T(1,128)S(1)} %bitcast.20), channel_id=1, replica_groups=mesh['tm'=8,'space'=4] {'tm','space'}, dimensions={0} | all-to-all | bytes 1343488 | tf_op jit(solution)/shard_map/all_to_all | solution.py:831
  118.9 0.0 copy-done.3
  118.9 0.0 copy-done.5
  118.9 0.0 copy-done.1
  118.9 3.2 %shard_map.55 = (f32[64,8,256]{2,1,0:T(8,128)}, f32[64,8,256]{2,1,0:T(8,128)}) custom-call(f32[1312,128]{1,0:T(8,128)S(1)} %bitcast.19, f32[64,8,256]{2,1,0:T(8,128)S(1)} %copy-done.1, f32[8,256]{1,0:T(8,128)S(1)} %copy-done.5, f32[2,8,256]{2,1,0:T(8,128)S(1)} %copy-done.3), custom_call_target="tpu_custom_call" | custom-call | tf_op jit(solution)/shard_map/pallas_call | solution.py:818
Async XLA Ops:
  0.6 1.0 copy-start
  1.7 0.7 copy-start.2
  2.4 0.7 copy-start.4
  7.6 31.1 %all-to-all-start = ((f32[32,57,1,128]{3,2,1,0:T(1,128)}), f32[32,57,1,128]{3,2,1,0:T(1,128)S(1)}, u32[]{:S(2)}, u32[]{:S(2)}) async-start(f32[32,57,1,128]{3,2,1,0:T(1,128)} %bitcast.2), calls=%async_computation | async-start | bytes 1867776 | tf_op jit(solution)/shard_map/all_to_all | solution.py:831
  47.4 13.3 %collective-permute-start = (f32[64,8,128]{2,1,0:T(8,128)S(1)}, f32[64,8,128]{2,1,0:T(8,128)S(1)}, u32[]{:S(2)}, u32[]{:S(2)}) collective-permute-start(f32[64,8,128]{2,1,0:T(8,128)S(1)} %get-tuple-element.20), channel_id=1, source_target_pairs={{0,1},{1,0},{2,3},{3,2},{6,7},{7,6},{4,5},{5,4},{12,13},{13,12},{1... | collective-permute-start | bytes 786440 | tf_op jit(solution)/shard_map/ppermute | solution.py:869
  47.5 13.2 %collective-permute-start.1 = (f32[64,8,128]{2,1,0:T(8,128)S(1)}, f32[64,8,128]{2,1,0:T(8,128)S(1)}, u32[]{:S(2)}, u32[]{:S(2)}) collective-permute-start(f32[64,8,128]{2,1,0:T(8,128)S(1)} %get-tuple-element.21), channel_id=1, source_target_pairs={{1,2},{2,1},{3,6},{6,3},{7,4},{4,7},{5,12},{12,5},{13,14},{14,13},... | collective-permute-start | bytes 786440 | tf_op jit(solution)/shard_map/ppermute | solution.py:870
  67.6 11.5 %collective-permute-start.2 = (f32[64,8,128]{2,1,0:T(8,128)S(1)}, f32[64,8,128]{2,1,0:T(8,128)S(1)}, u32[]{:S(2)}, u32[]{:S(2)}) collective-permute-start(f32[64,8,128]{2,1,0:T(8,128)S(1)} %get-tuple-element.26), channel_id=1, source_target_pairs={{0,1},{1,0},{2,3},{3,2},{6,7},{7,6},{4,5},{5,4},{12,13},{13,12},{1... | collective-permute-start | bytes 786440 | tf_op jit(solution)/shard_map/ppermute | solution.py:869
  67.7 11.4 %collective-permute-start.3 = (f32[64,8,128]{2,1,0:T(8,128)S(1)}, f32[64,8,128]{2,1,0:T(8,128)S(1)}, u32[]{:S(2)}, u32[]{:S(2)}) collective-permute-start(f32[64,8,128]{2,1,0:T(8,128)S(1)} %get-tuple-element.27), channel_id=1, source_target_pairs={{1,2},{2,1},{3,6},{6,3},{7,4},{4,7},{5,12},{12,5},{13,14},{14,13},... | collective-permute-start | bytes 786440 | tf_op jit(solution)/shard_map/ppermute | solution.py:870
  95.9 23.0 %copy-start.3 = (f32[2,8,256]{2,1,0:T(8,128)S(1)}, f32[2,8,256]{2,1,0:T(8,128)}, u32[]{:S(2)}) copy-start(f32[2,8,256]{2,1,0:T(8,128)} %refs_3_.3) | copy-start | bytes 49156
  95.9 23.0 %copy-start.5 = (f32[8,256]{1,0:T(8,128)S(1)}, f32[8,256]{1,0:T(8,128)}, u32[]{:S(2)}) copy-start(f32[8,256]{1,0:T(8,128)} %refs_2_.3) | copy-start | bytes 24580
  98.7 20.2 %copy-start.1 = (f32[64,8,256]{2,1,0:T(8,128)S(1)}, f32[64,8,256]{2,1,0:T(8,128)}, u32[]{:S(2)}) copy-start(f32[64,8,256]{2,1,0:T(8,128)} %refs_1_.3) | copy-start | bytes 1572868

commit v3 on v2

--- a/solution.py
+++ b/solution.py
@@ -195,7 +195,7 @@
 SUB = 8
 LANE = 128
 AXES = ("tm", "space")
-UNROLL = 8
+UNROLL = 16
 
 
 def spin(block, amount, axis=1):
@@ -263,6 +263,8 @@
             and self.groups * 2 == SUB
             and self.slot >= self.halo
             and self.space % 2 == 0
+            and KRYLOV == 3
+            and self.tiles % (UNROLL // SUB) == 0
         )
 
     def strip_of(self, t, s):
@@ -368,64 +370,62 @@
     return jnp.broadcast_to(value, (1, LANE))
 
 
-class Scalars:
-    def __init__(self, sums):
-        self.norms = []
-        self.scale = []
-        self.cross = {}
-        self.inner = {}
-        self.taken = {}
-        self.below = []
-        for j, totals in enumerate(sums):
-            norm = pick(totals, 0)
-            self.norms.append(norm)
-            if j == 0:
-                self.beta = jnp.sqrt(norm + epsilon)
-                self.scale.append(1.0 / self.beta)
-            else:
-                before = self.scale[j - 1]
-                length = jnp.sqrt(before * before * norm + epsilon)
-                self.below.append(length)
-                self.scale.append(before / length)
-            for i in range(j):
-                self.cross[i, j] = pick(totals, 1 + i)
-            for i in range(j + 1):
-                self.inner[i, j] = pick(totals, KRYLOV + i)
-                self.taken[i, j] = self.scale[i] * self.scale[i] * self.inner[i, j]
-
-    def finish(self, square):
-        last = KRYLOV - 1
-        for i in range(KRYLOV):
-            square = square - 2.0 * self.taken[i, last] * self.inner[i, last]
-            for k in range(KRYLOV):
-                pair = self.norms[i] if i == k else self.cross[min(i, k), max(i, k)]
-                square = square + self.taken[i, last] * self.taken[k, last] * pair
-        scale = self.scale[last]
-        self.below.append(jnp.sqrt(jnp.maximum(scale * scale * square, 0.0) + epsilon))
-        zero = jnp.zeros_like(self.beta)
-        hessen = [[zero] * KRYLOV for row in range(KRYLOV + 1)]
-        for j in range(KRYLOV):
-            for i in range(j + 1):
-                hessen[i][j] = self.scale[i] * self.scale[j] * self.inner[i, j]
-            hessen[j + 1][j] = self.below[j]
-        ortho = []
-        upper = [[None] * KRYLOV for row in range(KRYLOV)]
-        for column in range(KRYLOV):
-            current = [hessen[row][column] for row in range(KRYLOV + 1)]
-            for row in range(column):
-                factor = sum(a * b for a, b in zip(ortho[row], current))
-                upper[row][column] = factor
-                current = [b - factor * a for a, b in zip(ortho[row], current)]
-            length = jnp.sqrt(sum(b * b for b in current))
-            upper[column][column] = length
-            ortho.append([b / length for b in current])
-        values = [None] * KRYLOV
-        for row in reversed(range(KRYLOV)):
-            accum = ortho[row][0] * self.beta
-            for later in range(row + 1, KRYLOV):
-                accum = accum - upper[row][later] * values[later]
-            values[row] = accum / upper[row][row]
-        return [values[j] * self.scale[j] for j in range(KRYLOV)]
+def middle(totals):
+    aa, ab, bb, ac, bc = (pick(totals, k) for k in range(5))
+    scale = 1.0 / (aa + epsilon)
+    drop = scale * ab
+    norm = jnp.maximum(bb - drop * (2.0 * ab - drop * aa), 1e-5 * bb)
+    over = ac - drop * ab
+    along = bc - drop * (bb + ac - drop * ab)
+    return aa, drop, scale * over, scale * along / (scale * norm + epsilon)
+
+
+def iterate(middle_totals, totals):
+    aa, drop, over, along = middle(middle_totals)
+    pairs = [(0, 1), (1, 1), (0, 2), (1, 2), (2, 2), (0, 3), (1, 3), (2, 3), (3, 3)]
+    gram = {(0, 0): aa}
+    for k, (i, j) in enumerate(pairs):
+        gram[i, j] = gram[j, i] = pick(totals, k)
+    zero = jnp.zeros_like(aa)
+    one = jnp.ones_like(aa)
+    images = [[drop, one, zero, zero], [over, along, one, zero], [zero, zero, zero, one]]
+    size = KRYLOV + 1
+
+    def product(left, right):
+        return sum(left[i] * right[j] * gram[i, j] for i in range(size) for j in range(size))
+
+    beta = jnp.sqrt(aa + epsilon)
+    basis = [[1.0 / beta, zero, zero, zero]]
+    hessen = [[zero] * KRYLOV for row in range(size)]
+    for j in range(KRYLOV):
+        image = [sum(basis[j][k] * images[k][i] for k in range(KRYLOV)) for i in range(size)]
+        found = [product(basis[i], image) for i in range(j + 1)]
+        for i in range(j + 1):
+            hessen[i][j] = found[i]
+            image = [w - found[i] * v for w, v in zip(image, basis[i])]
+        length = jnp.sqrt(jnp.maximum(product(image, image), 0.0) + epsilon)
+        hessen[j + 1][j] = length
+        basis.append([w / length for w in image])
+    ortho = []
+    upper = [[None] * KRYLOV for row in range(KRYLOV)]
+    for column in range(KRYLOV):
+        current = [hessen[row][column] for row in range(size)]
+        for row in range(column):
+            factor = sum(x * y for x, y in zip(ortho[row], current))
+            upper[row][column] = factor
+            current = [y - factor * x for x, y in zip(ortho[row], current)]
+        length = jnp.sqrt(sum(y * y for y in current))
+        upper[column][column] = length
+        ortho.append([y / length for y in current])
+    values = [None] * KRYLOV
+    for row in reversed(range(KRYLOV)):
+        accum = ortho[row][0] * beta
+        for later in range(row + 1, KRYLOV):
+            accum = accum - upper[row][later] * values[later]
+        values[row] = accum / upper[row][row]
+    weights = [sum(values[j] * basis[j][k] for j in range(KRYLOV)) for k in range(KRYLOV)]
+    weights[0] = weights[0] - drop * weights[1]
+    return weights
 
 
 def coefficients(plan, recv_ref, strip, table_ref):
@@ -440,11 +440,10 @@
     for f in range(3):
         parts = []
         for line in lines:
-            part = jnp.where(lane < window, spin(line, -f * window), 0.0)
-            reach = window
-            while reach < LANE:
-                part = part + spin(part, reach)
-                reach *= 2
+            part = None
+            for g in range(plan.tm):
+                moved = spin(line, (g - f) * window)
+                part = moved if g == 0 else jnp.where(lane // window == g, moved, part)
             parts.append(part)
         fields.append(jnp.concatenate(parts, axis=0))
     diff, vel_col, vel_row = fields
@@ -471,27 +470,16 @@
     low_lane = lane_of((SUB, LANE))
     low_spot = low_lane % window
     even = strip % 2 == 0
-    older = []
     if j == 0:
-        recv_ref = refs.pop(0)
-        table_ref = refs.pop(0)
+        recv_ref, table_ref, q_ref, g_ref, w_ref, near_ref, far_ref, y_ref, tail_ref = refs
+        coefficients(plan, recv_ref, strip, table_ref)
+    elif not final:
+        table_ref, image_ref, near_in, far_in, first_ref = refs[:5]
+        q_ref, g_ref, w_ref, near_ref, far_ref, sum_ref, y_ref = refs[5:]
     else:
-        table_ref, image_ref, near_in, far_in = refs[:4]
-        older = refs[4 : 4 + j]
-        sums = refs[4 + j : 4 + 2 * j]
-        refs = refs[4 + 2 * j :]
-        scalars = Scalars([totals_of(ref) for ref in sums])
-        taken = [scalars.taken[i, j - 1] for i in range(j)]
-    q_ref, g_ref, w_ref = refs[:3]
-    refs = refs[3:]
-    near_ref = far_ref = None
-    if not final:
-        near_ref, far_ref = refs[:2]
-        refs = refs[2:]
-    sum_ref, y_ref = refs[:2]
-    if j == 0:
-        tail_ref = refs[2]
-        coefficients(plan, recv_ref, strip, table_ref)
+        table_ref, image_ref, near_in, far_in, first_ref, second_ref, mid_ref = refs[:7]
+        g_ref, sum_ref, y_ref, q_ref, w_ref, rest_ref = refs[7:]
+        _, drop, over, along = middle(totals_of(mid_ref))
     center = table_ref[0]
     inverse = table_ref[1]
     north, south, west, east = (table_ref[2 + k] for k in range(4))
@@ -510,20 +498,16 @@
     power = inverse
     for _ in range(int(math.log2(here))):
         power = power * power
-    opening = jnp.where(lane < window, alpha_corner, 1.0)
-    gains = [power * opening]
-    reach = window
-    while reach < LANE:
-        gains.append(gains[-1] * spin(gains[-1], reach))
-        reach *= 2
-    closing = 1.0 / (1.0 - gains[-1])
+    whole = power
+    for _ in range(int(math.log2(plan.tm))):
+        whole = whole * whole
+    closing = 1.0 / (1.0 - alpha_corner * whole)
 
     def entering(ends):
-        total = spin(ends, window) * opening
-        distance = window
-        for gain in gains[:-1]:
-            total = total + gain * spin(total, distance)
-            distance *= 2
+        total = alpha_corner * ends
+        for k in reversed(range(1, plan.tm)):
+            back = spin(ends, k * window)
+            total = total * power + jnp.where(lane < k * window, alpha_corner * back, back)
         return total * closing
 
     def settle(base, y):
@@ -555,27 +539,32 @@
 
         lax.fori_loop(0, plan.tm // 2, tails, 0)
 
-        def first(a, y):
-            whole = a < last_tile
-            at = jnp.minimum(a, last_tile - 1) * SUB
-            parts = []
-            for s in range(plan.space):
-                cut = []
-                for p in range(plan.tm):
-                    source = p * plan.space + s
-                    tile = recv_ref[pl.ds(source * plan.inward + at, SUB), :]
-                    cut.append(damping * jnp.where(whole, tile, tail_ref[source]))
-                parts.append(exchange_blocks(cut, window, SUB))
-            for i in range(SUB):
-                n = a * SUB + i
-                q = jnp.concatenate([part[i] for part in parts], axis=0)
-                q_ref[n] = q
-                y = (q + y) * inverse
-                y_ref[UNROLL + n] = y
-                blank(n)
+        pair = UNROLL // SUB
+
+        def first(k, y):
+            parts = [[] for _ in range(pair)]
+            for t in range(pair):
+                a = k * pair + t
+                whole = a < last_tile
+                at = jnp.minimum(a, last_tile - 1) * SUB
+                for s in range(plan.space):
+                    cut = []
+                    for p in range(plan.tm):
+                        source = p * plan.space + s
+                        tile = recv_ref[pl.ds(source * plan.inward + at, SUB), :]
+                        cut.append(damping * jnp.where(whole, tile, tail_ref[source]))
+                    parts[t].append(exchange_blocks(cut, window, 2))
+            for t in range(pair):
+                for i in range(SUB):
+                    n = k * UNROLL + t * SUB + i
+                    q = jnp.concatenate([part[i] for part in parts[t]], axis=0)
+                    q_ref[n] = q
+                    y = (q + y) * inverse
+                    y_ref[UNROLL + n] = y
+                    blank(n)
             return y
 
-        y = lax.fori_loop(0, plan.tiles, first, zero)
+        y = lax.fori_loop(0, plan.tiles // pair, first, zero)
     else:
         near_side = jnp.where(even, halo + own, 0)
         far_side = jnp.where(even, 0, halo + own)
@@ -597,8 +586,11 @@
                     part = jnp.where(far_mask, pltpu.roll(far, (far_side + shift) % LANE, 1), part)
                     parts.append(part)
                 q = jnp.concatenate(parts, axis=0)
-                for t, ref in zip(taken, older):
-                    q = q - t * ref[n]
+                if final:
+                    start, later = first_ref[n], second_ref[n]
+                    rest = later - drop * start
+                    rest_ref[n] = rest
+                    q = (q - drop * later) - over * start - along * rest
                 q_ref[n] = q
                 y_ref[UNROLL + n] = q
                 blank(n)
@@ -633,6 +625,8 @@
 
     def fold(block):
         return sum(block[s * SUB : (s + 1) * SUB] for s in range(plan.space))
+
+    size = KRYLOV + 1
 
     def gather(base, accs):
         for k in range(UNROLL):
@@ -649,13 +643,17 @@
                     far = b if far is None else jnp.where(inside, b, far)
                 near_ref[n] = near
                 far_ref[n] = far
+            if j == 0:
+                continue
             q = q_ref[n]
-            olds = [ref[n] for ref in older]
-            products = [q * q] + [old * q for old in olds] + [old * image for old in olds]
-            products.append(q * image)
-            if final:
-                products.append(image * image)
-            accs = [acc + fold(product) for acc, product in zip(accs, products)]
+            start = first_ref[n]
+            if not final:
+                pairs = [(start, start), (start, q), (q, q), (start, image), (q, image)]
+            else:
+                rest = rest_ref[n]
+                held = [start, rest, q, image]
+                pairs = [(held[i], held[k]) for k in range(1, size) for i in range(k + 1)]
+            accs = [acc + fold(x * y) for acc, (x, y) in zip(accs, pairs)]
         return accs
 
     def last(i, carry):
@@ -671,14 +669,15 @@
             before = damping * guess
         return (z, before, accs)
 
-    fields = 2 * (j + 1) + (1 if final else 0)
+    fields = (0, 5, 9)[j]
     _, _, accs = lax.fori_loop(0, here // UNROLL, last, (start, before, (low_zero,) * fields))
     accs = gather(here - UNROLL, list(accs))
-    places = [0] + [1 + i for i in range(j)] + [KRYLOV + i for i in range(j + 1)] + [2 * KRYLOV]
+    if j == 0:
+        return
     owned = (low_spot >= halo) & (low_spot < halo + own)
     record = jnp.zeros((1, LANE), jnp.float32)
     record_lane = lane_of((1, LANE))
-    for place, acc in zip(places, accs):
+    for place, acc in enumerate(accs):
         value = jnp.sum(jnp.where(owned, acc, 0.0), axis=0, keepdims=True)
         value = jnp.sum(value, axis=1, keepdims=True)
         record = jnp.where(record_lane == place, value, record)
@@ -687,10 +686,8 @@
 
 def combine_kernel(plan, *refs):
     z_refs = refs[:KRYLOV]
-    sums = refs[KRYLOV : 2 * KRYLOV]
-    out_ref = refs[-1]
-    totals = [totals_of(ref) for ref in sums]
-    along = Scalars(totals).finish(pick(totals[-1], 2 * KRYLOV))
+    mid_ref, end_ref, out_ref = refs[KRYLOV:]
+    along = iterate(totals_of(mid_ref), totals_of(end_ref))
     own, halo, window, groups = plan.own, plan.halo, plan.window, plan.groups
     lane = lane_of((SUB, LANE))
     front = lane % window < own
@@ -857,32 +854,34 @@
         scalars=1,
         scratch=[(count, SUB, LANE)],
     )[0]
-    table, q, z, image, near, far, sums = call(
+    table, q0, z0, image, near, far = call(
         bind(krylov_kernel, 0),
-        [(6, plan.rows, LANE), full, padded, full, side, side, small],
+        [(6, plan.rows, LANE), full, padded, full, side, side],
         [strip, everyone(sent, count)],
         scalars=1,
         scratch=[delayed, (count, SUB, LANE)],
     )
-    qs, zs, totals = [q], [z], []
-    for j in range(1, KRYLOV):
-        near = lax.ppermute(near, AXES, near_route)
-        far = lax.ppermute(far, AXES, far_route)
-        totals.append(everyone(sums, count))
-        sides = [side, side] if j < KRYLOV - 1 else []
-        q, z, image, *sides, sums = call(
-            bind(krylov_kernel, j),
-            [full, padded, full, *sides, small],
-            [strip, table, image, near, far, *qs, *totals],
-            scalars=1,
-            scratch=[delayed],
-        )
-        if sides:
-            near, far = sides
-        qs.append(q)
-        zs.append(z)
-    totals.append(everyone(sums, count))
-    packed = call(bind(combine_kernel), [(count * plan.outward, LANE)], [*zs, *totals])[0]
+    near = lax.ppermute(near, AXES, near_route)
+    far = lax.ppermute(far, AXES, far_route)
+    q1, z1, image, near, far, sums = call(
+        bind(krylov_kernel, 1),
+        [full, padded, full, side, side, small],
+        [strip, table, image, near, far, q0],
+        scalars=1,
+        scratch=[delayed],
+    )
+    near = lax.ppermute(near, AXES, near_route)
+    far = lax.ppermute(far, AXES, far_route)
+    mid = everyone(sums, count)
+    z2, sums = call(
+        bind(krylov_kernel, 2),
+        [padded, small],
+        [strip, table, image, near, far, q0, q1, mid],
+        scalars=1,
+        scratch=[delayed, full, full, full],
+    )
+    end = everyone(sums, count)
+    packed = call(bind(combine_kernel), [(count * plan.outward, LANE)], [z0, z1, z2, mid, end])[0]
     shape = right_side.shape
     return tuple(
         call(

time: 123 us -> 112 us (0.911)
  blocking collectives: 52.3 us -> 41.1 us
  Pallas kernels: 34.1 us -> 26.9 us
  starting transfers between devices: 8.82 us -> 15.5 us
    all_to_all x4 -> x3, blocking collectives: 52.3 us -> 41.1 us  [everyone(): lax.all_to_all(parts, AXES, split_axis=0, concat_axis=0, tiled=True)]
    pallas_call x6, Pallas kernels: 34.1 us -> 26.9 us  [call(): pl.pallas_call(kernel, out_shape=[jax.ShapeDtypeStruct(shape, jnp.float32...]
    ppermute x2, starting transfers between devices: 0.14 us -> 6.79 us  [strip_device(): near = lax.ppermute(near, AXES, near_route)]
  transfers between devices with their start and end apart: 5 -> 5, of which waited for: 1 -> 2; matrix products, arithmetic and copies ran while one was open for 0% -> 0% of each run, Pallas kernels for 0% -> 0%
where the time goes in v3:
time: 112 us; the launch traced here: 111 us
  blocking collectives  41.1 us (37%)
  Pallas kernels  26.9 us (24%)
  waiting for transfers between devices  24.5 us (22%)
  starting transfers between devices  15.5 us (14%)
  local copies, waits for them, and re-layouts  2.46 us (2%)
    all_to_all x3, blocking collectives, everyone(): lax.all_to_all(parts, AXES, split_axis=0, concat_axis=0, tiled=True)  41.1 us
    pallas_call x6, Pallas kernels, call(): pl.pallas_call(kernel, out_shape=[jax.ShapeDtypeStruct(shape, jnp.float32...  26.9 us
    all_to_all x1, waiting for transfers between devices, everyone(): lax.all_to_all(parts, AXES, split_axis=0, concat_axis=0, tiled=True)  23.7 us
    all_to_all x1, starting transfers between devices, everyone(): lax.all_to_all(parts, AXES, split_axis=0, concat_axis=0, tiled=True)  7.33 us
    ppermute x2, starting transfers between devices, strip_device(): near = lax.ppermute(near, AXES, near_route)  6.79 us
    unnamed x12, local copies, waits for them, and re-layouts  2.46 us
  transfers between devices with their start and end apart: 5, of which 2 were waited for; matrix products, arithmetic and copies ran while one was open for 0% of the time, Pallas kernels for 0%

profile of v3, /device:TPU:0, one launch (start us, length us, event | category | flops | bytes accessed | tf_op | source)
XLA Modules:
  0.0 111.2 jit_solution(10437470493512903586)
XLA Ops:
  0.6 0.0 copy-start
  0.6 1.0 copy-done
  1.7 0.0 copy-start.2
  1.7 0.7 copy-done.2
  2.4 0.0 copy-start.4
  2.4 0.7 copy-done.4
  3.1 4.5 %shard_map.50 = f32[1824,128]{1,0:T(8,128)} custom-call(s32[1]{0:T(128)} %bitcast.1.refs_0_, f32[64,8,256]{2,1,0:T(8,128)S(1)} %copy-done, f32[8,256]{1,0:T(8,128)S(1)} %copy-done.4, f32[2,8,256]{2,1,0:T(8,128)S(1)} %copy-done.2), custom_call_target="tpu_custom_call" | custom-call | tf_op jit(solution)/shard_map/pallas_call | solution.py:815
  7.6 7.3 %all-to-all-start = ((f32[32,57,1,128]{3,2,1,0:T(1,128)}), f32[32,57,1,128]{3,2,1,0:T(1,128)S(1)}, u32[]{:S(2)}, u32[]{:S(2)}) async-start(f32[32,57,1,128]{3,2,1,0:T(1,128)} %bitcast.2), calls=%async_computation | async-start | bytes 1867776 | tf_op jit(solution)/shard_map/all_to_all | solution.py:828
  15.0 23.7 %all-to-all-done = f32[32,57,1,128]{3,2,1,0:T(1,128)S(1)} async-done(((f32[32,57,1,128]{3,2,1,0:T(1,128)}), f32[32,57,1,128]{3,2,1,0:T(1,128)S(1)}, u32[]{:S(2)}, u32[]{:S(2)}) %all-to-all-start) | async-done | bytes 933920 | tf_op jit(solution)/shard_map/all_to_all | solution.py:828
  38.7 6.0 %shard_map.51 = (f32[6,32,128]{2,1,0:T(8,128)S(1)}, f32[64,32,128]{2,1,0:T(8,128)S(1)}, f32[64,48,128]{2,1,0:T(8,128)S(1)}, f32[64,32,128]{2,1,0:T(8,128)S(1)}, ...) custom-call(s32[1]{0:T(128)} %bitcast.refs_0_, f32[1824,128]{1,0:T(8,128)S(1)} %bitcast.14), custom_call_target="tpu_custom_call" | custom-call | tf_op jit(solution)/shard_map/pallas_call | solution.py:815
  44.7 0.1 collective-permute-start
  44.8 0.7 collective-permute-start.1
  45.4 0.8 collective-permute-done.refs_3_
  46.3 0.0 collective-permute-done.1.refs_4_
  46.3 5.0 %shard_map.52 = (f32[64,32,128]{2,1,0:T(8,128)S(1)}, f32[64,48,128]{2,1,0:T(8,128)S(1)}, f32[64,32,128]{2,1,0:T(8,128)S(1)}, f32[64,8,128]{2,1,0:T(8,128)S(1)}, ...) custom-call(s32[1]{0:T(128)} %bitcast.refs_0_, f32[6,32,128]{2,1,0:T(8,128)S(1)} %get-tuple-element.17.refs_1_, ...), custom_call_target="tpu_custom_call" | custom-call | tf_op jit(solution)/shard_map/pallas_call | solution.py:815
  51.3 6.7 %collective-permute-start.2 = (f32[64,8,128]{2,1,0:T(8,128)S(1)}, f32[64,8,128]{2,1,0:T(8,128)S(1)}, u32[]{:S(2)}, u32[]{:S(2)}) collective-permute-start(f32[64,8,128]{2,1,0:T(8,128)S(1)} %get-tuple-element.24), channel_id=1, source_target_pairs={{0,1},{1,0},{2,3},{3,2},{6,7},{7,6},{4,5},{5,4},{12,13},{13,12},{1... | collective-permute-start | bytes 786440 | tf_op jit(solution)/shard_map/ppermute | solution.py:873
  58.0 0.7 collective-permute-start.3
  58.7 12.1 %all_to_all.20 = f32[32,1,1,128]{3,2,1,0:T(1,128)S(1)} all-to-all(f32[32,1,1,128]{3,2,1,0:T(1,128)S(1)} %bitcast.20), channel_id=1, replica_groups=mesh['tm'=8,'space'=4] {'tm','space'}, dimensions={0} | all-to-all | bytes 32768 | tf_op jit(solution)/shard_map/all_to_all | solution.py:828
  70.8 0.0 collective-permute-done.2.refs_3_
  70.8 0.0 collective-permute-done.3.refs_4_
  70.8 5.2 %shard_map.53 = (f32[64,48,128]{2,1,0:T(8,128)S(1)}, f32[32,128]{1,0:T(8,128)S(1)}) custom-call(s32[1]{0:T(128)} %bitcast.refs_0_, f32[6,32,128]{2,1,0:T(8,128)S(1)} %get-tuple-element.17.refs_1_, f32[64,32,128]{2,1,0:T(8,128)S(1)} %get-tuple-element.23.refs_2_, f32[64,8,128]{2,1,0:T(8,128)S(1)} %collective-permute-done.2.refs_3_, ...), custom_call_target="tpu_custom_call" | custom-call | tf_op jit(solution)/shard_map/pallas_call | solution.py:815
  76.0 8.9 %all_to_all.21 = f32[32,1,1,128]{3,2,1,0:T(1,128)S(1)} all-to-all(f32[32,1,1,128]{3,2,1,0:T(1,128)S(1)} %bitcast.21), channel_id=1, replica_groups=mesh['tm'=8,'space'=4] {'tm','space'}, dimensions={0} | all-to-all | bytes 32768 | tf_op jit(solution)/shard_map/all_to_all | solution.py:828
  84.9 0.0 copy-start.3
  84.9 0.0 copy-start.5
  84.9 2.9 %shard_map.54 = f32[1312,128]{1,0:T(8,128)S(1)} custom-call(f32[64,48,128]{2,1,0:T(8,128)S(1)} %get-tuple-element.16.refs_0_, f32[64,48,128]{2,1,0:T(8,128)S(1)} %get-tuple-element.22.refs_1_, f32[64,48,128]{2,1,0:T(8,128)S(1)} %get-tuple-element.28.refs_2_, f32[32,128]{1,0:T(8,128)S(1)} %bitcast.18, f32[32,128]{1,0:T(8,128)S(1)} %bitcast.19), custom_call_target="tpu_custom_call" | custom-call | tf_op jit(solution)/shard_map/pallas_call | solution.py:815
  87.8 0.0 copy-start.1
  87.8 20.1 %all_to_all.22 = f32[32,41,1,128]{3,2,1,0:T(1,128)S(1)} all-to-all(f32[32,41,1,128]{3,2,1,0:T(1,128)S(1)} %bitcast.16), channel_id=1, replica_groups=mesh['tm'=8,'space'=4] {'tm','space'}, dimensions={0} | all-to-all | bytes 1343488 | tf_op jit(solution)/shard_map/all_to_all | solution.py:828
  108.0 0.0 copy-done.3
  108.0 0.0 copy-done.5
  108.0 0.0 copy-done.1
  108.0 3.2 %shard_map.55 = (f32[64,8,256]{2,1,0:T(8,128)}, f32[64,8,256]{2,1,0:T(8,128)}) custom-call(f32[1312,128]{1,0:T(8,128)S(1)} %bitcast.15, f32[64,8,256]{2,1,0:T(8,128)S(1)} %copy-done.1, f32[8,256]{1,0:T(8,128)S(1)} %copy-done.5, f32[2,8,256]{2,1,0:T(8,128)S(1)} %copy-done.3), custom_call_target="tpu_custom_call" | custom-call | tf_op jit(solution)/shard_map/pallas_call | solution.py:815
Async XLA Ops:
  0.6 1.0 copy-start
  1.7 0.7 copy-start.2
  2.4 0.7 copy-start.4
  7.6 31.1 %all-to-all-start = ((f32[32,57,1,128]{3,2,1,0:T(1,128)}), f32[32,57,1,128]{3,2,1,0:T(1,128)S(1)}, u32[]{:S(2)}, u32[]{:S(2)}) async-start(f32[32,57,1,128]{3,2,1,0:T(1,128)} %bitcast.2), calls=%async_computation | async-start | bytes 1867776 | tf_op jit(solution)/shard_map/all_to_all | solution.py:828
  44.7 1.6 %collective-permute-start = (f32[64,8,128]{2,1,0:T(8,128)S(1)}, f32[64,8,128]{2,1,0:T(8,128)S(1)}, u32[]{:S(2)}, u32[]{:S(2)}) collective-permute-start(f32[64,8,128]{2,1,0:T(8,128)S(1)} %get-tuple-element.19), channel_id=1, source_target_pairs={{0,1},{1,0},{2,3},{3,2},{6,7},{7,6},{4,5},{5,4},{12,13},{13,12},{1... | collective-permute-start | bytes 786440 | tf_op jit(solution)/shard_map/ppermute | solution.py:864
  44.8 1.5 %collective-permute-start.1 = (f32[64,8,128]{2,1,0:T(8,128)S(1)}, f32[64,8,128]{2,1,0:T(8,128)S(1)}, u32[]{:S(2)}, u32[]{:S(2)}) collective-permute-start(f32[64,8,128]{2,1,0:T(8,128)S(1)} %get-tuple-element.20), channel_id=1, source_target_pairs={{1,2},{2,1},{3,6},{6,3},{7,4},{4,7},{5,12},{12,5},{13,14},{14,13},... | collective-permute-start | bytes 786440 | tf_op jit(solution)/shard_map/ppermute | solution.py:865
  51.3 19.5 %collective-permute-start.2 = (f32[64,8,128]{2,1,0:T(8,128)S(1)}, f32[64,8,128]{2,1,0:T(8,128)S(1)}, u32[]{:S(2)}, u32[]{:S(2)}) collective-permute-start(f32[64,8,128]{2,1,0:T(8,128)S(1)} %get-tuple-element.24), channel_id=1, source_target_pairs={{0,1},{1,0},{2,3},{3,2},{6,7},{7,6},{4,5},{5,4},{12,13},{13,12},{1... | collective-permute-start | bytes 786440 | tf_op jit(solution)/shard_map/ppermute | solution.py:873
  58.0 12.8 %collective-permute-start.3 = (f32[64,8,128]{2,1,0:T(8,128)S(1)}, f32[64,8,128]{2,1,0:T(8,128)S(1)}, u32[]{:S(2)}, u32[]{:S(2)}) collective-permute-start(f32[64,8,128]{2,1,0:T(8,128)S(1)} %get-tuple-element.25), channel_id=1, source_target_pairs={{1,2},{2,1},{3,6},{6,3},{7,4},{4,7},{5,12},{12,5},{13,14},{14,13},... | collective-permute-start | bytes 786440 | tf_op jit(solution)/shard_map/ppermute | solution.py:874
  84.9 23.1 %copy-start.3 = (f32[2,8,256]{2,1,0:T(8,128)S(1)}, f32[2,8,256]{2,1,0:T(8,128)}, u32[]{:S(2)}) copy-start(f32[2,8,256]{2,1,0:T(8,128)} %refs_3_.3) | copy-start | bytes 49156
  84.9 23.1 %copy-start.5 = (f32[8,256]{1,0:T(8,128)S(1)}, f32[8,256]{1,0:T(8,128)}, u32[]{:S(2)}) copy-start(f32[8,256]{1,0:T(8,128)} %refs_2_.3) | copy-start | bytes 24580
  87.8 20.2 %copy-start.1 = (f32[64,8,256]{2,1,0:T(8,128)S(1)}, f32[64,8,256]{2,1,0:T(8,128)}, u32[]{:S(2)}) copy-start(f32[64,8,256]{2,1,0:T(8,128)} %refs_1_.3) | copy-start | bytes 1572868

commit v4 on v3

--- a/solution.py
+++ b/solution.py
@@ -195,7 +195,8 @@
 SUB = 8
 LANE = 128
 AXES = ("tm", "space")
-UNROLL = 16
+UNROLL = 32
+PAIR = 2
 
 
 def spin(block, amount, axis=1):
@@ -264,7 +265,9 @@
             and self.slot >= self.halo
             and self.space % 2 == 0
             and KRYLOV == 3
-            and self.tiles % (UNROLL // SUB) == 0
+            and self.tiles % PAIR == 0
+            and self.groups % PAIR == 0
+            and self.tm % 4 == 0
         )
 
     def strip_of(self, t, s):
@@ -275,7 +278,18 @@
         return (turn * half + x + odd * (half - 1 - 2 * x)) * 2 + core
 
 
-def pack_kernel(plan, place_ref, right_ref, diff_ref, vel_ref, out_ref, tail_ref):
+def pack_kernel(plan, place_ref, right_in, diff_in, vel_in, out_ref, *scratch):
+    tail_ref, right_ref, diff_ref, vel_ref, sems = scratch
+    split = plan.here - SUB
+    copies = [
+        pltpu.make_async_copy(right_in.at[split:], right_ref.at[split:], sems.at[0]),
+        pltpu.make_async_copy(right_in.at[:split], right_ref.at[:split], sems.at[1]),
+        pltpu.make_async_copy(diff_in, diff_ref, sems.at[2]),
+        pltpu.make_async_copy(vel_in, vel_ref, sems.at[3]),
+    ]
+    for copy in copies:
+        copy.start()
+    copies[0].wait()
     window, own, halo = plan.window, plan.own, plan.halo
     parts = plan.cols // LANE
     lane = lane_of((SUB, LANE))
@@ -318,6 +332,7 @@
         def _():
             for index, piece in enumerate(pieces):
                 tail_ref[index] = piece
+            copies[1].wait()
 
         @pl.when(k > 0)
         def _():
@@ -330,6 +345,8 @@
         return carry
 
     lax.fori_loop(0, plan.tiles, body, 0)
+    copies[2].wait()
+    copies[3].wait()
     row = pl.ds(place_ref[0], 1)
     lines = [diff_ref[row, :], vel_ref[0, row, :], vel_ref[1, row, :]]
     sub = lax.broadcasted_iota(jnp.int32, (SUB, LANE), 0)
@@ -526,7 +543,7 @@
         last_tile = plan.tiles - 1
 
         def tails(k, carry):
-            for p in (2 * k, 2 * k + 1):
+            for p in (4 * k, 4 * k + 1, 4 * k + 2, 4 * k + 3):
                 for s in range(plan.space):
                     source = p * plan.space + s
                     total = low_zero
@@ -537,14 +554,12 @@
                     tail_ref[source] = total
             return carry
 
-        lax.fori_loop(0, plan.tm // 2, tails, 0)
-
-        pair = UNROLL // SUB
+        lax.fori_loop(0, plan.tm // 4, tails, 0)
 
         def first(k, y):
-            parts = [[] for _ in range(pair)]
-            for t in range(pair):
-                a = k * pair + t
+            parts = [[] for _ in range(PAIR)]
+            for t in range(PAIR):
+                a = k * PAIR + t
                 whole = a < last_tile
                 at = jnp.minimum(a, last_tile - 1) * SUB
                 for s in range(plan.space):
@@ -554,9 +569,9 @@
                         tile = recv_ref[pl.ds(source * plan.inward + at, SUB), :]
                         cut.append(damping * jnp.where(whole, tile, tail_ref[source]))
                     parts[t].append(exchange_blocks(cut, window, 2))
-            for t in range(pair):
+            for t in range(PAIR):
                 for i in range(SUB):
-                    n = k * UNROLL + t * SUB + i
+                    n = (k * PAIR + t) * SUB + i
                     q = jnp.concatenate([part[i] for part in parts[t]], axis=0)
                     q_ref[n] = q
                     y = (q + y) * inverse
@@ -564,7 +579,7 @@
                     blank(n)
             return y
 
-        y = lax.fori_loop(0, plan.tiles // pair, first, zero)
+        y = lax.fori_loop(0, plan.tiles // PAIR, first, zero)
     else:
         near_side = jnp.where(even, halo + own, 0)
         far_side = jnp.where(even, 0, halo + own)
@@ -700,25 +715,26 @@
         here = slice((s + 1) * SUB, (s + 2) * SUB)
         return sum(c * ref[n, here, :] for c, ref in zip(along, z_refs))
 
-    def body(aa, carry):
-        for s in range(plan.space):
-            pieces = []
-            for i in range(SUB):
-                n = aa * 2 * SUB + 2 * i
-                pieces.append(
-                    jnp.where(front, spin(value(n, s), -halo), spin(value(n + 1, s), own - halo))
-                )
-            for p, piece in enumerate(exchange_blocks(pieces, window, SUB)):
-                out_ref[pl.ds(start_of(p, s) + aa * SUB, SUB), :] = piece
-                if s + 1 < plan.space:
-                    at = start_of(p, s + 1) + groups * SUB + aa
-                    out_ref[pl.ds(at, 1), :] = piece[SUB - 1 :]
-                if s > 0:
-                    at = start_of(p, s - 1) + groups * SUB + groups + aa
-                    out_ref[pl.ds(at, 1), :] = piece[:1]
+    def body(k, carry):
+        for t in range(PAIR):
+            aa = k * PAIR + t
+            for s in range(plan.space):
+                pieces = []
+                for i in range(SUB):
+                    n = aa * 2 * SUB + 2 * i
+                    left, right = spin(value(n, s), -halo), spin(value(n + 1, s), own - halo)
+                    pieces.append(jnp.where(front, left, right))
+                for p, piece in enumerate(exchange_blocks(pieces, window, 2)):
+                    out_ref[pl.ds(start_of(p, s) + aa * SUB, SUB), :] = piece
+                    if s + 1 < plan.space:
+                        at = start_of(p, s + 1) + groups * SUB + aa
+                        out_ref[pl.ds(at, 1), :] = piece[SUB - 1 :]
+                    if s > 0:
+                        at = start_of(p, s - 1) + groups * SUB + groups + aa
+                        out_ref[pl.ds(at, 1), :] = piece[:1]
         return carry
 
-    lax.fori_loop(0, groups, body, 0)
+    lax.fori_loop(0, groups // PAIR, body, 0)
     nothing = jnp.zeros((groups, LANE), jnp.float32)
     sub = lax.broadcasted_iota(jnp.int32, (SUB, LANE), 0)
     for p in range(plan.tm):
@@ -738,7 +754,8 @@
             out_ref[at : at + 1, :] = line
 
 
-def finish_kernel(plan, recv_ref, right_ref, diff_ref, vel_ref, out_ref, rest_ref, rim_ref):
+def finish_kernel(plan, recv_ref, right_ref, diff_ref, vel_ref, *refs):
+    results, (rim_ref, out_ref, rest_ref, sems) = refs[:2], refs[2:]
     groups, own, size = plan.groups, plan.own, plan.outward
     count = LANE // own
     parts = plan.cols // LANE
@@ -762,7 +779,7 @@
             pieces = [
                 recv_ref[pl.ds(start_of(part, m) + offset, SUB), :] for m in range(count)
             ]
-            wide.append(exchange_blocks(pieces, own, 4))
+            wide.append(exchange_blocks(pieces, own, 2))
         return [jnp.concatenate(pair, axis=1) for pair in zip(*wide)]
 
     for i, field in enumerate(spread(groups * SUB)):
@@ -790,35 +807,55 @@
         halves.append(total)
     before = jnp.concatenate(halves, axis=1)
 
-    def body(aa, before):
-        for i, field in enumerate(spread(aa * SUB)):
-            n = aa * count + i
-            above = rim_ref[i, pl.ds(aa, 1), :]
-            below = rim_ref[i, pl.ds(groups + aa, 1), :]
-            out_ref[n] = field
-            around = (
-                north * jnp.where(sub == 0, above, spin(field, 1, 0))
-                + south * jnp.where(sub == SUB - 1, below, spin(field, -1, 0))
-                + west * spin(field, 1)
-                + east * spin(field, -1)
-            )
-            rest_ref[n] = right_ref[n] - (center * field - around - before)
-            before = field
+    size_of = PAIR * count
+
+    def copies(k):
+        at = pl.ds(k * size_of, size_of)
+        return [
+            pltpu.make_async_copy(ref.at[at], result.at[at], sems.at[k, f])
+            for f, (ref, result) in enumerate(zip((out_ref, rest_ref), results))
+        ]
+
+    def body(k, before):
+        for t in range(PAIR):
+            aa = k * PAIR + t
+            for i, field in enumerate(spread(aa * SUB)):
+                n = aa * count + i
+                above = rim_ref[i, pl.ds(aa, 1), :]
+                below = rim_ref[i, pl.ds(groups + aa, 1), :]
+                out_ref[n] = field
+                around = (
+                    north * jnp.where(sub == 0, above, spin(field, 1, 0))
+                    + south * jnp.where(sub == SUB - 1, below, spin(field, -1, 0))
+                    + west * spin(field, 1)
+                    + east * spin(field, -1)
+                )
+                rest_ref[n] = right_ref[n] - (center * field - around - before)
+                before = field
+        for copy in copies(k):
+            copy.start()
         return before
 
-    lax.fori_loop(0, groups, body, before)
-
-
-def call(kernel, shapes, operands, scalars=0, scratch=()):
+    lax.fori_loop(0, groups // PAIR, body, before)
+    for k in range(groups // PAIR):
+        for copy in copies(k):
+            copy.wait()
+
+
+def call(kernel, shapes, operands, scalars=0, scratch=(), sems=None, far_in=False, far_out=False, room=16):
     vmem = pl.BlockSpec(memory_space=pltpu.VMEM)
     smem = pl.BlockSpec(memory_space=pltpu.SMEM)
+    hbm = pl.BlockSpec(memory_space=pltpu.HBM)
+    held = [pltpu.VMEM(shape, jnp.float32) for shape in scratch]
+    if sems:
+        held.append(pltpu.SemaphoreType.DMA(sems))
     return pl.pallas_call(
         kernel,
         out_shape=[jax.ShapeDtypeStruct(shape, jnp.float32) for shape in shapes],
-        in_specs=[smem] * scalars + [vmem] * (len(operands) - scalars),
-        out_specs=[vmem] * len(shapes),
-        scratch_shapes=[pltpu.VMEM(shape, jnp.float32) for shape in scratch],
-        compiler_params=pltpu.CompilerParams(vmem_limit_bytes=16 * 1024 * 1024),
+        in_specs=[smem] * scalars + [hbm if far_in else vmem] * (len(operands) - scalars),
+        out_specs=[hbm if far_out else vmem] * len(shapes),
+        scratch_shapes=held,
+        compiler_params=pltpu.CompilerParams(vmem_limit_bytes=room * 1024 * 1024),
     )(*operands)
 
 
@@ -852,7 +889,10 @@
         [(count * plan.inward, LANE)],
         [t.astype(jnp.int32).reshape(1), *given],
         scalars=1,
-        scratch=[(count, SUB, LANE)],
+        scratch=[(count, SUB, LANE), *(block.shape for block in given)],
+        sems=(4,),
+        far_in=True,
+        room=63,
     )[0]
     table, q0, z0, image, near, far = call(
         bind(krylov_kernel, 0),
@@ -888,7 +928,9 @@
             bind(finish_kernel),
             [shape, shape],
             [everyone(packed, count), *given],
-            scratch=[(2 * SUB, SUB, plan.cols)],
+            scratch=[(2 * SUB, SUB, plan.cols), shape, shape],
+            sems=(plan.groups // PAIR, 2),
+            far_out=True,
         )
     )
 

time: 112 us -> 107 us (0.955)
  Pallas kernels: 26.9 us -> 24.4 us
  local copies, waits for them, and re-layouts: 2.46 us -> 0.01 us
    unnamed x12 -> x6, local copies, waits for them, and re-layouts: 2.46 us -> 0.01 us
    pallas_call x6, Pallas kernels: 26.9 us -> 24.4 us  [call(): pl.pallas_call(kernel, out_shape=[jax.ShapeDtypeStruct(shape, jnp.float32...]
where the time goes in v4:
time: 107 us; the launch traced here: 106 us
  blocking collectives  41.1 us (38%)
  waiting for transfers between devices  24.5 us (23%)
  Pallas kernels  24.4 us (23%)
  starting transfers between devices  15.5 us (14%)
    all_to_all x3, blocking collectives, everyone(): lax.all_to_all(parts, AXES, split_axis=0, concat_axis=0, tiled=True)  41.1 us
    pallas_call x6, Pallas kernels, call(): pl.pallas_call(kernel, out_shape=[jax.ShapeDtypeStruct(shape, jnp.float32...  24.4 us
    all_to_all x1, waiting for transfers between devices, everyone(): lax.all_to_all(parts, AXES, split_axis=0, concat_axis=0, tiled=True)  23.7 us
    all_to_all x1, starting transfers between devices, everyone(): lax.all_to_all(parts, AXES, split_axis=0, concat_axis=0, tiled=True)  7.33 us
    ppermute x2, starting transfers between devices, strip_device(): near = lax.ppermute(near, AXES, near_route)  6.79 us
  transfers between devices with their start and end apart: 5, of which 2 were waited for; matrix products, arithmetic and copies ran while one was open for 0% of the time, Pallas kernels for 0%

profile of v4, /device:TPU:0, one launch (start us, length us, event | category | flops | bytes accessed | tf_op | source)
XLA Modules:
  0.0 106.3 jit_solution(8269607008388991567)
XLA Ops:
  0.6 5.4 %shard_map.50 = f32[1824,128]{1,0:T(8,128)} custom-call(s32[1]{0:T(128)} %bitcast.1.refs_0_, f32[64,8,256]{2,1,0:T(8,128)} %refs_1_.3, f32[8,256]{1,0:T(8,128)} %refs_2_.3, f32[2,8,256]{2,1,0:T(8,128)} %refs_3_.3), custom_call_target="tpu_custom_call" | custom-call | tf_op jit(solution)/shard_map/pallas_call | solution.py:852
  6.0 7.3 %all-to-all-start = ((f32[32,57,1,128]{3,2,1,0:T(1,128)}), f32[32,57,1,128]{3,2,1,0:T(1,128)S(1)}, u32[]{:S(2)}, u32[]{:S(2)}) async-start(f32[32,57,1,128]{3,2,1,0:T(1,128)} %bitcast.22), calls=%async_computation | async-start | bytes 1867776 | tf_op jit(solution)/shard_map/all_to_all | solution.py:865
  13.4 23.7 %all-to-all-done = f32[32,57,1,128]{3,2,1,0:T(1,128)S(1)} async-done(((f32[32,57,1,128]{3,2,1,0:T(1,128)}), f32[32,57,1,128]{3,2,1,0:T(1,128)S(1)}, u32[]{:S(2)}, u32[]{:S(2)}) %all-to-all-start) | async-done | bytes 933920 | tf_op jit(solution)/shard_map/all_to_all | solution.py:865
  37.1 5.5 %shard_map.51 = (f32[6,32,128]{2,1,0:T(8,128)S(1)}, f32[64,32,128]{2,1,0:T(8,128)S(1)}, f32[64,48,128]{2,1,0:T(8,128)S(1)}, f32[64,32,128]{2,1,0:T(8,128)S(1)}, ...) custom-call(s32[1]{0:T(128)} %bitcast.refs_0_, f32[1824,128]{1,0:T(8,128)S(1)} %bitcast.14), custom_call_target="tpu_custom_call" | custom-call | tf_op jit(solution)/shard_map/pallas_call | solution.py:852
  42.6 0.1 collective-permute-start
  42.7 0.7 collective-permute-start.1
  43.3 0.8 collective-permute-done.refs_3_
  44.2 0.0 collective-permute-done.1.refs_4_
  44.2 4.4 %shard_map.52 = (f32[64,32,128]{2,1,0:T(8,128)S(1)}, f32[64,48,128]{2,1,0:T(8,128)S(1)}, f32[64,32,128]{2,1,0:T(8,128)S(1)}, f32[64,8,128]{2,1,0:T(8,128)S(1)}, ...) custom-call(s32[1]{0:T(128)} %bitcast.refs_0_, f32[6,32,128]{2,1,0:T(8,128)S(1)} %get-tuple-element.17.refs_1_, ...), custom_call_target="tpu_custom_call" | custom-call | tf_op jit(solution)/shard_map/pallas_call | solution.py:852
  48.6 6.7 %collective-permute-start.2 = (f32[64,8,128]{2,1,0:T(8,128)S(1)}, f32[64,8,128]{2,1,0:T(8,128)S(1)}, u32[]{:S(2)}, u32[]{:S(2)}) collective-permute-start(f32[64,8,128]{2,1,0:T(8,128)S(1)} %get-tuple-element.24), channel_id=1, source_target_pairs={{0,1},{1,0},{2,3},{3,2},{6,7},{7,6},{4,5},{5,4},{12,13},{13,12},{1... | collective-permute-start | bytes 786440 | tf_op jit(solution)/shard_map/ppermute | solution.py:913
  55.3 0.7 collective-permute-start.3
  56.0 12.1 %all_to_all.20 = f32[32,1,1,128]{3,2,1,0:T(1,128)S(1)} all-to-all(f32[32,1,1,128]{3,2,1,0:T(1,128)S(1)} %bitcast.20), channel_id=1, replica_groups=mesh['tm'=8,'space'=4] {'tm','space'}, dimensions={0} | all-to-all | bytes 32768 | tf_op jit(solution)/shard_map/all_to_all | solution.py:865
  68.1 0.0 collective-permute-done.2.refs_3_
  68.1 0.0 collective-permute-done.3.refs_4_
  68.1 4.6 %shard_map.53 = (f32[64,48,128]{2,1,0:T(8,128)S(1)}, f32[32,128]{1,0:T(8,128)S(1)}) custom-call(s32[1]{0:T(128)} %bitcast.refs_0_, f32[6,32,128]{2,1,0:T(8,128)S(1)} %get-tuple-element.17.refs_1_, f32[64,32,128]{2,1,0:T(8,128)S(1)} %get-tuple-element.23.refs_2_, f32[64,8,128]{2,1,0:T(8,128)S(1)} %collective-permute-done.2.refs_3_, ...), custom_call_target="tpu_custom_call" | custom-call | tf_op jit(solution)/shard_map/pallas_call | solution.py:852
  72.7 8.9 %all_to_all.21 = f32[32,1,1,128]{3,2,1,0:T(1,128)S(1)} all-to-all(f32[32,1,1,128]{3,2,1,0:T(1,128)S(1)} %bitcast.21), channel_id=1, replica_groups=mesh['tm'=8,'space'=4] {'tm','space'}, dimensions={0} | all-to-all | bytes 32768 | tf_op jit(solution)/shard_map/all_to_all | solution.py:865
  81.6 0.0 copy-start.1
  81.6 0.0 copy-start.2
  81.6 1.8 %shard_map.54 = f32[1312,128]{1,0:T(8,128)S(1)} custom-call(f32[64,48,128]{2,1,0:T(8,128)S(1)} %get-tuple-element.16.refs_0_, f32[64,48,128]{2,1,0:T(8,128)S(1)} %get-tuple-element.22.refs_1_, f32[64,48,128]{2,1,0:T(8,128)S(1)} %get-tuple-element.28.refs_2_, f32[32,128]{1,0:T(8,128)S(1)} %bitcast.18, f32[32,128]{1,0:T(8,128)S(1)} %bitcast.19), custom_call_target="tpu_custom_call" | custom-call | tf_op jit(solution)/shard_map/pallas_call | solution.py:852
  83.4 0.0 copy-start
  83.4 20.1 %all_to_all.22 = f32[32,41,1,128]{3,2,1,0:T(1,128)S(1)} all-to-all(f32[32,41,1,128]{3,2,1,0:T(1,128)S(1)} %bitcast.16), channel_id=1, replica_groups=mesh['tm'=8,'space'=4] {'tm','space'}, dimensions={0} | all-to-all | bytes 1343488 | tf_op jit(solution)/shard_map/all_to_all | solution.py:865
  103.6 0.0 copy-done.1
  103.6 0.0 copy-done.2
  103.6 0.0 copy-done
  103.6 2.8 %shard_map.55 = (f32[64,8,256]{2,1,0:T(8,128)}, f32[64,8,256]{2,1,0:T(8,128)}) custom-call(f32[1312,128]{1,0:T(8,128)S(1)} %bitcast.15, f32[64,8,256]{2,1,0:T(8,128)S(1)} %copy-done, f32[8,256]{1,0:T(8,128)S(1)} %copy-done.2, f32[2,8,256]{2,1,0:T(8,128)S(1)} %copy-done.1), custom_call_target="tpu_custom_call" | custom-call | tf_op jit(solution)/shard_map/pallas_call | solution.py:852
Async XLA Ops:
  6.0 31.1 %all-to-all-start = ((f32[32,57,1,128]{3,2,1,0:T(1,128)}), f32[32,57,1,128]{3,2,1,0:T(1,128)S(1)}, u32[]{:S(2)}, u32[]{:S(2)}) async-start(f32[32,57,1,128]{3,2,1,0:T(1,128)} %bitcast.22), calls=%async_computation | async-start | bytes 1867776 | tf_op jit(solution)/shard_map/all_to_all | solution.py:865
  42.6 1.6 %collective-permute-start = (f32[64,8,128]{2,1,0:T(8,128)S(1)}, f32[64,8,128]{2,1,0:T(8,128)S(1)}, u32[]{:S(2)}, u32[]{:S(2)}) collective-permute-start(f32[64,8,128]{2,1,0:T(8,128)S(1)} %get-tuple-element.19), channel_id=1, source_target_pairs={{0,1},{1,0},{2,3},{3,2},{6,7},{7,6},{4,5},{5,4},{12,13},{13,12},{1... | collective-permute-start | bytes 786440 | tf_op jit(solution)/shard_map/ppermute | solution.py:904
  42.7 1.5 %collective-permute-start.1 = (f32[64,8,128]{2,1,0:T(8,128)S(1)}, f32[64,8,128]{2,1,0:T(8,128)S(1)}, u32[]{:S(2)}, u32[]{:S(2)}) collective-permute-start(f32[64,8,128]{2,1,0:T(8,128)S(1)} %get-tuple-element.20), channel_id=1, source_target_pairs={{1,2},{2,1},{3,6},{6,3},{7,4},{4,7},{5,12},{12,5},{13,14},{14,13},... | collective-permute-start | bytes 786440 | tf_op jit(solution)/shard_map/ppermute | solution.py:905
  48.6 19.5 %collective-permute-start.2 = (f32[64,8,128]{2,1,0:T(8,128)S(1)}, f32[64,8,128]{2,1,0:T(8,128)S(1)}, u32[]{:S(2)}, u32[]{:S(2)}) collective-permute-start(f32[64,8,128]{2,1,0:T(8,128)S(1)} %get-tuple-element.24), channel_id=1, source_target_pairs={{0,1},{1,0},{2,3},{3,2},{6,7},{7,6},{4,5},{5,4},{12,13},{13,12},{1... | collective-permute-start | bytes 786440 | tf_op jit(solution)/shard_map/ppermute | solution.py:913
  55.3 12.8 %collective-permute-start.3 = (f32[64,8,128]{2,1,0:T(8,128)S(1)}, f32[64,8,128]{2,1,0:T(8,128)S(1)}, u32[]{:S(2)}, u32[]{:S(2)}) collective-permute-start(f32[64,8,128]{2,1,0:T(8,128)S(1)} %get-tuple-element.25), channel_id=1, source_target_pairs={{1,2},{2,1},{3,6},{6,3},{7,4},{4,7},{5,12},{12,5},{13,14},{14,13},... | collective-permute-start | bytes 786440 | tf_op jit(solution)/shard_map/ppermute | solution.py:914
  81.6 22.0 %copy-start.1 = (f32[2,8,256]{2,1,0:T(8,128)S(1)}, f32[2,8,256]{2,1,0:T(8,128)}, u32[]{:S(2)}) copy-start(f32[2,8,256]{2,1,0:T(8,128)} %refs_3_.3) | copy-start | bytes 49156
  81.6 22.0 %copy-start.2 = (f32[8,256]{1,0:T(8,128)S(1)}, f32[8,256]{1,0:T(8,128)}, u32[]{:S(2)}) copy-start(f32[8,256]{1,0:T(8,128)} %refs_2_.3) | copy-start | bytes 24580
  83.4 20.2 %copy-start = (f32[64,8,256]{2,1,0:T(8,128)S(1)}, f32[64,8,256]{2,1,0:T(8,128)}, u32[]{:S(2)}) copy-start(f32[64,8,256]{2,1,0:T(8,128)} %refs_1_.3) | copy-start | bytes 1572868

commit v5 on v4

--- a/solution.py
+++ b/solution.py
@@ -278,7 +278,7 @@
         return (turn * half + x + odd * (half - 1 - 2 * x)) * 2 + core
 
 
-def pack_kernel(plan, place_ref, right_in, diff_in, vel_in, out_ref, *scratch):
+def pack_kernel(plan, right_in, diff_in, vel_in, out_ref, *scratch):
     tail_ref, right_ref, diff_ref, vel_ref, sems = scratch
     split = plan.here - SUB
     copies = [
@@ -347,7 +347,7 @@
     lax.fori_loop(0, plan.tiles, body, 0)
     copies[2].wait()
     copies[3].wait()
-    row = pl.ds(place_ref[0], 1)
+    row = pl.ds(lax.axis_index("tm"), 1)
     lines = [diff_ref[row, :], vel_ref[0, row, :], vel_ref[1, row, :]]
     sub = lax.broadcasted_iota(jnp.int32, (SUB, LANE), 0)
     blocks = [
@@ -478,14 +478,14 @@
 
 def krylov_kernel(plan, j, *refs):
     refs = list(refs)
-    strip = refs.pop(0)[0]
+    strip = plan.strip_of(lax.axis_index("tm"), lax.axis_index("space"))
     here, window, rows, halo, own = plan.here, plan.window, plan.rows, plan.halo, plan.own
     slot = plan.slot
     final = j == KRYLOV - 1
     shape = (rows, LANE)
     lane = lane_of(shape)
     low_lane = lane_of((SUB, LANE))
-    low_spot = low_lane % window
+    low_spot = low_lane & (window - 1)
     even = strip % 2 == 0
     if j == 0:
         recv_ref, table_ref, q_ref, g_ref, w_ref, near_ref, far_ref, y_ref, tail_ref = refs
@@ -581,10 +581,8 @@
 
         y = lax.fori_loop(0, plan.tiles // PAIR, first, zero)
     else:
-        near_side = jnp.where(even, halo + own, 0)
-        far_side = jnp.where(even, 0, halo + own)
-        near_mask = (low_spot >= near_side) & (low_spot < near_side + halo)
-        far_mask = (low_spot >= far_side) & (low_spot < far_side + halo)
+        right_mask = (low_spot >= halo + own) & (low_spot < halo + own + halo)
+        left_mask = low_spot < halo
 
         def first(i, y):
             base = i * UNROLL
@@ -592,13 +590,14 @@
             for k in range(UNROLL):
                 n = base + k
                 near, far = near_in[n], far_in[n]
+                right = jnp.where(even, near, far)
+                left = jnp.where(even, far, near)
                 image = image_ref[n]
                 parts = []
                 for s in range(plan.space):
                     part = image[s * SUB : (s + 1) * SUB]
-                    shift = LANE - slot * s
-                    part = jnp.where(near_mask, pltpu.roll(near, (near_side + shift) % LANE, 1), part)
-                    part = jnp.where(far_mask, pltpu.roll(far, (far_side + shift) % LANE, 1), part)
+                    part = jnp.where(right_mask, spin(right, halo + own - slot * s), part)
+                    part = jnp.where(left_mask, spin(left, halo - own - slot * s), part)
                     parts.append(part)
                 q = jnp.concatenate(parts, axis=0)
                 if final:
@@ -635,8 +634,9 @@
     ending = (1.0 - damping) * g_ref[here - 1, inner, :] + (y + start * power)
     before = jnp.where(lane < window, 0.0, damping * spin(ending, window))
 
-    near_from = jnp.where(even, own, halo)
-    far_from = jnp.where(even, halo, own)
+    ahead = [
+        ((low_lane - slot * s - (own - halo)) & (window - 1)) < halo for s in range(plan.space)
+    ]
 
     def fold(block):
         return sum(block[s * SUB : (s + 1) * SUB] for s in range(plan.space))
@@ -648,16 +648,13 @@
             n = base + k
             image = w_ref[n]
             if not final:
-                near = far = None
+                left = right = None
                 for s in range(plan.space):
-                    part = image[s * SUB : (s + 1) * SUB]
-                    a = pltpu.roll(part, (slot * s - near_from + LANE) % LANE, 1)
-                    b = pltpu.roll(part, (slot * s - far_from + LANE) % LANE, 1)
-                    inside = low_spot // slot == s
-                    near = a if near is None else jnp.where(inside, a, near)
-                    far = b if far is None else jnp.where(inside, b, far)
-                near_ref[n] = near
-                far_ref[n] = far
+                    moved = spin(image[s * SUB : (s + 1) * SUB], slot * s - halo)
+                    left = moved if s == 0 else jnp.where(low_spot // slot == s, moved, left)
+                    right = moved if s == 0 else jnp.where(ahead[s], moved, right)
+                near_ref[n] = jnp.where(even, right, left)
+                far_ref[n] = jnp.where(even, left, right)
             if j == 0:
                 continue
             q = q_ref[n]
@@ -842,9 +839,8 @@
             copy.wait()
 
 
-def call(kernel, shapes, operands, scalars=0, scratch=(), sems=None, far_in=False, far_out=False, room=16):
+def call(kernel, shapes, operands, scratch=(), sems=None, far_in=False, far_out=False, room=16):
     vmem = pl.BlockSpec(memory_space=pltpu.VMEM)
-    smem = pl.BlockSpec(memory_space=pltpu.SMEM)
     hbm = pl.BlockSpec(memory_space=pltpu.HBM)
     held = [pltpu.VMEM(shape, jnp.float32) for shape in scratch]
     if sems:
@@ -852,7 +848,7 @@
     return pl.pallas_call(
         kernel,
         out_shape=[jax.ShapeDtypeStruct(shape, jnp.float32) for shape in shapes],
-        in_specs=[smem] * scalars + [hbm if far_in else vmem] * (len(operands) - scalars),
+        in_specs=[hbm if far_in else vmem] * len(operands),
         out_specs=[hbm if far_out else vmem] * len(shapes),
         scratch_shapes=held,
         compiler_params=pltpu.CompilerParams(vmem_limit_bytes=room * 1024 * 1024),
@@ -866,9 +862,6 @@
 
 
 def strip_device(plan, right_side, diffusion, velocity):
-    t = lax.axis_index("tm")
-    s = lax.axis_index("space")
-    strip = plan.strip_of(t, s).astype(jnp.int32).reshape(1)
     count = plan.devices
     hold = plan.holder
     near_route = []
@@ -887,8 +880,7 @@
     sent = call(
         bind(pack_kernel),
         [(count * plan.inward, LANE)],
-        [t.astype(jnp.int32).reshape(1), *given],
-        scalars=1,
+        given,
         scratch=[(count, SUB, LANE), *(block.shape for block in given)],
         sems=(4,),
         far_in=True,
@@ -897,8 +889,7 @@
     table, q0, z0, image, near, far = call(
         bind(krylov_kernel, 0),
         [(6, plan.rows, LANE), full, padded, full, side, side],
-        [strip, everyone(sent, count)],
-        scalars=1,
+        [everyone(sent, count)],
         scratch=[delayed, (count, SUB, LANE)],
     )
     near = lax.ppermute(near, AXES, near_route)
@@ -906,8 +897,7 @@
     q1, z1, image, near, far, sums = call(
         bind(krylov_kernel, 1),
         [full, padded, full, side, side, small],
-        [strip, table, image, near, far, q0],
-        scalars=1,
+        [table, image, near, far, q0],
         scratch=[delayed],
     )
     near = lax.ppermute(near, AXES, near_route)
@@ -916,8 +906,7 @@
     z2, sums = call(
         bind(krylov_kernel, 2),
         [padded, small],
-        [strip, table, image, near, far, q0, q1, mid],
-        scalars=1,
+        [table, image, near, far, q0, q1, mid],
         scratch=[delayed, full, full, full],
     )
     end = everyone(sums, count)

time: 107 us -> 106 us (level)
  blocking collectives: 41.1 us -> 72.2 us
  waiting for transfers between devices: 24.5 us -> 0.84 us
  starting transfers between devices: 15.5 us -> 8.13 us
    all_to_all x3 -> x4, blocking collectives: 41.1 us -> 72.2 us  [everyone(): lax.all_to_all(parts, AXES, split_axis=0, concat_axis=0, tiled=True)]
    all_to_all x1 -> x0, waiting for transfers between devices: 23.7 us -> none  [everyone(): lax.all_to_all(parts, AXES, split_axis=0, concat_axis=0, tiled=True)]
    all_to_all x1 -> x0, starting transfers between devices: 7.33 us -> none  [everyone(): lax.all_to_all(parts, AXES, split_axis=0, concat_axis=0, tiled=True)]
  transfers between devices with their start and end apart: 5 -> 4, of which waited for: 2 -> 1; matrix products, arithmetic and copies ran while one was open for 0% -> 0% of each run, Pallas kernels for 0% -> 0%
where the time goes in v5:
time: 106 us
  blocking collectives  72.2 us (68%)
  Pallas kernels  23.7 us (22%)
  starting transfers between devices  8.13 us (8%)
    all_to_all x4, blocking collectives, everyone(): lax.all_to_all(parts, AXES, split_axis=0, concat_axis=0, tiled=True)  72.2 us
    pallas_call x6, Pallas kernels, call(): pl.pallas_call(kernel, out_shape=[jax.ShapeDtypeStruct(shape, jnp.float32...  23.7 us
    ppermute x2, starting transfers between devices, strip_device(): near = lax.ppermute(near, AXES, near_route)  6.79 us
  transfers between devices with their start and end apart: 4, of which 1 were waited for; matrix products, arithmetic and copies ran while one was open for 0% of the time, Pallas kernels for 0%

profile of v5, /device:TPU:0, one launch (start us, length us, event | category | flops | bytes accessed | tf_op | source)
XLA Modules:
  0.0 105.6 jit_solution(5768423007072104867)
XLA Ops:
  0.6 5.4 %shard_map.50 = f32[1824,128]{1,0:T(8,128)} custom-call(f32[64,8,256]{2,1,0:T(8,128)} %refs_1_.3, f32[8,256]{1,0:T(8,128)} %refs_2_.3, f32[2,8,256]{2,1,0:T(8,128)} %refs_3_.1), custom_call_target="tpu_custom_call" | custom-call | tf_op jit(solution)/shard_map/pallas_call | solution.py:848
  6.0 31.1 %all_to_all.20 = f32[32,57,1,128]{3,2,1,0:T(1,128)S(1)} all-to-all(f32[32,57,1,128]{3,2,1,0:T(1,128)} %bitcast.20), channel_id=1, replica_groups=mesh['tm'=8,'space'=4] {'tm','space'}, dimensions={0} | all-to-all | bytes 1867776 | tf_op jit(solution)/shard_map/all_to_all | solution.py:861
  37.1 5.0 %shard_map.51 = (f32[6,32,128]{2,1,0:T(8,128)S(1)}, f32[64,32,128]{2,1,0:T(8,128)S(1)}, f32[64,48,128]{2,1,0:T(8,128)S(1)}, f32[64,32,128]{2,1,0:T(8,128)S(1)}, ...) custom-call(f32[1824,128]{1,0:T(8,128)S(1)} %bitcast.12), custom_call_target="tpu_custom_call" | custom-call | tf_op jit(solution)/shard_map/pallas_call | solution.py:848
  42.2 0.1 collective-permute-start
  42.2 0.7 collective-permute-start.1
  42.9 0.8 collective-permute-done.refs_2_
  43.8 0.0 collective-permute-done.1.refs_3_
  43.8 4.1 %shard_map.52 = (f32[64,32,128]{2,1,0:T(8,128)S(1)}, f32[64,48,128]{2,1,0:T(8,128)S(1)}, f32[64,32,128]{2,1,0:T(8,128)S(1)}, f32[64,8,128]{2,1,0:T(8,128)S(1)}, ...) custom-call(f32[6,32,128]{2,1,0:T(8,128)S(1)} %get-tuple-element.17.refs_0_, ...), custom_call_target="tpu_custom_call" | custom-call | tf_op jit(solution)/shard_map/pallas_call | solution.py:848
  47.9 6.7 %collective-permute-start.2 = (f32[64,8,128]{2,1,0:T(8,128)S(1)}, f32[64,8,128]{2,1,0:T(8,128)S(1)}, u32[]{:S(2)}, u32[]{:S(2)}) collective-permute-start(f32[64,8,128]{2,1,0:T(8,128)S(1)} %get-tuple-element.24), channel_id=1, source_target_pairs={{0,1},{1,0},{2,3},{3,2},{6,7},{7,6},{4,5},{5,4},{12,13},{13,12},{1... | collective-permute-start | bytes 786440 | tf_op jit(solution)/shard_map/ppermute | solution.py:903
  54.6 0.7 collective-permute-start.3
  55.3 12.1 %all_to_all.21 = f32[32,1,1,128]{3,2,1,0:T(1,128)S(1)} all-to-all(f32[32,1,1,128]{3,2,1,0:T(1,128)S(1)} %bitcast.18), channel_id=1, replica_groups=mesh['tm'=8,'space'=4] {'tm','space'}, dimensions={0} | all-to-all | bytes 32768 | tf_op jit(solution)/shard_map/all_to_all | solution.py:861
  67.4 0.0 collective-permute-done.2.refs_2_
  67.4 0.0 collective-permute-done.3.refs_3_
  67.4 4.6 %shard_map.53 = (f32[64,48,128]{2,1,0:T(8,128)S(1)}, f32[32,128]{1,0:T(8,128)S(1)}) custom-call(f32[6,32,128]{2,1,0:T(8,128)S(1)} %get-tuple-element.17.refs_0_, f32[64,32,128]{2,1,0:T(8,128)S(1)} %get-tuple-element.23.refs_1_, f32[64,8,128]{2,1,0:T(8,128)S(1)} %collective-permute-done.2.refs_2_, f32[64,8,128]{2,1,0:T(8,128)S(1)} %collective-permute-done.3.refs_3_, ...), custom_call_target="tpu_custom_call" | custom-call | tf_op jit(solution)/shard_map/pallas_call | solution.py:848
  72.0 8.9 %all_to_all.22 = f32[32,1,1,128]{3,2,1,0:T(1,128)S(1)} all-to-all(f32[32,1,1,128]{3,2,1,0:T(1,128)S(1)} %bitcast.19), channel_id=1, replica_groups=mesh['tm'=8,'space'=4] {'tm','space'}, dimensions={0} | all-to-all | bytes 32768 | tf_op jit(solution)/shard_map/all_to_all | solution.py:861
  80.8 0.0 copy-start.1
  80.8 0.0 copy-start.2
  80.8 1.8 %shard_map.54 = f32[1312,128]{1,0:T(8,128)S(1)} custom-call(f32[64,48,128]{2,1,0:T(8,128)S(1)} %get-tuple-element.16.refs_0_, f32[64,48,128]{2,1,0:T(8,128)S(1)} %get-tuple-element.22.refs_1_, f32[64,48,128]{2,1,0:T(8,128)S(1)} %get-tuple-element.28.refs_2_, f32[32,128]{1,0:T(8,128)S(1)} %bitcast.16, f32[32,128]{1,0:T(8,128)S(1)} %bitcast.17), custom_call_target="tpu_custom_call" | custom-call | tf_op jit(solution)/shard_map/pallas_call | solution.py:848
  82.6 0.0 copy-start
  82.6 20.1 %all_to_all.23 = f32[32,41,1,128]{3,2,1,0:T(1,128)S(1)} all-to-all(f32[32,41,1,128]{3,2,1,0:T(1,128)S(1)} %bitcast.14), channel_id=1, replica_groups=mesh['tm'=8,'space'=4] {'tm','space'}, dimensions={0} | all-to-all | bytes 1343488 | tf_op jit(solution)/shard_map/all_to_all | solution.py:861
  102.8 0.0 copy-done.1
  102.8 0.0 copy-done.2
  102.8 0.0 copy-done
  102.8 2.8 %shard_map.55 = (f32[64,8,256]{2,1,0:T(8,128)}, f32[64,8,256]{2,1,0:T(8,128)}) custom-call(f32[1312,128]{1,0:T(8,128)S(1)} %bitcast.13, f32[64,8,256]{2,1,0:T(8,128)S(1)} %copy-done, f32[8,256]{1,0:T(8,128)S(1)} %copy-done.2, f32[2,8,256]{2,1,0:T(8,128)S(1)} %copy-done.1), custom_call_target="tpu_custom_call" | custom-call | tf_op jit(solution)/shard_map/pallas_call | solution.py:848
Async XLA Ops:
  42.2 1.6 %collective-permute-start = (f32[64,8,128]{2,1,0:T(8,128)S(1)}, f32[64,8,128]{2,1,0:T(8,128)S(1)}, u32[]{:S(2)}, u32[]{:S(2)}) collective-permute-start(f32[64,8,128]{2,1,0:T(8,128)S(1)} %get-tuple-element.19), channel_id=1, source_target_pairs={{0,1},{1,0},{2,3},{3,2},{6,7},{7,6},{4,5},{5,4},{12,13},{13,12},{1... | collective-permute-start | bytes 786440 | tf_op jit(solution)/shard_map/ppermute | solution.py:895
  42.2 1.5 %collective-permute-start.1 = (f32[64,8,128]{2,1,0:T(8,128)S(1)}, f32[64,8,128]{2,1,0:T(8,128)S(1)}, u32[]{:S(2)}, u32[]{:S(2)}) collective-permute-start(f32[64,8,128]{2,1,0:T(8,128)S(1)} %get-tuple-element.20), channel_id=1, source_target_pairs={{1,2},{2,1},{3,6},{6,3},{7,4},{4,7},{5,12},{12,5},{13,14},{14,13},... | collective-permute-start | bytes 786440 | tf_op jit(solution)/shard_map/ppermute | solution.py:896
  47.9 19.5 %collective-permute-start.2 = (f32[64,8,128]{2,1,0:T(8,128)S(1)}, f32[64,8,128]{2,1,0:T(8,128)S(1)}, u32[]{:S(2)}, u32[]{:S(2)}) collective-permute-start(f32[64,8,128]{2,1,0:T(8,128)S(1)} %get-tuple-element.24), channel_id=1, source_target_pairs={{0,1},{1,0},{2,3},{3,2},{6,7},{7,6},{4,5},{5,4},{12,13},{13,12},{1... | collective-permute-start | bytes 786440 | tf_op jit(solution)/shard_map/ppermute | solution.py:903
  54.6 12.8 %collective-permute-start.3 = (f32[64,8,128]{2,1,0:T(8,128)S(1)}, f32[64,8,128]{2,1,0:T(8,128)S(1)}, u32[]{:S(2)}, u32[]{:S(2)}) collective-permute-start(f32[64,8,128]{2,1,0:T(8,128)S(1)} %get-tuple-element.25), channel_id=1, source_target_pairs={{1,2},{2,1},{3,6},{6,3},{7,4},{4,7},{5,12},{12,5},{13,14},{14,13},... | collective-permute-start | bytes 786440 | tf_op jit(solution)/shard_map/ppermute | solution.py:904
  80.8 22.0 %copy-start.1 = (f32[2,8,256]{2,1,0:T(8,128)S(1)}, f32[2,8,256]{2,1,0:T(8,128)}, u32[]{:S(2)}) copy-start(f32[2,8,256]{2,1,0:T(8,128)} %refs_3_.1) | copy-start | bytes 49156
  80.8 22.0 %copy-start.2 = (f32[8,256]{1,0:T(8,128)S(1)}, f32[8,256]{1,0:T(8,128)}, u32[]{:S(2)}) copy-start(f32[8,256]{1,0:T(8,128)} %refs_2_.3) | copy-start | bytes 24580
  82.6 20.2 %copy-start = (f32[64,8,256]{2,1,0:T(8,128)S(1)}, f32[64,8,256]{2,1,0:T(8,128)}, u32[]{:S(2)}) copy-start(f32[64,8,256]{2,1,0:T(8,128)} %refs_1_.3) | copy-start | bytes 1572868

commit v6 on v5

--- a/solution.py
+++ b/solution.py
@@ -302,49 +302,36 @@
                 for m in range(SUB):
                     yield parity, part, m, plan.holder[2 * (part * SUB + m) + parity]
 
+    def windows(a):
+        pieces = []
+        fields = [right_ref[a * SUB + i] for i in range(SUB)]
+        for parity in range(2):
+            turned = [spin(field, halo - parity * own) for field in fields]
+            for part in range(parts):
+                cut = [field[:, part * LANE : (part + 1) * LANE] for field in turned]
+                pieces += exchange_blocks(cut, window, 2)
+        return pieces
+
+    def spread(a, pieces):
+        amount = plan.used - plan.spare * a
+        for index, (_, _, _, target) in enumerate(strips()):
+            tail = pltpu.roll(tail_ref[index], amount, 1)
+            piece = jnp.where(spot >= plan.used, tail, pieces[index])
+            out_ref[pl.ds(target * plan.inward + a * SUB, SUB), :] = piece
+
+    for index, piece in enumerate(windows(plan.tiles - 1)):
+        tail_ref[index] = piece
+    copies[1].wait()
+
     def body(k, carry):
-        a = plan.tiles - 1 - k
-        fields = [right_ref[a * SUB + i] for i in range(SUB)]
-        cache = {}
-
-        def turned(i, part, amount):
-            key = (i, part % parts, amount % LANE)
-            if key not in cache:
-                block = fields[i][:, key[1] * LANE : (key[1] + 1) * LANE]
-                cache[key] = spin(block, amount)
-            return cache[key]
-
-        pieces = []
-        for parity, part, m, _ in strips():
-            base = parity * own - halo
-            total = None
-            for i in range(SUB):
-                amount = window * (i - m) - base
-                value = turned(i, part, amount)
-                if parity == 0 and m == 0:
-                    value = jnp.where(spot < halo, turned(i, part - 1, amount), value)
-                if parity == 1 and m == SUB - 1:
-                    value = jnp.where(spot >= edge, turned(i, part + 1, amount), value)
-                total = value if total is None else jnp.where(group == i, value, total)
-            pieces.append(total)
-
-        @pl.when(k == 0)
-        def _():
-            for index, piece in enumerate(pieces):
-                tail_ref[index] = piece
-            copies[1].wait()
-
-        @pl.when(k > 0)
-        def _():
-            amount = plan.used - plan.spare * a
-            for index, (_, _, _, target) in enumerate(strips()):
-                tail = pltpu.roll(tail_ref[index], amount, 1)
-                piece = jnp.where(spot >= plan.used, tail, pieces[index])
-                out_ref[pl.ds(target * plan.inward + a * SUB, SUB), :] = piece
-
+        both = [(a, windows(a)) for a in (2 * k, 2 * k + 1)]
+        for a, pieces in both:
+            spread(a, pieces)
         return carry
 
-    lax.fori_loop(0, plan.tiles, body, 0)
+    lax.fori_loop(0, (plan.tiles - 1) // 2, body, 0)
+    for a in range((plan.tiles - 1) // 2 * 2, plan.tiles - 1):
+        spread(a, windows(a))
     copies[2].wait()
     copies[3].wait()
     row = pl.ds(lax.axis_index("tm"), 1)

time: 106 us -> 106 us (level)
  no operation moved by 1% of the time
where the time goes in v6:
time: 106 us; the launch traced here: 105 us
  blocking collectives  72.2 us (68%)
  Pallas kernels  23.4 us (22%)
  starting transfers between devices  8.13 us (8%)
    all_to_all x4, blocking collectives, everyone(): lax.all_to_all(parts, AXES, split_axis=0, concat_axis=0, tiled=True)  72.2 us
    pallas_call x6, Pallas kernels, call(): pl.pallas_call(kernel, out_shape=[jax.ShapeDtypeStruct(shape, jnp.float32...  23.4 us
    ppermute x2, starting transfers between devices, strip_device(): near = lax.ppermute(near, AXES, near_route)  6.79 us
  transfers between devices with their start and end apart: 4, of which 1 were waited for; matrix products, arithmetic and copies ran while one was open for 0% of the time, Pallas kernels for 0%

profile of v6, /device:TPU:0, one launch (start us, length us, event | category | flops | bytes accessed | tf_op | source)
XLA Modules:
  0.0 105.3 jit_solution(4345449041512357954)
XLA Ops:
  0.6 5.1 %shard_map.50 = f32[1824,128]{1,0:T(8,128)} custom-call(f32[64,8,256]{2,1,0:T(8,128)} %refs_1_.3, f32[8,256]{1,0:T(8,128)} %refs_2_.3, f32[2,8,256]{2,1,0:T(8,128)} %refs_3_.1), custom_call_target="tpu_custom_call" | custom-call | tf_op jit(solution)/shard_map/pallas_call | solution.py:835
  5.8 31.1 %all_to_all.20 = f32[32,57,1,128]{3,2,1,0:T(1,128)S(1)} all-to-all(f32[32,57,1,128]{3,2,1,0:T(1,128)} %bitcast.20), channel_id=1, replica_groups=mesh['tm'=8,'space'=4] {'tm','space'}, dimensions={0} | all-to-all | bytes 1867776 | tf_op jit(solution)/shard_map/all_to_all | solution.py:848
  36.9 5.0 %shard_map.51 = (f32[6,32,128]{2,1,0:T(8,128)S(1)}, f32[64,32,128]{2,1,0:T(8,128)S(1)}, f32[64,48,128]{2,1,0:T(8,128)S(1)}, f32[64,32,128]{2,1,0:T(8,128)S(1)}, ...) custom-call(f32[1824,128]{1,0:T(8,128)S(1)} %bitcast.12), custom_call_target="tpu_custom_call" | custom-call | tf_op jit(solution)/shard_map/pallas_call | solution.py:835
  41.9 0.1 collective-permute-start
  42.0 0.7 collective-permute-start.1
  42.7 0.8 collective-permute-done.refs_2_
  43.5 0.0 collective-permute-done.1.refs_3_
  43.5 4.1 %shard_map.52 = (f32[64,32,128]{2,1,0:T(8,128)S(1)}, f32[64,48,128]{2,1,0:T(8,128)S(1)}, f32[64,32,128]{2,1,0:T(8,128)S(1)}, f32[64,8,128]{2,1,0:T(8,128)S(1)}, ...) custom-call(f32[6,32,128]{2,1,0:T(8,128)S(1)} %get-tuple-element.17.refs_0_, ...), custom_call_target="tpu_custom_call" | custom-call | tf_op jit(solution)/shard_map/pallas_call | solution.py:835
  47.6 6.7 %collective-permute-start.2 = (f32[64,8,128]{2,1,0:T(8,128)S(1)}, f32[64,8,128]{2,1,0:T(8,128)S(1)}, u32[]{:S(2)}, u32[]{:S(2)}) collective-permute-start(f32[64,8,128]{2,1,0:T(8,128)S(1)} %get-tuple-element.24), channel_id=1, source_target_pairs={{0,1},{1,0},{2,3},{3,2},{6,7},{7,6},{4,5},{5,4},{12,13},{13,12},{1... | collective-permute-start | bytes 786440 | tf_op jit(solution)/shard_map/ppermute | solution.py:890
  54.3 0.7 collective-permute-start.3
  55.0 12.1 %all_to_all.21 = f32[32,1,1,128]{3,2,1,0:T(1,128)S(1)} all-to-all(f32[32,1,1,128]{3,2,1,0:T(1,128)S(1)} %bitcast.18), channel_id=1, replica_groups=mesh['tm'=8,'space'=4] {'tm','space'}, dimensions={0} | all-to-all | bytes 32768 | tf_op jit(solution)/shard_map/all_to_all | solution.py:848
  67.1 0.0 collective-permute-done.2.refs_2_
  67.1 0.0 collective-permute-done.3.refs_3_
  67.1 4.6 %shard_map.53 = (f32[64,48,128]{2,1,0:T(8,128)S(1)}, f32[32,128]{1,0:T(8,128)S(1)}) custom-call(f32[6,32,128]{2,1,0:T(8,128)S(1)} %get-tuple-element.17.refs_0_, f32[64,32,128]{2,1,0:T(8,128)S(1)} %get-tuple-element.23.refs_1_, f32[64,8,128]{2,1,0:T(8,128)S(1)} %collective-permute-done.2.refs_2_, f32[64,8,128]{2,1,0:T(8,128)S(1)} %collective-permute-done.3.refs_3_, ...), custom_call_target="tpu_custom_call" | custom-call | tf_op jit(solution)/shard_map/pallas_call | solution.py:835
  71.7 8.9 %all_to_all.22 = f32[32,1,1,128]{3,2,1,0:T(1,128)S(1)} all-to-all(f32[32,1,1,128]{3,2,1,0:T(1,128)S(1)} %bitcast.19), channel_id=1, replica_groups=mesh['tm'=8,'space'=4] {'tm','space'}, dimensions={0} | all-to-all | bytes 32768 | tf_op jit(solution)/shard_map/all_to_all | solution.py:848
  80.5 0.0 copy-start.1
  80.5 0.0 copy-start.2
  80.6 1.8 %shard_map.54 = f32[1312,128]{1,0:T(8,128)S(1)} custom-call(f32[64,48,128]{2,1,0:T(8,128)S(1)} %get-tuple-element.16.refs_0_, f32[64,48,128]{2,1,0:T(8,128)S(1)} %get-tuple-element.22.refs_1_, f32[64,48,128]{2,1,0:T(8,128)S(1)} %get-tuple-element.28.refs_2_, f32[32,128]{1,0:T(8,128)S(1)} %bitcast.16, f32[32,128]{1,0:T(8,128)S(1)} %bitcast.17), custom_call_target="tpu_custom_call" | custom-call | tf_op jit(solution)/shard_map/pallas_call | solution.py:835
  82.3 0.0 copy-start
  82.4 20.1 %all_to_all.23 = f32[32,41,1,128]{3,2,1,0:T(1,128)S(1)} all-to-all(f32[32,41,1,128]{3,2,1,0:T(1,128)S(1)} %bitcast.14), channel_id=1, replica_groups=mesh['tm'=8,'space'=4] {'tm','space'}, dimensions={0} | all-to-all | bytes 1343488 | tf_op jit(solution)/shard_map/all_to_all | solution.py:848
  102.5 0.0 copy-done.1
  102.5 0.0 copy-done.2
  102.5 0.0 copy-done
  102.5 2.8 %shard_map.55 = (f32[64,8,256]{2,1,0:T(8,128)}, f32[64,8,256]{2,1,0:T(8,128)}) custom-call(f32[1312,128]{1,0:T(8,128)S(1)} %bitcast.13, f32[64,8,256]{2,1,0:T(8,128)S(1)} %copy-done, f32[8,256]{1,0:T(8,128)S(1)} %copy-done.2, f32[2,8,256]{2,1,0:T(8,128)S(1)} %copy-done.1), custom_call_target="tpu_custom_call" | custom-call | tf_op jit(solution)/shard_map/pallas_call | solution.py:835
Async XLA Ops:
  41.9 1.6 %collective-permute-start = (f32[64,8,128]{2,1,0:T(8,128)S(1)}, f32[64,8,128]{2,1,0:T(8,128)S(1)}, u32[]{:S(2)}, u32[]{:S(2)}) collective-permute-start(f32[64,8,128]{2,1,0:T(8,128)S(1)} %get-tuple-element.19), channel_id=1, source_target_pairs={{0,1},{1,0},{2,3},{3,2},{6,7},{7,6},{4,5},{5,4},{12,13},{13,12},{1... | collective-permute-start | bytes 786440 | tf_op jit(solution)/shard_map/ppermute | solution.py:882
  42.0 1.5 %collective-permute-start.1 = (f32[64,8,128]{2,1,0:T(8,128)S(1)}, f32[64,8,128]{2,1,0:T(8,128)S(1)}, u32[]{:S(2)}, u32[]{:S(2)}) collective-permute-start(f32[64,8,128]{2,1,0:T(8,128)S(1)} %get-tuple-element.20), channel_id=1, source_target_pairs={{1,2},{2,1},{3,6},{6,3},{7,4},{4,7},{5,12},{12,5},{13,14},{14,13},... | collective-permute-start | bytes 786440 | tf_op jit(solution)/shard_map/ppermute | solution.py:883
  47.6 19.5 %collective-permute-start.2 = (f32[64,8,128]{2,1,0:T(8,128)S(1)}, f32[64,8,128]{2,1,0:T(8,128)S(1)}, u32[]{:S(2)}, u32[]{:S(2)}) collective-permute-start(f32[64,8,128]{2,1,0:T(8,128)S(1)} %get-tuple-element.24), channel_id=1, source_target_pairs={{0,1},{1,0},{2,3},{3,2},{6,7},{7,6},{4,5},{5,4},{12,13},{13,12},{1... | collective-permute-start | bytes 786440 | tf_op jit(solution)/shard_map/ppermute | solution.py:890
  54.3 12.8 %collective-permute-start.3 = (f32[64,8,128]{2,1,0:T(8,128)S(1)}, f32[64,8,128]{2,1,0:T(8,128)S(1)}, u32[]{:S(2)}, u32[]{:S(2)}) collective-permute-start(f32[64,8,128]{2,1,0:T(8,128)S(1)} %get-tuple-element.25), channel_id=1, source_target_pairs={{1,2},{2,1},{3,6},{6,3},{7,4},{4,7},{5,12},{12,5},{13,14},{14,13},... | collective-permute-start | bytes 786440 | tf_op jit(solution)/shard_map/ppermute | solution.py:891
  80.5 22.0 %copy-start.1 = (f32[2,8,256]{2,1,0:T(8,128)S(1)}, f32[2,8,256]{2,1,0:T(8,128)}, u32[]{:S(2)}) copy-start(f32[2,8,256]{2,1,0:T(8,128)} %refs_3_.1) | copy-start | bytes 49156
  80.5 22.0 %copy-start.2 = (f32[8,256]{1,0:T(8,128)S(1)}, f32[8,256]{1,0:T(8,128)}, u32[]{:S(2)}) copy-start(f32[8,256]{1,0:T(8,128)} %refs_2_.3) | copy-start | bytes 24580
  82.3 20.2 %copy-start = (f32[64,8,256]{2,1,0:T(8,128)S(1)}, f32[64,8,256]{2,1,0:T(8,128)}, u32[]{:S(2)}) copy-start(f32[64,8,256]{2,1,0:T(8,128)} %refs_1_.3) | copy-start | bytes 1572868

commit v7 on v6

--- a/solution.py
+++ b/solution.py
@@ -197,6 +197,7 @@
 AXES = ("tm", "space")
 UNROLL = 32
 PAIR = 2
+TAIL = 16
 
 
 def spin(block, amount, axis=1):
@@ -261,6 +262,7 @@
             and self.window == 2 * self.own
             and self.spare * (self.tiles - 1) == self.used
             and self.here % UNROLL == 0
+            and self.here % TAIL == 0
             and self.groups * 2 == SUB
             and self.slot >= self.halo
             and self.space % 2 == 0
@@ -631,7 +633,7 @@
     size = KRYLOV + 1
 
     def gather(base, accs):
-        for k in range(UNROLL):
+        for k in range(TAIL):
             n = base + k
             image = w_ref[n]
             if not final:
@@ -657,10 +659,10 @@
 
     def last(i, carry):
         z, before, accs = carry
-        accs = gather(jnp.maximum(i - 1, 0) * UNROLL, accs)
+        accs = gather(jnp.maximum(i - 1, 0) * TAIL, accs)
         accs = tuple(jnp.where(i > 0, acc, 0.0) for acc in accs)
-        for k in range(UNROLL):
-            n = i * UNROLL + k
+        for k in range(TAIL):
+            n = i * TAIL + k
             z = z * inverse
             guess = (1.0 - damping) * g_ref[n, inner, :] + (y_ref[UNROLL + n] + z)
             g_ref[n, inner, :] = guess
@@ -669,8 +671,8 @@
         return (z, before, accs)
 
     fields = (0, 5, 9)[j]
-    _, _, accs = lax.fori_loop(0, here // UNROLL, last, (start, before, (low_zero,) * fields))
-    accs = gather(here - UNROLL, list(accs))
+    _, _, accs = lax.fori_loop(0, here // TAIL, last, (start, before, (low_zero,) * fields))
+    accs = gather(here - TAIL, list(accs))
     if j == 0:
         return
     owned = (low_spot >= halo) & (low_spot < halo + own)

time: 106 us -> 106 us (level)
  no operation moved by 1% of the time
where the time goes in v7:
time: 106 us; the launch traced here: 105 us
  blocking collectives  72.2 us (68%)
  Pallas kernels  23.4 us (22%)
  starting transfers between devices  8.13 us (8%)
    all_to_all x4, blocking collectives, everyone(): lax.all_to_all(parts, AXES, split_axis=0, concat_axis=0, tiled=True)  72.2 us
    pallas_call x6, Pallas kernels, call(): pl.pallas_call(kernel, out_shape=[jax.ShapeDtypeStruct(shape, jnp.float32...  23.4 us
    ppermute x2, starting transfers between devices, strip_device(): near = lax.ppermute(near, AXES, near_route)  6.79 us
  transfers between devices with their start and end apart: 4, of which 1 were waited for; matrix products, arithmetic and copies ran while one was open for 0% of the time, Pallas kernels for 0%

profile of v7, /device:TPU:0, one launch (start us, length us, event | category | flops | bytes accessed | tf_op | source)
XLA Modules:
  0.0 105.3 jit_solution(530945288440136121)
XLA Ops:
  0.6 5.1 %shard_map.50 = f32[1824,128]{1,0:T(8,128)} custom-call(f32[64,8,256]{2,1,0:T(8,128)} %refs_1_.3, f32[8,256]{1,0:T(8,128)} %refs_2_.3, f32[2,8,256]{2,1,0:T(8,128)} %refs_3_.1), custom_call_target="tpu_custom_call" | custom-call | tf_op jit(solution)/shard_map/pallas_call | solution.py:837
  5.8 31.1 %all_to_all.20 = f32[32,57,1,128]{3,2,1,0:T(1,128)S(1)} all-to-all(f32[32,57,1,128]{3,2,1,0:T(1,128)} %bitcast.20), channel_id=1, replica_groups=mesh['tm'=8,'space'=4] {'tm','space'}, dimensions={0} | all-to-all | bytes 1867776 | tf_op jit(solution)/shard_map/all_to_all | solution.py:850
  36.9 5.1 %shard_map.51 = (f32[6,32,128]{2,1,0:T(8,128)S(1)}, f32[64,32,128]{2,1,0:T(8,128)S(1)}, f32[64,48,128]{2,1,0:T(8,128)S(1)}, f32[64,32,128]{2,1,0:T(8,128)S(1)}, ...) custom-call(f32[1824,128]{1,0:T(8,128)S(1)} %bitcast.12), custom_call_target="tpu_custom_call" | custom-call | tf_op jit(solution)/shard_map/pallas_call | solution.py:837
  42.0 0.1 collective-permute-start
  42.0 0.7 collective-permute-start.1
  42.7 0.8 collective-permute-done.refs_2_
  43.6 0.0 collective-permute-done.1.refs_3_
  43.6 4.1 %shard_map.52 = (f32[64,32,128]{2,1,0:T(8,128)S(1)}, f32[64,48,128]{2,1,0:T(8,128)S(1)}, f32[64,32,128]{2,1,0:T(8,128)S(1)}, f32[64,8,128]{2,1,0:T(8,128)S(1)}, ...) custom-call(f32[6,32,128]{2,1,0:T(8,128)S(1)} %get-tuple-element.17.refs_0_, ...), custom_call_target="tpu_custom_call" | custom-call | tf_op jit(solution)/shard_map/pallas_call | solution.py:837
  47.7 6.7 %collective-permute-start.2 = (f32[64,8,128]{2,1,0:T(8,128)S(1)}, f32[64,8,128]{2,1,0:T(8,128)S(1)}, u32[]{:S(2)}, u32[]{:S(2)}) collective-permute-start(f32[64,8,128]{2,1,0:T(8,128)S(1)} %get-tuple-element.24), channel_id=1, source_target_pairs={{0,1},{1,0},{2,3},{3,2},{6,7},{7,6},{4,5},{5,4},{12,13},{13,12},{1... | collective-permute-start | bytes 786440 | tf_op jit(solution)/shard_map/ppermute | solution.py:892
  54.4 0.7 collective-permute-start.3
  55.1 12.1 %all_to_all.21 = f32[32,1,1,128]{3,2,1,0:T(1,128)S(1)} all-to-all(f32[32,1,1,128]{3,2,1,0:T(1,128)S(1)} %bitcast.18), channel_id=1, replica_groups=mesh['tm'=8,'space'=4] {'tm','space'}, dimensions={0} | all-to-all | bytes 32768 | tf_op jit(solution)/shard_map/all_to_all | solution.py:850
  67.2 0.0 collective-permute-done.2.refs_2_
  67.2 0.0 collective-permute-done.3.refs_3_
  67.2 4.5 %shard_map.53 = (f32[64,48,128]{2,1,0:T(8,128)S(1)}, f32[32,128]{1,0:T(8,128)S(1)}) custom-call(f32[6,32,128]{2,1,0:T(8,128)S(1)} %get-tuple-element.17.refs_0_, f32[64,32,128]{2,1,0:T(8,128)S(1)} %get-tuple-element.23.refs_1_, f32[64,8,128]{2,1,0:T(8,128)S(1)} %collective-permute-done.2.refs_2_, f32[64,8,128]{2,1,0:T(8,128)S(1)} %collective-permute-done.3.refs_3_, ...), custom_call_target="tpu_custom_call" | custom-call | tf_op jit(solution)/shard_map/pallas_call | solution.py:837
  71.7 8.9 %all_to_all.22 = f32[32,1,1,128]{3,2,1,0:T(1,128)S(1)} all-to-all(f32[32,1,1,128]{3,2,1,0:T(1,128)S(1)} %bitcast.19), channel_id=1, replica_groups=mesh['tm'=8,'space'=4] {'tm','space'}, dimensions={0} | all-to-all | bytes 32768 | tf_op jit(solution)/shard_map/all_to_all | solution.py:850
  80.6 0.0 copy-start.1
  80.6 0.0 copy-start.2
  80.6 1.8 %shard_map.54 = f32[1312,128]{1,0:T(8,128)S(1)} custom-call(f32[64,48,128]{2,1,0:T(8,128)S(1)} %get-tuple-element.16.refs_0_, f32[64,48,128]{2,1,0:T(8,128)S(1)} %get-tuple-element.22.refs_1_, f32[64,48,128]{2,1,0:T(8,128)S(1)} %get-tuple-element.28.refs_2_, f32[32,128]{1,0:T(8,128)S(1)} %bitcast.16, f32[32,128]{1,0:T(8,128)S(1)} %bitcast.17), custom_call_target="tpu_custom_call" | custom-call | tf_op jit(solution)/shard_map/pallas_call | solution.py:837
  82.4 0.0 copy-start
  82.4 20.1 %all_to_all.23 = f32[32,41,1,128]{3,2,1,0:T(1,128)S(1)} all-to-all(f32[32,41,1,128]{3,2,1,0:T(1,128)S(1)} %bitcast.14), channel_id=1, replica_groups=mesh['tm'=8,'space'=4] {'tm','space'}, dimensions={0} | all-to-all | bytes 1343488 | tf_op jit(solution)/shard_map/all_to_all | solution.py:850
  102.5 0.0 copy-done.1
  102.5 0.0 copy-done.2
  102.5 0.0 copy-done
  102.5 2.8 %shard_map.55 = (f32[64,8,256]{2,1,0:T(8,128)}, f32[64,8,256]{2,1,0:T(8,128)}) custom-call(f32[1312,128]{1,0:T(8,128)S(1)} %bitcast.13, f32[64,8,256]{2,1,0:T(8,128)S(1)} %copy-done, f32[8,256]{1,0:T(8,128)S(1)} %copy-done.2, f32[2,8,256]{2,1,0:T(8,128)S(1)} %copy-done.1), custom_call_target="tpu_custom_call" | custom-call | tf_op jit(solution)/shard_map/pallas_call | solution.py:837
Async XLA Ops:
  42.0 1.6 %collective-permute-start = (f32[64,8,128]{2,1,0:T(8,128)S(1)}, f32[64,8,128]{2,1,0:T(8,128)S(1)}, u32[]{:S(2)}, u32[]{:S(2)}) collective-permute-start(f32[64,8,128]{2,1,0:T(8,128)S(1)} %get-tuple-element.19), channel_id=1, source_target_pairs={{0,1},{1,0},{2,3},{3,2},{6,7},{7,6},{4,5},{5,4},{12,13},{13,12},{1... | collective-permute-start | bytes 786440 | tf_op jit(solution)/shard_map/ppermute | solution.py:884
  42.0 1.5 %collective-permute-start.1 = (f32[64,8,128]{2,1,0:T(8,128)S(1)}, f32[64,8,128]{2,1,0:T(8,128)S(1)}, u32[]{:S(2)}, u32[]{:S(2)}) collective-permute-start(f32[64,8,128]{2,1,0:T(8,128)S(1)} %get-tuple-element.20), channel_id=1, source_target_pairs={{1,2},{2,1},{3,6},{6,3},{7,4},{4,7},{5,12},{12,5},{13,14},{14,13},... | collective-permute-start | bytes 786440 | tf_op jit(solution)/shard_map/ppermute | solution.py:885
  47.7 19.5 %collective-permute-start.2 = (f32[64,8,128]{2,1,0:T(8,128)S(1)}, f32[64,8,128]{2,1,0:T(8,128)S(1)}, u32[]{:S(2)}, u32[]{:S(2)}) collective-permute-start(f32[64,8,128]{2,1,0:T(8,128)S(1)} %get-tuple-element.24), channel_id=1, source_target_pairs={{0,1},{1,0},{2,3},{3,2},{6,7},{7,6},{4,5},{5,4},{12,13},{13,12},{1... | collective-permute-start | bytes 786440 | tf_op jit(solution)/shard_map/ppermute | solution.py:892
  54.4 12.8 %collective-permute-start.3 = (f32[64,8,128]{2,1,0:T(8,128)S(1)}, f32[64,8,128]{2,1,0:T(8,128)S(1)}, u32[]{:S(2)}, u32[]{:S(2)}) collective-permute-start(f32[64,8,128]{2,1,0:T(8,128)S(1)} %get-tuple-element.25), channel_id=1, source_target_pairs={{1,2},{2,1},{3,6},{6,3},{7,4},{4,7},{5,12},{12,5},{13,14},{14,13},... | collective-permute-start | bytes 786440 | tf_op jit(solution)/shard_map/ppermute | solution.py:893
  80.6 22.0 %copy-start.1 = (f32[2,8,256]{2,1,0:T(8,128)S(1)}, f32[2,8,256]{2,1,0:T(8,128)}, u32[]{:S(2)}) copy-start(f32[2,8,256]{2,1,0:T(8,128)} %refs_3_.1) | copy-start | bytes 49156
  80.6 22.0 %copy-start.2 = (f32[8,256]{1,0:T(8,128)S(1)}, f32[8,256]{1,0:T(8,128)}, u32[]{:S(2)}) copy-start(f32[8,256]{1,0:T(8,128)} %refs_2_.3) | copy-start | bytes 24580
  82.4 20.2 %copy-start = (f32[64,8,256]{2,1,0:T(8,128)S(1)}, f32[64,8,256]{2,1,0:T(8,128)}, u32[]{:S(2)}) copy-start(f32[64,8,256]{2,1,0:T(8,128)} %refs_1_.3) | copy-start | bytes 1572868
